TPU v7x, 256 devices: a whole 4x4x8 slice. The times are simulated.
256 devices in a mesh: row: 8 (over x, core), col: 32 (over y, z).
Axes of the slice: x: 4, y: 4, z: 8, core: 2. Of those that a mesh axis runs over, the one named last changes fastest.
Arguments:
- right_sides: bfloat16 [8192, 64, 128], P(('row', 'col')), may hold values from -7 to 7
- weights_fine: bfloat16 [8192, 3, 128, 128], P(('row', 'col')), may hold values from 0 to 2
- columns_fine: int32 [8192, 3], P(('row', 'col')), may hold values from 0 to 8191, as said below
- degree_fine: float32 [8192, 128], P(('row', 'col')), may hold values from 0.05 to 0.5
- owners_fine: int32 [8192, 128], P(('row', 'col')), may hold values from 0 to 255, as said below
- slots_fine: int32 [8192, 128], P(('row', 'col')), may hold values from 0 to 1023
- weights_second: bfloat16 [2048, 3, 128, 128], P(('row', 'col')), may hold values from 0 to 8
- columns_second: int32 [2048, 3], P(('row', 'col')), may hold values from 0 to 2047, as said below
- degree_second: float32 [2048, 128], P(('row', 'col')), may hold values from 0.2 to 2
- owners_second: int32 [2048, 128], P(('row', 'col')), may hold values from 0 to 255, as said below
- slots_second: int32 [2048, 128], P(('row', 'col')), may hold values from 0 to 255
- weights_third: bfloat16 [512, 3, 128, 128], P(('row', 'col')), may hold values from 0 to 32
- columns_third: int32 [512, 3], P(('row', 'col')), may hold values from 0 to 511, as said below
- degree_third: float32 [512, 128], P(('row', 'col')), may hold values from 0.8 to 8
- owners_third: int32 [512, 128], P(('row', 'col')), may hold values from 0 to 255, as said below
- slots_third: int32 [512, 128], P(('row', 'col')), may hold values from 0 to 127
- coarse_inverse: bfloat16 [32768, 4096], P(('row', 'col')), may hold values from -1 to 1, as said below
Outputs:
- solution: float32 [8192, 64, 128], P(('row', 'col'))
Inputs may be any that keep to these rules, and one draw needn't show every extreme that they name: `columns_fine`: every entry lies within 2 blocks of its own row block's index, on the same level. `columns_second`: every entry lies within 2 blocks of its own row block's index, on the same level. `columns_third`: every entry lies within 2 blocks of its own row block's index, on the same level. `owners_fine`: each entry is the device holding the vertex or the one just before or after it in device order. `owners_second`: each entry is the device holding the vertex or the one just before or after it in device order. `owners_third`: each entry is the device holding the vertex or the one just before or after it in device order. `coarse_inverse`: each row group's block is symmetric.
All inputs are finite; a program needn't handle non-finite values.
Results may differ from a plain program's by a relative error of at most 0.0003.
Values may be sent and summed in bfloat16 or wider, within the bound.
No kernel may reach another device: no remote copies, remote signals or barrier semaphores. Data moves between devices by JAX's collectives and lax.ppermute only.
A program may use at most 64 MiB of HBM per device.

v0:
```python
import jax
import jax.numpy as jnp
from jax import lax
from jax.sharding import PartitionSpec as P

BS = 128
K = 3
HB = 2
SWEEPS = 2
NB2 = 2
NB1 = 8
C3 = 128


damping = 0.8


def padded(x, sides, width):
    edges = {}
    for axis, dim in sides:
        devices, length = (lax.axis_size(axis), x.shape[dim])
        up = [(i, (i + 1) % devices) for i in range(devices - 1)]
        last = lax.slice_in_dim(x, length - width, length, axis=dim)
        initial = lax.slice_in_dim(x, 0, width, axis=dim)
        edges[dim] = (
            lax.ppermute(last, axis, up),
            lax.ppermute(initial, axis, [(b, a) for a, b in up]),
        )
    done = []
    for _, dim in sides:
        low, high = edges[dim]
        around = [(width, width) if d in done else (0, 0) for d in range(x.ndim)]
        x = jnp.concatenate([jnp.pad(low, around), x, jnp.pad(high, around)], axis=dim)
        done.append(dim)
    return x


def as_sent(x):
    return jax.tree.map(lambda a: a.astype(jnp.bfloat16) if a.dtype == jnp.float32 else a, x)


def passed_along(value, axis, steps):
    count = lax.axis_size(axis)
    initial, last = (max(0, -steps), min(count, count - steps))
    return lax.ppermute(value, axis, [(source, source + steps) for source in range(initial, last)])


def joined_along(blocks, dim):
    shape = list(blocks.shape[1:])
    shape[dim] *= blocks.shape[0]
    return jnp.moveaxis(blocks, 0, dim).reshape(shape)


def sent_to_all(x, axis):
    devices = lax.axis_size(axis)
    return lax.all_to_all(jnp.broadcast_to(x[None], (devices, *x.shape)), axis, 0, 0, tiled=True)


def collect(x, axis, dim):
    return joined_along(sent_to_all(x, axis), dim)


def gather_rows(blocks):
    return jnp.transpose(blocks, (0, 2, 1)).reshape(-1, blocks.shape[1])


def make_blocks(rows_data):
    return jnp.transpose(rows_data.reshape(-1, BS, rows_data.shape[1]), (0, 2, 1))


def complete_diagonal_entries(weights, shift):
    return shift + jnp.sum(weights, axis=(1, 2), dtype=jnp.float32) / (K * BS)


def apply_operator(current_iterate, weights, columns, degree, device):
    block_total_number = current_iterate.shape[0]
    rounded = current_iterate.astype(jnp.bfloat16)
    extended = padded(rounded, ((("row", "col"), 0),), HB)
    offset = device * block_total_number - HB
    picked = extended[columns - offset]
    product = jnp.einsum("nkrb,nkbc->nrc", picked, weights, preferred_element_type=jnp.float32)
    return degree[:, None, :] * current_iterate - product / (K * BS)


def restrict(residual, aggregate_owners, slots, coarse_count, device):
    targets = ((aggregate_owners - device + 1) * coarse_count + slots).reshape(-1)
    partial_value = jax.ops.segment_sum(
        gather_rows(residual), targets, num_segments=3 * coarse_count
    )
    upward = passed_along(as_sent(partial_value[2 * coarse_count :]), ("row", "col"), 1)
    downward = passed_along(as_sent(partial_value[:coarse_count]), ("row", "col"), -1)
    return partial_value[coarse_count : 2 * coarse_count] + upward + downward


def prolong(current_iterate, coarse_correction_rows, aggregate_owners, slots, coarse_count, device):
    extended = padded(as_sent(coarse_correction_rows), ((("row", "col"), 0),), coarse_count).astype(
        coarse_correction_rows.dtype
    )
    targets = ((aggregate_owners - device + 1) * coarse_count + slots).reshape(-1)
    return current_iterate + make_blocks(extended[targets])


def coarse_solve(coarse_rows, coarse_inverse):
    rounded = jnp.transpose(coarse_rows).astype(jnp.bfloat16)
    solved = lax.dot_general(
        collect(rounded, "col", 1),
        coarse_inverse,
        (((1,), (1,)), ((), ())),
        preferred_element_type=jnp.float32,
    )
    return jnp.transpose(solved)


def on_device(
    right_sides,
    weights_fine,
    columns_fine,
    degree_fine,
    owners_fine,
    slots_fine,
    weights_second,
    columns_second,
    degree_second,
    owners_second,
    slots_second,
    weights_third,
    columns_third,
    degree_third,
    owners_third,
    slots_third,
    coarse_inverse,
):
    device = lax.axis_index(("row", "col"))
    levels = [
        (
            weights_fine,
            columns_fine,
            complete_diagonal_entries(weights_fine, degree_fine),
            owners_fine,
            slots_fine,
            NB1 * BS,
        ),
        (
            weights_second,
            columns_second,
            complete_diagonal_entries(weights_second, degree_second),
            owners_second,
            slots_second,
            NB2 * BS,
        ),
        (
            weights_third,
            columns_third,
            complete_diagonal_entries(weights_third, degree_third),
            owners_third,
            slots_third,
            C3,
        ),
    ]
    source = right_sides.astype(jnp.float32)
    stored = []
    coarse_rows = None
    for position in range(3):
        weights, columns, degree, aggregate_owners, slots, coarse_count = levels[position]
        scale = degree[:, None, :]
        current_iterate = damping * source / scale
        current_iterate = (
            current_iterate
            + damping
            * (source - apply_operator(current_iterate, weights, columns, degree, device))
            / scale
        )
        residual = source - apply_operator(current_iterate, weights, columns, degree, device)
        stored.append((current_iterate, source))
        coarse_rows = restrict(residual, aggregate_owners, slots, coarse_count, device)
        if position < 2:
            source = make_blocks(coarse_rows)
    coarse_correction_rows = coarse_solve(coarse_rows, coarse_inverse)
    current_iterate = None
    for position in (2, 1, 0):
        weights, columns, degree, aggregate_owners, slots, coarse_count = levels[position]
        current_iterate, source = stored[position]
        current_iterate = prolong(
            current_iterate, coarse_correction_rows, aggregate_owners, slots, coarse_count, device
        )
        scale = degree[:, None, :]
        for repeat in range(SWEEPS):
            current_iterate = (
                current_iterate
                + damping
                * (source - apply_operator(current_iterate, weights, columns, degree, device))
                / scale
            )
        coarse_correction_rows = gather_rows(current_iterate)
    return current_iterate


def solution(mesh):
    in_specs = (
        P(("row", "col"), None, None),
        P(("row", "col"), None, None, None),
        P(("row", "col"), None),
        P(("row", "col"), None),
        P(("row", "col"), None),
        P(("row", "col"), None),
        P(("row", "col"), None, None, None),
        P(("row", "col"), None),
        P(("row", "col"), None),
        P(("row", "col"), None),
        P(("row", "col"), None),
        P(("row", "col"), None, None, None),
        P(("row", "col"), None),
        P(("row", "col"), None),
        P(("row", "col"), None),
        P(("row", "col"), None),
        P(("row", "col"), None),
    )
    out_specs = P(("row", "col"), None, None)
    return jax.shard_map(
        on_device, mesh=mesh, in_specs=in_specs, out_specs=out_specs, check_vma=False
    )
```

profile of v0, /device:TPU:6, one launch (start us, length us, event | category | flops | bytes accessed | tf_op | source)
XLA Modules:
  0.0 331.0 jit_solution(8018686676936958492)
XLA Ops:
  6.7 8.0 %collective-permute-start.1 = (bf16[2,64,128]{2,1,0:T(8,128)(2,1)S(1)}, bf16[2,64,128]{2,1,0:T(8,128)(2,1)S(1)}, u32[]{:S(2)}, u32[]{:S(2)}) collective-permute-start(bf16[2,64,128]{2,1,0:T(8,128)(2,1)S(1)} %get-tuple-element.18), channel_id=1, source_target_pairs={{1,0},{2,1},{3,2},{4,3},{5,4},{6,5},{7,6},{8,7},{9,8},{10,9},{11,1... | collective-permute-start | bytes 98312 | tf_op jit(solution)/shard_map/ppermute | solution.py:27
  24.5 7.9 %collective-permute-start.3 = (bf16[2,64,128]{2,1,0:T(8,128)(2,1)S(1)}, bf16[2,64,128]{2,1,0:T(8,128)(2,1)S(1)}, u32[]{:S(2)}, u32[]{:S(2)}) collective-permute-start(bf16[2,64,128]{2,1,0:T(8,128)(2,1)S(1)} %get-tuple-element.16), channel_id=1, source_target_pairs={{1,0},{2,1},{3,2},{4,3},{5,4},{6,5},{7,6},{8,7},{9,8},{10,9},{11,1... | collective-permute-start | bytes 98312 | tf_op jit(solution)/shard_map/ppermute | solution.py:27
  42.3 23.0 %scatter_custom_fusion = f32[3072,64]{1,0:T(8,128)S(1)} fusion(s32[4096]{0:T(1024)S(1)} %bitcast.392, f32[4096,64]{1,0:T(8,128)} %bitcast.369, f32[]{:T(128)} %constant.22.clone.1), kind=kCustom, calls=%fused_computation.89 | custom fusion | flops 262144 | bytes 786944 | tf_op jit(solution)/shard_map/scatter-add | solution.py:87
  68.1 7.9 %collective-permute-start.5 = (bf16[1024,64]{1,0:T(8,128)(2,1)S(1)}, bf16[1024,64]{1,0:T(8,128)(2,1)}, u32[]{:S(2)}, u32[]{:S(2)}) collective-permute-start(bf16[1024,64]{1,0:T(8,128)(2,1)S(1)} %get-tuple-element.10), channel_id=1, source_target_pairs={{1,0},{2,1},{3,2},{4,3},{5,4},{6,5},{7,6},{8,7},{9,8},{10,9},{11,1... | collective-permute-start | bytes 393224 | tf_op jit(solution)/shard_map/ppermute | solution.py:45
  83.8 8.1 %collective-permute-start.7 = (bf16[2,64,128]{2,1,0:T(8,128)(2,1)S(1)}, bf16[2,64,128]{2,1,0:T(8,128)(2,1)S(1)}, u32[]{:S(2)}, u32[]{:S(2)}) collective-permute-start(bf16[2,64,128]{2,1,0:T(8,128)(2,1)S(1)} %get-tuple-element.28), channel_id=1, source_target_pairs={{1,0},{2,1},{3,2},{4,3},{5,4},{6,5},{7,6},{8,7},{9,8},{10,9},{11,1... | collective-permute-start | bytes 98312 | tf_op jit(solution)/shard_map/ppermute | solution.py:27
  96.4 7.9 %collective-permute-start.9 = (bf16[2,64,128]{2,1,0:T(8,128)(2,1)S(1)}, bf16[2,64,128]{2,1,0:T(8,128)(2,1)S(1)}, u32[]{:S(2)}, u32[]{:S(2)}) collective-permute-start(bf16[2,64,128]{2,1,0:T(8,128)(2,1)S(1)} %get-tuple-element.26), channel_id=1, source_target_pairs={{1,0},{2,1},{3,2},{4,3},{5,4},{6,5},{7,6},{8,7},{9,8},{10,9},{11,1... | collective-permute-start | bytes 98312 | tf_op jit(solution)/shard_map/ppermute | solution.py:27
  107.1 6.1 %scatter_custom_fusion.1 = f32[768,64]{1,0:T(8,128)S(1)} fusion(s32[1024]{0:T(1024)S(1)} %bitcast.395, f32[1024,64]{1,0:T(8,128)S(1)} %bitcast.379, f32[]{:T(128)} %constant.22.clone.1), kind=kCustom, calls=%fused_computation.129 | custom fusion | flops 65536 | bytes 196612 | tf_op jit(solution)/shard_map/scatter-add | solution.py:87
  115.2 7.9 %collective-permute-start.11 = (bf16[256,64]{1,0:T(8,128)(2,1)S(1)}, bf16[256,64]{1,0:T(8,128)(2,1)S(1)}, u32[]{:S(2)}, u32[]{:S(2)}) collective-permute-start(bf16[256,64]{1,0:T(8,128)(2,1)S(1)} %get-tuple-element.20), channel_id=1, source_target_pairs={{1,0},{2,1},{3,2},{4,3},{5,4},{6,5},{7,6},{8,7},{9,8},{10,9},{11,1... | collective-permute-start | bytes 98312 | tf_op jit(solution)/shard_map/ppermute | solution.py:45
  127.7 7.9 %collective-permute-start.13 = (bf16[2,64,128]{2,1,0:T(8,128)(2,1)S(1)}, bf16[2,64,128]{2,1,0:T(8,128)(2,1)S(1)}, u32[]{:S(2)}, u32[]{:S(2)}) collective-permute-start(bf16[2,64,128]{2,1,0:T(8,128)(2,1)S(1)} %fusion.96), channel_id=1, source_target_pairs={{1,0},{2,1},{3,2},{4,3},{5,4},{6,5},{7,6},{8,7},{9,8},{10,9},{11,1... | collective-permute-start | bytes 98312 | tf_op jit(solution)/shard_map/ppermute | solution.py:27
  140.6 8.1 %collective-permute-start.15 = (bf16[2,64,128]{2,1,0:T(8,128)(2,1)S(1)}, bf16[2,64,128]{2,1,0:T(8,128)(2,1)S(1)}, u32[]{:S(2)}, u32[]{:S(2)}) collective-permute-start(bf16[2,64,128]{2,1,0:T(8,128)(2,1)S(1)} %get-tuple-element.5), channel_id=1, source_target_pairs={{1,0},{2,1},{3,2},{4,3},{5,4},{6,5},{7,6},{8,7},{9,8},{10,9},{11,1... | collective-permute-start | bytes 98312 | tf_op jit(solution)/shard_map/ppermute | solution.py:27
  154.3 7.9 %collective-permute-start.17 = (bf16[128,64]{1,0:T(8,128)(2,1)S(1)}, bf16[128,64]{1,0:T(8,128)(2,1)S(1)}, u32[]{:S(2)}, u32[]{:S(2)}) collective-permute-start(bf16[128,64]{1,0:T(8,128)(2,1)S(1)} %get-tuple-element.30), channel_id=1, source_target_pairs={{1,0},{2,1},{3,2},{4,3},{5,4},{6,5},{7,6},{8,7},{9,8},{10,9},{11,1... | collective-permute-start | bytes 49160 | tf_op jit(solution)/shard_map/ppermute | solution.py:45
  170.4 12.0 %all-to-all-done = bf16[32,64,128]{2,1,0:T(8,128)(2,1)S(1)} async-done(((bf16[32,64,128]{2,1,0:T(8,128)(2,1)}), bf16[32,64,128]{2,1,0:T(8,128)(2,1)S(1)}, u32[]{:S(2)}, u32[]{:S(2)}) %all-to-all-start) | async-done | bytes 524320 | tf_op jit(solution)/shard_map/all_to_all | solution.py:56
  182.9 4.3 %collective-permute-start.18 = (bf16[128,64]{0,1:T(8,128)(2,1)S(1)}, bf16[128,64]{0,1:T(8,128)(2,1)S(1)}, u32[]{:S(2)}, u32[]{:S(2)}) collective-permute-start(bf16[128,64]{0,1:T(8,128)(2,1)S(1)} %fusion.46), channel_id=1, source_target_pairs={{0,1},{1,2},{2,3},{3,4},{4,5},{5,6},{6,7},{7,8},{8,9},{9,10},{10,1... | collective-permute-start | bytes 49160 | tf_op jit(solution)/shard_map/ppermute | solution.py:26
  187.2 6.9 %collective-permute-start.19 = (bf16[128,64]{0,1:T(8,128)(2,1)S(1)}, bf16[128,64]{0,1:T(8,128)(2,1)S(1)}, u32[]{:S(2)}, u32[]{:S(2)}) collective-permute-start(bf16[128,64]{0,1:T(8,128)(2,1)S(1)} %fusion.46), channel_id=1, source_target_pairs={{1,0},{2,1},{3,2},{4,3},{5,4},{6,5},{7,6},{8,7},{9,8},{10,9},{11,1... | collective-permute-start | bytes 49160 | tf_op jit(solution)/shard_map/ppermute | solution.py:27
  198.5 7.9 %collective-permute-start.21 = (bf16[2,64,128]{2,1,0:T(8,128)(2,1)S(1)}, bf16[2,64,128]{2,1,0:T(8,128)(2,1)S(1)}, u32[]{:S(2)}, u32[]{:S(2)}) collective-permute-start(bf16[2,64,128]{2,1,0:T(8,128)(2,1)S(1)} %fusion.98), channel_id=1, source_target_pairs={{1,0},{2,1},{3,2},{4,3},{5,4},{6,5},{7,6},{8,7},{9,8},{10,9},{11,1... | collective-permute-start | bytes 98312 | tf_op jit(solution)/shard_map/ppermute | solution.py:27
  210.7 8.1 %collective-permute-start.23 = (bf16[2,64,128]{2,1,0:T(8,128)(2,1)S(1)}, bf16[2,64,128]{2,1,0:T(8,128)(2,1)S(1)}, u32[]{:S(2)}, u32[]{:S(2)}) collective-permute-start(bf16[2,64,128]{2,1,0:T(8,128)(2,1)S(1)} %get-tuple-element.35), channel_id=1, source_target_pairs={{1,0},{2,1},{3,2},{4,3},{5,4},{6,5},{7,6},{8,7},{9,8},{10,9},{11,1... | collective-permute-start | bytes 98312 | tf_op jit(solution)/shard_map/ppermute | solution.py:27
  223.2 7.9 %collective-permute-start.25 = (bf16[256,64]{1,0:T(8,128)(2,1)S(1)}, bf16[256,64]{1,0:T(8,128)(2,1)S(1)}, u32[]{:S(2)}, u32[]{:S(2)}) collective-permute-start(bf16[256,64]{1,0:T(8,128)(2,1)S(1)} %bitcast.386), channel_id=1, source_target_pairs={{1,0},{2,1},{3,2},{4,3},{5,4},{6,5},{7,6},{8,7},{9,8},{10,9},{11,1... | collective-permute-start | bytes 98312 | tf_op jit(solution)/shard_map/ppermute | solution.py:27
  238.0 7.9 %collective-permute-start.27 = (bf16[2,64,128]{2,1,0:T(8,128)(2,1)S(1)}, bf16[2,64,128]{2,1,0:T(8,128)(2,1)S(1)}, u32[]{:S(2)}, u32[]{:S(2)}) collective-permute-start(bf16[2,64,128]{2,1,0:T(8,128)(2,1)S(1)} %get-tuple-element.24), channel_id=1, source_target_pairs={{1,0},{2,1},{3,2},{4,3},{5,4},{6,5},{7,6},{8,7},{9,8},{10,9},{11,1... | collective-permute-start | bytes 98312 | tf_op jit(solution)/shard_map/ppermute | solution.py:27
  251.1 7.9 %collective-permute-start.29 = (bf16[2,64,128]{2,1,0:T(8,128)(2,1)S(1)}, bf16[2,64,128]{2,1,0:T(8,128)(2,1)S(1)}, u32[]{:S(2)}, u32[]{:S(2)}) collective-permute-start(bf16[2,64,128]{2,1,0:T(8,128)(2,1)S(1)} %get-tuple-element.22), channel_id=1, source_target_pairs={{1,0},{2,1},{3,2},{4,3},{5,4},{6,5},{7,6},{8,7},{9,8},{10,9},{11,1... | collective-permute-start | bytes 98312 | tf_op jit(solution)/shard_map/ppermute | solution.py:27
  264.8 7.9 %collective-permute-start.31 = (bf16[1024,64]{1,0:T(8,128)(2,1)S(1)}, bf16[1024,64]{1,0:T(8,128)(2,1)S(1)}, u32[]{:S(2)}, u32[]{:S(2)}) collective-permute-start(bf16[1024,64]{1,0:T(8,128)(2,1)S(1)} %bitcast.376), channel_id=1, source_target_pairs={{1,0},{2,1},{3,2},{4,3},{5,4},{6,5},{7,6},{8,7},{9,8},{10,9},{11,1... | collective-permute-start | bytes 393224 | tf_op jit(solution)/shard_map/ppermute | solution.py:27
  276.6 14.1 %gather_fusion.12 = f32[4096,64]{1,0:T(8,128)} fusion(f32[3072,64]{1,0:T(8,128)S(1)} %maximum_convert_fusion, s32[4096]{0:T(1024)S(1)} %broadcast_clamp_fusion), kind=kCustom, calls=%fused_computation.12 | custom fusion | bytes 2113536 | tf_op jit(solution)/shard_map/gather | solution.py:100
  297.3 8.0 %collective-permute-start.33 = (bf16[2,64,128]{2,1,0:T(8,128)(2,1)S(1)}, bf16[2,64,128]{2,1,0:T(8,128)(2,1)S(1)}, u32[]{:S(2)}, u32[]{:S(2)}) collective-permute-start(bf16[2,64,128]{2,1,0:T(8,128)(2,1)S(1)} %get-tuple-element.14), channel_id=1, source_target_pairs={{1,0},{2,1},{3,2},{4,3},{5,4},{6,5},{7,6},{8,7},{9,8},{10,9},{11,1... | collective-permute-start | bytes 98312 | tf_op jit(solution)/shard_map/ppermute | solution.py:27
  309.0 4.4 %fusion.115 = (bf16[32,64,128]{2,1,0:T(8,128)(2,1)S(1)}, f32[32,64,128]{2,1,0:T(8,128)}) fusion(bf16[32,3,64,128]{3,2,1,0:T(8,128)(2,1)} %bitcast.371, bf16[32,3,128,128]{3,2,1,0:T(8,128)(2,1)} %param.18, f32[32,128]{1,0:T(8,128)S(1)} %copy-done.9, bf16[32,64,128]{2,1,0:T(8,128)(2,1)S(1)} %copy-done.5, f32[32,64,128]{2,1,0:T(8,128)S(1)} %copy-done.1, ...), kind=kOutput, calls=%fused_computation.201 | convolution fusion | flops 203948032 | bytes 8929280 | tf_op jit(solution)/shard_map/nkrb,nkbc->nrc/dot_general | solution.py:81
  315.3 7.9 %collective-permute-start.35 = (bf16[2,64,128]{2,1,0:T(8,128)(2,1)S(1)}, bf16[2,64,128]{2,1,0:T(8,128)(2,1)S(1)}, u32[]{:S(2)}, u32[]{:S(2)}) collective-permute-start(bf16[2,64,128]{2,1,0:T(8,128)(2,1)S(1)} %get-tuple-element.12), channel_id=1, source_target_pairs={{1,0},{2,1},{3,2},{4,3},{5,4},{6,5},{7,6},{8,7},{9,8},{10,9},{11,1... | collective-permute-start | bytes 98312 | tf_op jit(solution)/shard_map/ppermute | solution.py:27
  (218 shorter events, 123.8 us)
Async XLA Ops:
  2.9 12.3 %collective-permute-start = (bf16[2,64,128]{2,1,0:T(8,128)(2,1)S(1)}, bf16[2,64,128]{2,1,0:T(8,128)(2,1)S(1)}, u32[]{:S(2)}, u32[]{:S(2)}) collective-permute-start(bf16[2,64,128]{2,1,0:T(8,128)(2,1)S(1)} %get-tuple-element.17), channel_id=1, source_target_pairs={{0,1},{1,2},{2,3},{3,4},{4,5},{5,6},{6,7},{7,8},{8,9},{9,10},{10,1... | collective-permute-start | bytes 98312 | tf_op jit(solution)/shard_map/ppermute | solution.py:26
  22.6 9.9 %collective-permute-start.2 = (bf16[2,64,128]{2,1,0:T(8,128)(2,1)S(1)}, bf16[2,64,128]{2,1,0:T(8,128)(2,1)S(1)}, u32[]{:S(2)}, u32[]{:S(2)}) collective-permute-start(bf16[2,64,128]{2,1,0:T(8,128)(2,1)S(1)} %get-tuple-element.15), channel_id=1, source_target_pairs={{0,1},{1,2},{2,3},{3,4},{4,5},{5,6},{6,7},{7,8},{8,9},{9,10},{10,1... | collective-permute-start | bytes 98312 | tf_op jit(solution)/shard_map/ppermute | solution.py:26
  66.1 14.2 %collective-permute-start.4 = (bf16[1024,64]{1,0:T(8,128)(2,1)}, bf16[1024,64]{1,0:T(8,128)(2,1)S(1)}, u32[]{:S(2)}, u32[]{:S(2)}) collective-permute-start(bf16[1024,64]{1,0:T(8,128)(2,1)} %get-tuple-element.9), channel_id=1, source_target_pairs={{0,1},{1,2},{2,3},{3,4},{4,5},{5,6},{6,7},{7,8},{8,9},{9,10},{10,1... | collective-permute-start | bytes 393224 | tf_op jit(solution)/shard_map/ppermute | solution.py:45
  68.1 12.5 %collective-permute-start.5 = (bf16[1024,64]{1,0:T(8,128)(2,1)S(1)}, bf16[1024,64]{1,0:T(8,128)(2,1)}, u32[]{:S(2)}, u32[]{:S(2)}) collective-permute-start(bf16[1024,64]{1,0:T(8,128)(2,1)S(1)} %get-tuple-element.10), channel_id=1, source_target_pairs={{1,0},{2,1},{3,2},{4,3},{5,4},{6,5},{7,6},{8,7},{9,8},{10,9},{11,1... | collective-permute-start | bytes 393224 | tf_op jit(solution)/shard_map/ppermute | solution.py:45
  81.8 10.1 %collective-permute-start.6 = (bf16[2,64,128]{2,1,0:T(8,128)(2,1)S(1)}, bf16[2,64,128]{2,1,0:T(8,128)(2,1)S(1)}, u32[]{:S(2)}, u32[]{:S(2)}) collective-permute-start(bf16[2,64,128]{2,1,0:T(8,128)(2,1)S(1)} %get-tuple-element.27), channel_id=1, source_target_pairs={{0,1},{1,2},{2,3},{3,4},{4,5},{5,6},{6,7},{7,8},{8,9},{9,10},{10,1... | collective-permute-start | bytes 98312 | tf_op jit(solution)/shard_map/ppermute | solution.py:26
  94.5 10.4 %collective-permute-start.8 = (bf16[2,64,128]{2,1,0:T(8,128)(2,1)S(1)}, bf16[2,64,128]{2,1,0:T(8,128)(2,1)S(1)}, u32[]{:S(2)}, u32[]{:S(2)}) collective-permute-start(bf16[2,64,128]{2,1,0:T(8,128)(2,1)S(1)} %get-tuple-element.25), channel_id=1, source_target_pairs={{0,1},{1,2},{2,3},{3,4},{4,5},{5,6},{6,7},{7,8},{8,9},{9,10},{10,1... | collective-permute-start | bytes 98312 | tf_op jit(solution)/shard_map/ppermute | solution.py:26
  113.2 10.6 %collective-permute-start.10 = (bf16[256,64]{1,0:T(8,128)(2,1)S(1)}, bf16[256,64]{1,0:T(8,128)(2,1)S(1)}, u32[]{:S(2)}, u32[]{:S(2)}) collective-permute-start(bf16[256,64]{1,0:T(8,128)(2,1)S(1)} %get-tuple-element.19), channel_id=1, source_target_pairs={{0,1},{1,2},{2,3},{3,4},{4,5},{5,6},{6,7},{7,8},{8,9},{9,10},{10,1... | collective-permute-start | bytes 98312 | tf_op jit(solution)/shard_map/ppermute | solution.py:45
  115.2 9.8 %collective-permute-start.11 = (bf16[256,64]{1,0:T(8,128)(2,1)S(1)}, bf16[256,64]{1,0:T(8,128)(2,1)S(1)}, u32[]{:S(2)}, u32[]{:S(2)}) collective-permute-start(bf16[256,64]{1,0:T(8,128)(2,1)S(1)} %get-tuple-element.20), channel_id=1, source_target_pairs={{1,0},{2,1},{3,2},{4,3},{5,4},{6,5},{7,6},{8,7},{9,8},{10,9},{11,1... | collective-permute-start | bytes 98312 | tf_op jit(solution)/shard_map/ppermute | solution.py:45
  125.7 9.9 %collective-permute-start.12 = (bf16[2,64,128]{2,1,0:T(8,128)(2,1)S(1)}, bf16[2,64,128]{2,1,0:T(8,128)(2,1)S(1)}, u32[]{:S(2)}, u32[]{:S(2)}) collective-permute-start(bf16[2,64,128]{2,1,0:T(8,128)(2,1)S(1)} %fusion.96), channel_id=1, source_target_pairs={{0,1},{1,2},{2,3},{3,4},{4,5},{5,6},{6,7},{7,8},{8,9},{9,10},{10,1... | collective-permute-start | bytes 98312 | tf_op jit(solution)/shard_map/ppermute | solution.py:26
  138.6 10.7 %collective-permute-start.14 = (bf16[2,64,128]{2,1,0:T(8,128)(2,1)S(1)}, bf16[2,64,128]{2,1,0:T(8,128)(2,1)S(1)}, u32[]{:S(2)}, u32[]{:S(2)}) collective-permute-start(bf16[2,64,128]{2,1,0:T(8,128)(2,1)S(1)} %get-tuple-element.5), channel_id=1, source_target_pairs={{0,1},{1,2},{2,3},{3,4},{4,5},{5,6},{6,7},{7,8},{8,9},{9,10},{10,1... | collective-permute-start | bytes 98312 | tf_op jit(solution)/shard_map/ppermute | solution.py:26
  152.4 9.8 %collective-permute-start.16 = (bf16[128,64]{1,0:T(8,128)(2,1)S(1)}, bf16[128,64]{1,0:T(8,128)(2,1)S(1)}, u32[]{:S(2)}, u32[]{:S(2)}) collective-permute-start(bf16[128,64]{1,0:T(8,128)(2,1)S(1)} %get-tuple-element.29), channel_id=1, source_target_pairs={{0,1},{1,2},{2,3},{3,4},{4,5},{5,6},{6,7},{7,8},{8,9},{9,10},{10,1... | collective-permute-start | bytes 49160 | tf_op jit(solution)/shard_map/ppermute | solution.py:45
  154.3 10.4 %collective-permute-start.17 = (bf16[128,64]{1,0:T(8,128)(2,1)S(1)}, bf16[128,64]{1,0:T(8,128)(2,1)S(1)}, u32[]{:S(2)}, u32[]{:S(2)}) collective-permute-start(bf16[128,64]{1,0:T(8,128)(2,1)S(1)} %get-tuple-element.30), channel_id=1, source_target_pairs={{1,0},{2,1},{3,2},{4,3},{5,4},{6,5},{7,6},{8,7},{9,8},{10,9},{11,1... | collective-permute-start | bytes 49160 | tf_op jit(solution)/shard_map/ppermute | solution.py:45
  165.8 16.6 %all-to-all-start = ((bf16[32,64,128]{2,1,0:T(8,128)(2,1)}), bf16[32,64,128]{2,1,0:T(8,128)(2,1)S(1)}, u32[]{:S(2)}, u32[]{:S(2)}) async-start(bf16[32,64,128]{2,1,0:T(8,128)(2,1)} %broadcast_in_dim.20), calls=%async_computation | async-start | bytes 1048576 | tf_op jit(solution)/shard_map/all_to_all | solution.py:56
  182.9 11.3 %collective-permute-start.18 = (bf16[128,64]{0,1:T(8,128)(2,1)S(1)}, bf16[128,64]{0,1:T(8,128)(2,1)S(1)}, u32[]{:S(2)}, u32[]{:S(2)}) collective-permute-start(bf16[128,64]{0,1:T(8,128)(2,1)S(1)} %fusion.46), channel_id=1, source_target_pairs={{0,1},{1,2},{2,3},{3,4},{4,5},{5,6},{6,7},{7,8},{8,9},{9,10},{10,1... | collective-permute-start | bytes 49160 | tf_op jit(solution)/shard_map/ppermute | solution.py:26
  196.6 9.8 %collective-permute-start.20 = (bf16[2,64,128]{2,1,0:T(8,128)(2,1)S(1)}, bf16[2,64,128]{2,1,0:T(8,128)(2,1)S(1)}, u32[]{:S(2)}, u32[]{:S(2)}) collective-permute-start(bf16[2,64,128]{2,1,0:T(8,128)(2,1)S(1)} %fusion.98), channel_id=1, source_target_pairs={{0,1},{1,2},{2,3},{3,4},{4,5},{5,6},{6,7},{7,8},{8,9},{9,10},{10,1... | collective-permute-start | bytes 98312 | tf_op jit(solution)/shard_map/ppermute | solution.py:26
  208.8 10.1 %collective-permute-start.22 = (bf16[2,64,128]{2,1,0:T(8,128)(2,1)S(1)}, bf16[2,64,128]{2,1,0:T(8,128)(2,1)S(1)}, u32[]{:S(2)}, u32[]{:S(2)}) collective-permute-start(bf16[2,64,128]{2,1,0:T(8,128)(2,1)S(1)} %get-tuple-element.35), channel_id=1, source_target_pairs={{0,1},{1,2},{2,3},{3,4},{4,5},{5,6},{6,7},{7,8},{8,9},{9,10},{10,1... | collective-permute-start | bytes 98312 | tf_op jit(solution)/shard_map/ppermute | solution.py:26
  221.3 10.4 %collective-permute-start.24 = (bf16[256,64]{1,0:T(8,128)(2,1)S(1)}, bf16[256,64]{1,0:T(8,128)(2,1)S(1)}, u32[]{:S(2)}, u32[]{:S(2)}) collective-permute-start(bf16[256,64]{1,0:T(8,128)(2,1)S(1)} %bitcast.385), channel_id=1, source_target_pairs={{0,1},{1,2},{2,3},{3,4},{4,5},{5,6},{6,7},{7,8},{8,9},{9,10},{10,1... | collective-permute-start | bytes 98312 | tf_op jit(solution)/shard_map/ppermute | solution.py:26
  223.2 9.8 %collective-permute-start.25 = (bf16[256,64]{1,0:T(8,128)(2,1)S(1)}, bf16[256,64]{1,0:T(8,128)(2,1)S(1)}, u32[]{:S(2)}, u32[]{:S(2)}) collective-permute-start(bf16[256,64]{1,0:T(8,128)(2,1)S(1)} %bitcast.386), channel_id=1, source_target_pairs={{1,0},{2,1},{3,2},{4,3},{5,4},{6,5},{7,6},{8,7},{9,8},{10,9},{11,1... | collective-permute-start | bytes 98312 | tf_op jit(solution)/shard_map/ppermute | solution.py:27
  236.1 9.9 %collective-permute-start.26 = (bf16[2,64,128]{2,1,0:T(8,128)(2,1)S(1)}, bf16[2,64,128]{2,1,0:T(8,128)(2,1)S(1)}, u32[]{:S(2)}, u32[]{:S(2)}) collective-permute-start(bf16[2,64,128]{2,1,0:T(8,128)(2,1)S(1)} %get-tuple-element.23), channel_id=1, source_target_pairs={{0,1},{1,2},{2,3},{3,4},{4,5},{5,6},{6,7},{7,8},{8,9},{9,10},{10,1... | collective-permute-start | bytes 98312 | tf_op jit(solution)/shard_map/ppermute | solution.py:26
  249.2 9.8 %collective-permute-start.28 = (bf16[2,64,128]{2,1,0:T(8,128)(2,1)S(1)}, bf16[2,64,128]{2,1,0:T(8,128)(2,1)S(1)}, u32[]{:S(2)}, u32[]{:S(2)}) collective-permute-start(bf16[2,64,128]{2,1,0:T(8,128)(2,1)S(1)} %get-tuple-element.21), channel_id=1, source_target_pairs={{0,1},{1,2},{2,3},{3,4},{4,5},{5,6},{6,7},{7,8},{8,9},{9,10},{10,1... | collective-permute-start | bytes 98312 | tf_op jit(solution)/shard_map/ppermute | solution.py:26
  262.8 12.2 %collective-permute-start.30 = (bf16[1024,64]{1,0:T(8,128)(2,1)S(1)}, bf16[1024,64]{1,0:T(8,128)(2,1)S(1)}, u32[]{:S(2)}, u32[]{:S(2)}) collective-permute-start(bf16[1024,64]{1,0:T(8,128)(2,1)S(1)} %bitcast.375), channel_id=1, source_target_pairs={{0,1},{1,2},{2,3},{3,4},{4,5},{5,6},{6,7},{7,8},{8,9},{9,10},{10,1... | collective-permute-start | bytes 393224 | tf_op jit(solution)/shard_map/ppermute | solution.py:26
  264.8 11.7 %collective-permute-start.31 = (bf16[1024,64]{1,0:T(8,128)(2,1)S(1)}, bf16[1024,64]{1,0:T(8,128)(2,1)S(1)}, u32[]{:S(2)}, u32[]{:S(2)}) collective-permute-start(bf16[1024,64]{1,0:T(8,128)(2,1)S(1)} %bitcast.376), channel_id=1, source_target_pairs={{1,0},{2,1},{3,2},{4,3},{5,4},{6,5},{7,6},{8,7},{9,8},{10,9},{11,1... | collective-permute-start | bytes 393224 | tf_op jit(solution)/shard_map/ppermute | solution.py:27
  295.4 10.0 %collective-permute-start.32 = (bf16[2,64,128]{2,1,0:T(8,128)(2,1)S(1)}, bf16[2,64,128]{2,1,0:T(8,128)(2,1)S(1)}, u32[]{:S(2)}, u32[]{:S(2)}) collective-permute-start(bf16[2,64,128]{2,1,0:T(8,128)(2,1)S(1)} %get-tuple-element.13), channel_id=1, source_target_pairs={{0,1},{1,2},{2,3},{3,4},{4,5},{5,6},{6,7},{7,8},{8,9},{9,10},{10,1... | collective-permute-start | bytes 98312 | tf_op jit(solution)/shard_map/ppermute | solution.py:26
  313.4 9.8 %collective-permute-start.34 = (bf16[2,64,128]{2,1,0:T(8,128)(2,1)S(1)}, bf16[2,64,128]{2,1,0:T(8,128)(2,1)S(1)}, u32[]{:S(2)}, u32[]{:S(2)}) collective-permute-start(bf16[2,64,128]{2,1,0:T(8,128)(2,1)S(1)} %get-tuple-element.11), channel_id=1, source_target_pairs={{0,1},{1,2},{2,3},{3,4},{4,5},{5,6},{6,7},{7,8},{8,9},{9,10},{10,1... | collective-permute-start | bytes 98312 | tf_op jit(solution)/shard_map/ppermute | solution.py:26
  (43 other events, 815.6 us)
where the time goes:
time: 332 us; the launch traced here: 331 us
  starting transfers between devices  185 us (56%)
  waiting for transfers between devices  43.9 us (13%)
  other arithmetic  40.3 us (12%)
  local copies, waits for them, and re-layouts  39.2 us (12%)
  matrix products  21.7 us (7%)
    ppermute x15, starting transfers between devices, padded(): lax.ppermute(initial, axis, [(b, a) for a, b in up])  118 us
    ppermute x15, starting transfers between devices, padded(): lax.ppermute(last, axis, up)  33.1 us
    scatter-add x3, other arithmetic, restrict(): jax.ops.segment_sum(gather_rows(residual), targets, num_segments=3 * coar...  30.6 us
    ppermute x6, starting transfers between devices, passed_along(): lax.ppermute(value, axis, [(source, source + steps) for source in range(i...  29.4 us
    dot_general x12, matrix products, apply_operator(): jnp.einsum('nkrb,nkbc->nrc', picked, weights, preferred_element_type=jnp....  21.2 us
    ppermute x15, waiting for transfers between devices, padded(): lax.ppermute(initial, axis, [(b, a) for a, b in up])  20.9 us
    gather x3, local copies, waits for them, and re-layouts, prolong(): return current_iterate + make_blocks(extended[targets])  17.6 us
    all_to_all x1, waiting for transfers between devices, sent_to_all(): lax.all_to_all(jnp.broadcast_to(x[None], (devices, *x.shape)), axis, 0, 0...  12 us
  transfers between devices with their start and end apart: 37, of which 22 were waited for; matrix products, arithmetic and copies ran while one was open for 1% of the time, Pallas kernels for 0%

commit v1 on v0

v1 whole, which is shorter than its diff:
```python
import functools

import jax
import jax.numpy as jnp
from jax import lax
from jax.experimental import pallas as pl
from jax.experimental.pallas import tpu as pltpu
from jax.sharding import PartitionSpec as P

BS = 128
R = 64
K = 3
HB = 2
NB2 = 2
NB1 = 8
NB0 = 32
C3 = 128
AXES = ("row", "col")
EDGE = 2 * HB
damping = 0.8
bf16 = jnp.bfloat16
f32 = jnp.float32


def passed_along(value, steps):
    count = lax.axis_size(AXES)
    initial, last = (max(0, -steps), min(count, count - steps))
    return lax.ppermute(value, AXES, [(s, s + steps) for s in range(initial, last)])


def both_ways(up, down):
    return passed_along(up, 1), passed_along(down, -1)


def split(x):
    high = x.astype(bf16)
    return high, (x - high.astype(f32)).astype(bf16)


def full_diagonal(weights, shift):
    return shift + jnp.sum(weights, axis=(1, 2), dtype=f32) / (K * BS)


def edge_rows(weights, diagonal, near, first):
    n = weights.shape[0]
    w = weights[:HB] if first else weights[n - HB :]
    g = diagonal[:EDGE] if first else diagonal[n - EDGE :]
    c = near[:HB] if first else near[n - HB :]
    c = jnp.pad(c.reshape(1, HB * K).astype(bf16), ((0, 7), (0, BS - HB * K)))
    return [w.reshape(HB * K * BS, BS), *split(g), c]


G_AT = HB * K * BS
C_AT = G_AT + 2 * EDGE
STATIC = C_AT + 8


def near_of(static_rows, offset):
    return static_rows[offset + C_AT, : HB * K].astype(jnp.int32).reshape(HB, K)


def blocks_product(v_ref, w, near_ref, row, base):
    parts = [v_ref[base + near_ref[row * K + k]] for k in range(K)]
    return jnp.dot(jnp.concatenate(parts, axis=1), w, preferred_element_type=f32) * (1.0 / (K * BS))


def halo_diag(ref, offset, i):
    at = offset + G_AT
    return ref[at + i : at + i + 1, :].astype(f32) + ref[at + EDGE + i : at + EDGE + i + 1, :].astype(f32)


def halo_weights(ref, offset, i):
    return ref[offset + i * K * BS : offset + (i + 1) * K * BS, :]


def load_weights(w_hbm, w_ref, sem, n, chunks):
    size = n // chunks
    return [
        pltpu.make_async_copy(w_hbm.at[pl.ds(c * size, size)], w_ref.at[pl.ds(c * size, size)], sem.at[c])
        for c in range(chunks)
    ]


def down_kernel(
    n, nc, so, chunks,
    near_ref, f_ref, g_ref, t_ref, flo_ref, fhi_ref, slo_ref, shi_ref, w_hbm,
    x_ref, down_ref, mid_ref, up_ref,
    w_ref, v0_ref, v1_ref, r_ref, acc_ref, sem,
):
    copies = load_weights(w_hbm, w_ref, sem, n, chunks)
    for c in copies:
        c.start()
    size = n // chunks

    def start_of(b):
        return f_ref[b].astype(f32) * (damping / g_ref[pl.ds(b, 1), :])

    def fill(b, carry):
        v0_ref[b + EDGE] = start_of(b).astype(bf16)
        return carry

    lax.fori_loop(0, n, fill, 0, unroll=2)
    edges = {}
    for side, fr, sr in ((0, flo_ref, slo_ref), (1, fhi_ref, shi_ref)):
        for i in range(EDGE):
            g = halo_diag(sr, so, i)
            s = jnp.where(g > 0, damping / g, 0.0)
            x0 = fr[i * R : (i + 1) * R, :].astype(f32) * s
            v0_ref[i + side * (n + EDGE)] = x0.astype(bf16)
            edges[side, i] = (s, x0)
    for side, sr in ((0, slo_ref), (1, shi_ref)):
        for i in range(HB):
            s, x0 = edges[side, i + HB * (1 - side)]
            j = i + side * (n + HB)
            p = blocks_product(v0_ref, halo_weights(sr, so, i), near_ref, j, j)
            v1_ref[j] = (1.2 * x0 + s * p).astype(bf16)

    def first(b, carry):
        p = blocks_product(v0_ref, w_ref[b], near_ref, b + HB, b + HB)
        s = damping / g_ref[pl.ds(b, 1), :]
        x = 1.2 * (f_ref[b].astype(f32) * s) + s * p
        x_ref[b] = x
        v1_ref[b + HB] = x.astype(bf16)
        return carry

    for c in range(chunks):
        copies[c].wait()
        lax.fori_loop(c * size, (c + 1) * size, first, 0, unroll=4 if size % 4 == 0 else 2)

    def residual(b, half):
        p = blocks_product(v1_ref, w_ref[b], near_ref, b + HB, b)
        return f_ref[b].astype(f32) - g_ref[pl.ds(b, 1), :] * x_ref[b] + p

    def second(q, carry):
        r_ref[q] = jnp.concatenate([residual(2 * q, 0), residual(2 * q + 1, 1)], axis=1).astype(bf16)
        return carry

    lax.fori_loop(0, n // 2, second, 0, unroll=2)

    highs = 3 * nc // 2
    group = 4
    acc_ref[...] = jnp.zeros_like(acc_ref)

    def gather(q, carry):
        left = []
        right = []
        for i in range(group):
            t = t_ref[q * group + i]
            r = r_ref[q * group + i]
            high = t // 256
            left.append(
                jnp.concatenate([r * jnp.where(high == h, 1.0, 0.0).astype(bf16) for h in range(highs)], axis=0)
            )
            low = t % 256
            rows = lax.broadcasted_iota(jnp.int32, (256, 256), 0)
            right.append(jnp.where(rows == low, 1.0, 0.0).astype(bf16))
        acc_ref[...] += lax.dot_general(
            jnp.concatenate(left, axis=1),
            jnp.concatenate(right, axis=1),
            (((1,), (1,)), ((), ())),
            preferred_element_type=f32,
        )
        return carry

    lax.fori_loop(0, n // 2 // group, gather, 0)

    for b in range(3 * nc):
        part = acc_ref[(b // 2) * R : (b // 2 + 1) * R, (b % 2) * BS : (b % 2 + 1) * BS]
        where = b // nc
        ref = (down_ref, mid_ref, up_ref)[where]
        ref[b - where * nc] = part.astype(ref.dtype)


def vmem():
    return pl.BlockSpec(memory_space=pltpu.VMEM)


def smem():
    return pl.BlockSpec(memory_space=pltpu.SMEM)


LIMIT = 16 * 1024 * 1024


def go_down(n, nc, near, f, g, t, f_edges, statics, so, weights):
    chunks = 4
    highs = 3 * nc // 2
    return pl.pallas_call(
        functools.partial(down_kernel, n, nc, so, chunks),
        out_shape=(
            jax.ShapeDtypeStruct((n, R, BS), f32),
            jax.ShapeDtypeStruct((nc, R, BS), bf16),
            jax.ShapeDtypeStruct((nc, R, BS), f32),
            jax.ShapeDtypeStruct((nc, R, BS), bf16),
        ),
        in_specs=[smem()] + [vmem()] * 7 + [pl.BlockSpec(memory_space=pl.ANY)],
        out_specs=(vmem(),) * 4,
        scratch_shapes=[
            pltpu.VMEM((n, K * BS, BS), bf16),
            pltpu.VMEM((n + 2 * EDGE, R, BS), bf16),
            pltpu.VMEM((n + EDGE, R, BS), bf16),
            pltpu.VMEM((n // 2, R, 2 * BS), bf16),
            pltpu.VMEM((highs * R, 2 * BS), f32),
            pltpu.SemaphoreType.DMA((chunks,)),
        ],
        compiler_params=pltpu.CompilerParams(vmem_limit_bytes=LIMIT),
        cost_estimate=pl.CostEstimate(
            flops=4 * n * R * K * BS * BS, transcendentals=0, bytes_accessed=n * K * BS * BS * 2
        ),
        name=f"down{n}",
    )(near, f, g, t, *f_edges, *statics, weights)


def prolong_kernel(n, nc, t_ref, lo_ref, own_ref, hi_ref, x_ref, out_ref, first_ref, last_ref, e_ref):
    highs = 3 * nc // 2
    for b in range(3 * nc):
        ref = (lo_ref, own_ref, hi_ref)[b // nc]
        e_ref[(b // 2) * R : (b // 2 + 1) * R, (b % 2) * BS : (b % 2 + 1) * BS] = ref[b % nc]

    def step(q, carry):
        t = t_ref[q]
        rows = lax.broadcasted_iota(jnp.int32, (256, 256), 0)
        pick = jnp.where(rows == t % 256, 1.0, 0.0).astype(bf16)
        found = jnp.dot(e_ref[...], pick, preferred_element_type=f32)
        high = t // 256
        y = jnp.zeros((R, 256), f32)
        for h in range(highs):
            y = y + jnp.where(high == h, found[h * R : (h + 1) * R], 0.0)
        out_ref[2 * q] = x_ref[2 * q] + y[:, :BS]
        out_ref[2 * q + 1] = x_ref[2 * q + 1] + y[:, BS:]
        return carry

    lax.fori_loop(0, n // 2, step, 0)
    first_ref[...] = out_ref[:EDGE].astype(bf16)
    last_ref[...] = out_ref[n - EDGE :].astype(bf16)


def prolong(n, nc, t, lo, own, hi, x):
    return pl.pallas_call(
        functools.partial(prolong_kernel, n, nc),
        out_shape=(
            jax.ShapeDtypeStruct((n, R, BS), f32),
            jax.ShapeDtypeStruct((EDGE, R, BS), bf16),
            jax.ShapeDtypeStruct((EDGE, R, BS), bf16),
        ),
        in_specs=[vmem()] * 5,
        out_specs=(vmem(),) * 3,
        scratch_shapes=[pltpu.VMEM((3 * nc // 2 * R, 2 * BS), bf16)],
        compiler_params=pltpu.CompilerParams(vmem_limit_bytes=LIMIT),
        cost_estimate=pl.CostEstimate(
            flops=2 * n * BS * 3 * nc * BS * R, transcendentals=0, bytes_accessed=2 * n * R * BS * 4
        ),
        name=f"prolong{n}",
    )(t, lo, own, hi, x)


def up_kernel(
    n, so, chunks,
    near_ref, x_ref, xlo_ref, xhi_ref, f_ref, g_ref, flo_ref, fhi_ref, slo_ref, shi_ref, w_hbm,
    out_ref,
    w_ref, v0_ref, v1_ref, keep_ref, sem,
):
    copies = load_weights(w_hbm, w_ref, sem, n, chunks)
    for c in copies:
        c.start()
    size = n // chunks

    def fill(b, carry):
        v0_ref[b + EDGE] = x_ref[b].astype(bf16)
        return carry

    lax.fori_loop(0, n, fill, 0, unroll=2)
    v0_ref[:EDGE] = xlo_ref[...]
    v0_ref[n + EDGE :] = xhi_ref[...]

    for side, fr, sr, xr in ((0, flo_ref, slo_ref, xlo_ref), (1, fhi_ref, shi_ref, xhi_ref)):
        for i in range(HB):
            e = i + HB * (1 - side)
            g = halo_diag(sr, so, e)
            s = jnp.where(g > 0, damping / g, 0.0)
            f = fr[e * R : (e + 1) * R, :].astype(f32)
            j = i + side * (n + HB)
            p = blocks_product(v0_ref, halo_weights(sr, so, i), near_ref, j, j)
            v1_ref[j] = (0.2 * xr[e].astype(f32) + s * (f + p)).astype(bf16)

    def sweep(b, x, p):
        s = damping / g_ref[pl.ds(b, 1), :]
        return 0.2 * x + s * (f_ref[b].astype(f32) + p)

    def first(b, carry):
        x = sweep(b, x_ref[b], blocks_product(v0_ref, w_ref[b], near_ref, b + HB, b + HB))
        keep_ref[b] = x
        v1_ref[b + HB] = x.astype(bf16)
        return carry

    for c in range(chunks):
        copies[c].wait()
        lax.fori_loop(c * size, (c + 1) * size, first, 0, unroll=4 if size % 4 == 0 else 2)

    def second(b, carry):
        p = blocks_product(v1_ref, w_ref[b], near_ref, b + HB, b)
        out_ref[b] = sweep(b, keep_ref[b], p).astype(out_ref.dtype)
        return carry

    lax.fori_loop(0, n, second, 0, unroll=4)


def go_up(n, near, x, x_edges, f, g, f_edges, statics, so, weights, dtype):
    chunks = 4
    return pl.pallas_call(
        functools.partial(up_kernel, n, so, chunks),
        out_shape=jax.ShapeDtypeStruct((n, R, BS), dtype),
        in_specs=[smem()] + [vmem()] * 9 + [pl.BlockSpec(memory_space=pl.ANY)],
        out_specs=vmem(),
        scratch_shapes=[
            pltpu.VMEM((n, K * BS, BS), bf16),
            pltpu.VMEM((n + 2 * EDGE, R, BS), bf16),
            pltpu.VMEM((n + EDGE, R, BS), bf16),
            pltpu.VMEM((n, R, BS), f32),
            pltpu.SemaphoreType.DMA((chunks,)),
        ],
        compiler_params=pltpu.CompilerParams(vmem_limit_bytes=LIMIT),
        cost_estimate=pl.CostEstimate(
            flops=4 * n * R * K * BS * BS, transcendentals=0, bytes_accessed=n * K * BS * BS * 2
        ),
        name=f"up{n}",
    )(near, x, *x_edges, f, g, *f_edges, *statics, weights)


def gather_rows(blocks):
    return jnp.transpose(blocks, (0, 2, 1)).reshape(-1, R)


def make_blocks(rows_data):
    return jnp.transpose(rows_data.reshape(-1, BS, R), (0, 2, 1))


def apply_operator(x, weights, near, degree):
    n = x.shape[0]
    rounded = x.astype(bf16)
    lo, hi = both_ways(rounded[n - HB :], rounded[:HB])
    extended = jnp.concatenate([lo, rounded, hi], axis=0)
    picked = extended[near + jnp.arange(n, dtype=jnp.int32)[:, None]]
    product = jnp.einsum("nkrb,nkbc->nrc", picked, weights, preferred_element_type=f32)
    return degree[:, None, :] * x - product / (K * BS)


def restrict(residual, targets, cc):
    partial = jax.ops.segment_sum(gather_rows(residual), targets.reshape(-1), num_segments=3 * cc)
    lo, hi = both_ways(partial[2 * cc :].astype(bf16), partial[:cc].astype(bf16))
    return partial[cc : 2 * cc] + lo + hi


def coarse_solve(coarse_rows, coarse_inverse):
    rounded = jnp.transpose(coarse_rows).astype(bf16)
    devices = lax.axis_size("col")
    got = lax.all_to_all(jnp.broadcast_to(rounded[None], (devices, *rounded.shape)), "col", 0, 0, tiled=True)
    got = jnp.moveaxis(got, 0, 1).reshape(R, -1)
    solved = lax.dot_general(got, coarse_inverse, (((1,), (1,)), ((), ())), preferred_element_type=f32)
    return jnp.transpose(solved)


def on_device(
    right_sides,
    weights_fine, columns_fine, degree_fine, owners_fine, slots_fine,
    weights_second, columns_second, degree_second, owners_second, slots_second,
    weights_third, columns_third, degree_third, owners_third, slots_third,
    coarse_inverse,
):
    device = lax.axis_index(AXES)

    def near_columns(columns):
        n = columns.shape[0]
        return columns - (device * n - HB + jnp.arange(n, dtype=jnp.int32)[:, None])

    def targets_of(owners, slots, cc):
        return (owners - device + 1) * cc + slots

    g1 = full_diagonal(weights_fine, degree_fine)
    g2 = full_diagonal(weights_second, degree_second)
    g3 = full_diagonal(weights_third, degree_third)
    near1, near2, near3 = near_columns(columns_fine), near_columns(columns_second), near_columns(columns_third)
    t1 = targets_of(owners_fine, slots_fine, NB1 * BS).reshape(NB0 // 2, 1, 2 * BS)
    t2 = targets_of(owners_second, slots_second, NB2 * BS).reshape(NB1 // 2, 1, 2 * BS)
    t3 = targets_of(owners_third, slots_third, C3)

    f = right_sides
    flat = lambda a: a.reshape(-1, BS)
    up1 = jnp.concatenate([flat(f[NB0 - EDGE :])] + edge_rows(weights_fine, g1, near1, False), axis=0)
    down1 = jnp.concatenate([flat(f[:EDGE])] + edge_rows(weights_fine, g1, near1, True), axis=0)
    e1 = both_ways(up1, down1)
    up2 = jnp.concatenate(edge_rows(weights_second, g2, near2, False), axis=0)
    down2 = jnp.concatenate(edge_rows(weights_second, g2, near2, True), axis=0)
    e2 = both_ways(up2, down2)
    fo = EDGE * R
    ext1 = jnp.concatenate([near_of(e1[0], fo), near1, near_of(e1[1], fo)], axis=0).reshape(-1)
    ext2 = jnp.concatenate([near_of(e2[0], 0), near2, near_of(e2[1], 0)], axis=0).reshape(-1)
    w1 = weights_fine.reshape(NB0, K * BS, BS)
    w2 = weights_second.reshape(NB1, K * BS, BS)

    x1, lower, middle, upper = go_down(NB0, NB1, ext1, f, g1, t1, e1, e1, fo, w1)
    lo, hi = both_ways(upper, lower)
    f2 = middle + lo.astype(f32) + hi.astype(f32)
    f2b = f2.astype(bf16)
    fe2 = both_ways(flat(f2b[NB1 - EDGE :]), flat(f2b[:EDGE]))
    x2, lower, middle, upper = go_down(NB1, NB2, ext2, f2, g2, t2, fe2, e2, 0, w2)
    lo, hi = both_ways(upper, lower)
    f3 = middle + lo.astype(f32) + hi.astype(f32)

    scale = g3[:, None, :]
    x3 = damping * f3 / scale
    x3 = x3 + damping * (f3 - apply_operator(x3, weights_third, near3, g3)) / scale
    residual = f3 - apply_operator(x3, weights_third, near3, g3)
    c = restrict(residual, t3, C3)
    u = coarse_solve(c, coarse_inverse).astype(bf16)
    lo, hi = both_ways(u, u)
    extended = jnp.concatenate([lo, u, hi], axis=0).astype(f32)
    x3 = x3 + make_blocks(extended[t3.reshape(-1)])
    for _ in range(2):
        x3 = x3 + damping * (f3 - apply_operator(x3, weights_third, near3, g3)) / scale

    x3 = x3.astype(bf16)
    lo, hi = both_ways(x3, x3)
    x2, first, last = prolong(NB1, NB2, t2, lo, x3, hi, x2)
    xe = both_ways(last, first)
    x2 = go_up(NB1, ext2, x2, xe, f2, g2, fe2, e2, 0, w2, bf16)
    lo, hi = both_ways(x2, x2)
    x1, first, last = prolong(NB0, NB1, t1, lo, x2, hi, x1)
    xe = both_ways(last, first)
    return go_up(NB0, ext1, x1, xe, f, g1, e1, e1, fo, w1, f32)


def solution(mesh):
    block = P(AXES, None, None)
    pair = P(AXES, None)
    four = P(AXES, None, None, None)
    level = (four, pair, pair, pair, pair)
    return jax.shard_map(
        on_device, mesh=mesh, in_specs=(block, *level, *level, *level, pair), out_specs=block, check_vma=False
    )
```

time: 332 us -> 297 us (0.89)
  starting transfers between devices: 185 us -> 156 us
  Pallas kernels: 0 us -> 26.9 us
  waiting for transfers between devices: 43.9 us -> 25 us
  matrix products: 21.7 us -> 8.19 us
  other arithmetic: 40.3 us -> 28.5 us
  local copies, waits for them, and re-layouts: 39.2 us -> 49.7 us
    ppermute x36 -> x30, starting transfers between devices: 181 us -> 151 us  [passed_along(): lax.ppermute(value, AXES, [(s, s + steps) for s in range(initial, last)])]
    scatter-add x3 -> x1, other arithmetic: 30.6 us -> 2.42 us  [restrict(): jax.ops.segment_sum(gather_rows(residual), targets.reshape(-1), num_segme...]
    pallas_call x0 -> x6, Pallas kernels: none -> 26.9 us  [the longest x2 12.3 us: go_down(): pl.pallas_call(functools.partial(down_kernel, n, nc, so, chunks), out_sha...]
    ppermute x36 -> x30, waiting for transfers between devices: 31.8 us -> 13.8 us  [passed_along(): lax.ppermute(value, AXES, [(s, s + steps) for s in range(initial, last)])]
    gather x15 -> x5, local copies, waits for them, and re-layouts: 29.2 us -> 11.2 us  [the longest x4 8.81 us: apply_operator(): picked = extended[near + jnp.arange(n, dtype=jnp.int32)[:, None]]]
    dot_general x13 -> x5, matrix products: 21.7 us -> 8.19 us  [the longest x4 6.67 us: apply_operator(): jnp.einsum('nkrb,nkbc->nrc', picked, weights, preferred_element_type=f32)]
    unnamed x60 -> x64, local copies, waits for them, and re-layouts: 0.15 us -> 12.5 us
    convert_element_type x4 -> x14, local copies, waits for them, and re-layouts: 0.5 us -> 7.04 us  [the longest x4 2.05 us: edge_rows(): c = jnp.pad(c.reshape(1, HB * K).astype(bf16), ((0, 7), (0, BS - HB * K)))]
  transfers between devices with their start and end apart: 37 -> 31, of which waited for: 22 -> 14; matrix products, arithmetic and copies ran while one was open for 1% -> 9% of each run, Pallas kernels for 0% -> 3%
where the time goes in v1:
time: 297 us; the launch traced here: 295 us
  starting transfers between devices  156 us (53%)
  local copies, waits for them, and re-layouts  49.7 us (17%)
  other arithmetic  28.5 us (10%)
  Pallas kernels  26.9 us (9%)
  waiting for transfers between devices  25 us (8%)
  matrix products  8.19 us (3%)
    ppermute x30, starting transfers between devices, passed_along(): lax.ppermute(value, AXES, [(s, s + steps) for s in range(initial, last)])  151 us
    ppermute x30, waiting for transfers between devices, passed_along(): lax.ppermute(value, AXES, [(s, s + steps) for s in range(initial, last)])  13.8 us
    unnamed x64, local copies, waits for them, and re-layouts  12.5 us
    pallas_call x2, Pallas kernels, go_down(): pl.pallas_call(functools.partial(down_kernel, n, nc, so, chunks), out_sha...  12.3 us
    all_to_all x1, waiting for transfers between devices, coarse_solve(): lax.all_to_all(jnp.broadcast_to(rounded[None], (devices, *rounded.shape))...  11.2 us
    pallas_call x2, Pallas kernels, go_up(): pl.pallas_call(functools.partial(up_kernel, n, so, chunks), out_shape=jax...  8.97 us
    gather x4, local copies, waits for them, and re-layouts, apply_operator(): picked = extended[near + jnp.arange(n, dtype=jnp.int32)[:, None]]  8.81 us
    dot_general x4, matrix products, apply_operator(): jnp.einsum('nkrb,nkbc->nrc', picked, weights, preferred_element_type=f32)  6.67 us
  transfers between devices with their start and end apart: 31, of which 14 were waited for; matrix products, arithmetic and copies ran while one was open for 9% of the time, Pallas kernels for 3%

profile of v1, /device:TPU:6, one launch (start us, length us, event | category | flops | bytes accessed | tf_op | source)
XLA Modules:
  0.0 295.1 jit_solution(10994372698969265741)
XLA Ops:
  6.7 3.8 %collective-permute-start = (bf16[1040,128]{1,0:T(8,128)(2,1)}, bf16[1040,128]{1,0:T(8,128)(2,1)S(1)}, u32[]{:S(2)}, u32[]{:S(2)}) collective-permute-start(bf16[1040,128]{1,0:T(8,128)(2,1)} %concatenate.33), channel_id=1, source_target_pairs={{0,1},{1,2},{2,3},{3,4},{4,5},{5,6},{6,7},{7,8},{8,9},{9,10},{10,1... | collective-permute-start | bytes 798728 | tf_op jit(solution)/shard_map/ppermute | solution.py:28
  13.2 8.0 %collective-permute-start.1 = (bf16[1040,128]{1,0:T(8,128)(2,1)}, bf16[1040,128]{1,0:T(8,128)(2,1)S(1)}, u32[]{:S(2)}, u32[]{:S(2)}) collective-permute-start(bf16[1040,128]{1,0:T(8,128)(2,1)} %concatenate.34), channel_id=1, source_target_pairs={{1,0},{2,1},{3,2},{4,3},{5,4},{6,5},{7,6},{8,7},{9,8},{10,9},{11,1... | collective-permute-start | bytes 798728 | tf_op jit(solution)/shard_map/ppermute | solution.py:28
  32.4 7.8 %collective-permute-start.3 = (bf16[784,128]{1,0:T(8,128)(2,1)}, bf16[784,128]{1,0:T(8,128)(2,1)S(1)}, u32[]{:S(2)}, u32[]{:S(2)}) collective-permute-start(bf16[784,128]{1,0:T(8,128)(2,1)} %fusion.18), channel_id=1, source_target_pairs={{1,0},{2,1},{3,2},{4,3},{5,4},{6,5},{7,6},{8,7},{9,8},{10,9},{11,1... | collective-permute-start | bytes 602120 | tf_op jit(solution)/shard_map/ppermute | solution.py:28
  44.8 8.0 %down32.1 = (f32[32,64,128]{2,1,0:T(8,128)S(1)}, bf16[8,64,128]{2,1,0:T(8,128)(2,1)S(1)}, f32[8,64,128]{2,1,0:T(8,128)S(1)}, bf16[8,64,128]{2,1,0:T(8,128)(2,1)}) custom-call(s32[108]{0:T(128)S(1)} %reshape.173.near_ref, bf16[32,64,128]{2,1,0:T(8,128)(2,1)S(1)} %copy-done.4, f32[32,128]{1,0:T(8,128)S(1)} %multiply_add_fusion.1.g_ref, ...), custom_call_target="tpu_custom_call" | custom-call | flops 402653184 | bytes 3145728 | tf_op jit(solution)/shard_map/down32/pallas_call | solution.py:188
  56.4 7.9 %collective-permute-start.5 = (bf16[8,64,128]{2,1,0:T(8,128)(2,1)S(1)}, bf16[8,64,128]{2,1,0:T(8,128)(2,1)}, u32[]{:S(2)}, u32[]{:S(2)}) collective-permute-start(bf16[8,64,128]{2,1,0:T(8,128)(2,1)S(1)} %get-tuple-element.21), channel_id=1, source_target_pairs={{1,0},{2,1},{3,2},{4,3},{5,4},{6,5},{7,6},{8,7},{9,8},{10,9},{11,1... | collective-permute-start | bytes 393224 | tf_op jit(solution)/shard_map/ppermute | solution.py:28
  70.5 8.1 %collective-permute-start.7 = (bf16[256,128]{1,0:T(8,128)(2,1)}, bf16[256,128]{1,0:T(8,128)(2,1)}, u32[]{:S(2)}, u32[]{:S(2)}) collective-permute-start(bf16[256,128]{1,0:T(8,128)(2,1)} %bitcast.10), channel_id=1, source_target_pairs={{1,0},{2,1},{3,2},{4,3},{5,4},{6,5},{7,6},{8,7},{9,8},{10,9},{11,1... | collective-permute-start | bytes 196616 | tf_op jit(solution)/shard_map/ppermute | solution.py:28
  84.7 4.4 %down8.1 = (f32[8,64,128]{2,1,0:T(8,128)S(1)}, bf16[2,64,128]{2,1,0:T(8,128)(2,1)}, f32[2,64,128]{2,1,0:T(8,128)S(1)}, bf16[2,64,128]{2,1,0:T(8,128)(2,1)}) custom-call(s32[36]{0:T(128)S(1)} %copy-done.16, f32[8,64,128]{2,1,0:T(8,128)S(1)} %get-tuple-element.36.f_ref, f32[8,128]{1,0:T(8,128)S(1)} %copy-done.9, s32[4,1,256]{2,1,0:T(1,128)S(1)} %bitcast.96, ...), custom_call_target="tpu_custom_call" | custom-call | flops 100663296 | bytes 786432 | tf_op jit(solution)/shard_map/down8/pallas_call | solution.py:188
  92.3 7.9 %collective-permute-start.9 = (bf16[2,64,128]{2,1,0:T(8,128)(2,1)}, bf16[2,64,128]{2,1,0:T(8,128)(2,1)}, u32[]{:S(2)}, u32[]{:S(2)}) collective-permute-start(bf16[2,64,128]{2,1,0:T(8,128)(2,1)} %get-tuple-element.24), channel_id=1, source_target_pairs={{1,0},{2,1},{3,2},{4,3},{5,4},{6,5},{7,6},{8,7},{9,8},{10,9},{11,1... | collective-permute-start | bytes 98312 | tf_op jit(solution)/shard_map/ppermute | solution.py:28
  106.3 7.9 %collective-permute-start.11 = (bf16[2,64,128]{2,1,0:T(8,128)(2,1)S(1)}, bf16[2,64,128]{2,1,0:T(8,128)(2,1)S(1)}, u32[]{:S(2)}, u32[]{:S(2)}) collective-permute-start(bf16[2,64,128]{2,1,0:T(8,128)(2,1)S(1)} %get-tuple-element.33), channel_id=1, source_target_pairs={{1,0},{2,1},{3,2},{4,3},{5,4},{6,5},{7,6},{8,7},{9,8},{10,9},{11,1... | collective-permute-start | bytes 98312 | tf_op jit(solution)/shard_map/ppermute | solution.py:28
  122.3 7.9 %collective-permute-start.13 = (bf16[2,64,128]{2,1,0:T(8,128)(2,1)S(1)}, bf16[2,64,128]{2,1,0:T(8,128)(2,1)S(1)}, u32[]{:S(2)}, u32[]{:S(2)}) collective-permute-start(bf16[2,64,128]{2,1,0:T(8,128)(2,1)S(1)} %get-tuple-element.67), channel_id=1, source_target_pairs={{1,0},{2,1},{3,2},{4,3},{5,4},{6,5},{7,6},{8,7},{9,8},{10,9},{11,1... | collective-permute-start | bytes 98312 | tf_op jit(solution)/shard_map/ppermute | solution.py:28
  143.4 7.9 %collective-permute-start.15 = (bf16[128,64]{1,0:T(8,128)(2,1)S(1)}, bf16[128,64]{1,0:T(8,128)(2,1)S(1)}, u32[]{:S(2)}, u32[]{:S(2)}) collective-permute-start(bf16[128,64]{1,0:T(8,128)(2,1)S(1)} %get-tuple-element.58), channel_id=1, source_target_pairs={{1,0},{2,1},{3,2},{4,3},{5,4},{6,5},{7,6},{8,7},{9,8},{10,9},{11,1... | collective-permute-start | bytes 49160 | tf_op jit(solution)/shard_map/ppermute | solution.py:28
  157.4 4.6 %all-to-all-start = ((bf16[32,64,128]{2,1,0:T(8,128)(2,1)}), bf16[32,64,128]{2,1,0:T(8,128)(2,1)}, u32[]{:S(2)}, u32[]{:S(2)}) async-start(bf16[32,64,128]{2,1,0:T(8,128)(2,1)} %broadcast_in_dim.8), calls=%async_computation | async-start | bytes 1048576 | tf_op jit(solution)/shard_map/all_to_all | solution.py:357
  163.3 11.2 %all-to-all-done = bf16[32,64,128]{2,1,0:T(8,128)(2,1)} async-done(((bf16[32,64,128]{2,1,0:T(8,128)(2,1)}), bf16[32,64,128]{2,1,0:T(8,128)(2,1)}, u32[]{:S(2)}, u32[]{:S(2)}) %all-to-all-start) | async-done | bytes 524320 | tf_op jit(solution)/shard_map/all_to_all | solution.py:357
  176.0 4.6 %collective-permute-start.16 = (bf16[128,64]{0,1:T(8,128)(2,1)S(1)}, bf16[128,64]{0,1:T(8,128)(2,1)S(1)}, u32[]{:S(2)}, u32[]{:S(2)}) collective-permute-start(bf16[128,64]{0,1:T(8,128)(2,1)S(1)} %fusion.12), channel_id=1, source_target_pairs={{0,1},{1,2},{2,3},{3,4},{4,5},{5,6},{6,7},{7,8},{8,9},{9,10},{10,1... | collective-permute-start | bytes 49160 | tf_op jit(solution)/shard_map/ppermute | solution.py:28
  180.6 7.2 %collective-permute-start.17 = (bf16[128,64]{0,1:T(8,128)(2,1)S(1)}, bf16[128,64]{0,1:T(8,128)(2,1)S(1)}, u32[]{:S(2)}, u32[]{:S(2)}) collective-permute-start(bf16[128,64]{0,1:T(8,128)(2,1)S(1)} %fusion.12), channel_id=1, source_target_pairs={{1,0},{2,1},{3,2},{4,3},{5,4},{6,5},{7,6},{8,7},{9,8},{10,9},{11,1... | collective-permute-start | bytes 49160 | tf_op jit(solution)/shard_map/ppermute | solution.py:28
  198.4 7.9 %collective-permute-start.19 = (bf16[2,64,128]{2,1,0:T(8,128)(2,1)S(1)}, bf16[2,64,128]{2,1,0:T(8,128)(2,1)S(1)}, u32[]{:S(2)}, u32[]{:S(2)}) collective-permute-start(bf16[2,64,128]{2,1,0:T(8,128)(2,1)S(1)} %fusion.25), channel_id=1, source_target_pairs={{1,0},{2,1},{3,2},{4,3},{5,4},{6,5},{7,6},{8,7},{9,8},{10,9},{11,1... | collective-permute-start | bytes 98312 | tf_op jit(solution)/shard_map/ppermute | solution.py:28
  214.5 7.9 %collective-permute-start.21 = (bf16[2,64,128]{2,1,0:T(8,128)(2,1)S(1)}, bf16[2,64,128]{2,1,0:T(8,128)(2,1)S(1)}, u32[]{:S(2)}, u32[]{:S(2)}) collective-permute-start(bf16[2,64,128]{2,1,0:T(8,128)(2,1)S(1)} %get-tuple-element.69), channel_id=1, source_target_pairs={{1,0},{2,1},{3,2},{4,3},{5,4},{6,5},{7,6},{8,7},{9,8},{10,9},{11,1... | collective-permute-start | bytes 98312 | tf_op jit(solution)/shard_map/ppermute | solution.py:28
  229.9 7.9 %collective-permute-start.23 = (bf16[2,64,128]{2,1,0:T(8,128)(2,1)S(1)}, bf16[2,64,128]{2,1,0:T(8,128)(2,1)S(1)}, u32[]{:S(2)}, u32[]{:S(2)}) collective-permute-start(bf16[2,64,128]{2,1,0:T(8,128)(2,1)S(1)} %add_convert_fusion.own_ref), channel_id=1, source_target_pairs={{1,0},{2,1},{3,2},{4,3},{5,4},{6,5},{7,6},{8,7},{9,8},{10,9},{11,1... | collective-permute-start | bytes 98312 | tf_op jit(solution)/shard_map/ppermute | solution.py:28
  243.8 7.9 %collective-permute-start.25 = (bf16[4,64,128]{2,1,0:T(8,128)(2,1)S(1)}, bf16[4,64,128]{2,1,0:T(8,128)(2,1)S(1)}, u32[]{:S(2)}, u32[]{:S(2)}) collective-permute-start(bf16[4,64,128]{2,1,0:T(8,128)(2,1)S(1)} %get-tuple-element.28), channel_id=1, source_target_pairs={{1,0},{2,1},{3,2},{4,3},{5,4},{6,5},{7,6},{8,7},{9,8},{10,9},{11,1... | collective-permute-start | bytes 196616 | tf_op jit(solution)/shard_map/ppermute | solution.py:28
  254.9 3.3 %up8.1.own_ref = bf16[8,64,128]{2,1,0:T(8,128)(2,1)S(1)} custom-call(s32[36]{0:T(128)S(1)} %copy-done.17, f32[8,64,128]{2,1,0:T(8,128)S(1)} %get-tuple-element.26.x_ref, bf16[4,64,128]{2,1,0:T(8,128)(2,1)S(1)} %collective-permute-done.24.xlo_ref, bf16[4,64,128]{2,1,0:T(8,128)(2,1)S(1)} %collective-permute-done.25.xhi_ref, ...), custom_call_target="tpu_custom_call" | custom-call | flops 100663296 | bytes 786432 | tf_op jit(solution)/shard_map/up8/pallas_call | solution.py:310
  260.5 7.9 %collective-permute-start.27 = (bf16[8,64,128]{2,1,0:T(8,128)(2,1)S(1)}, bf16[8,64,128]{2,1,0:T(8,128)(2,1)S(1)}, u32[]{:S(2)}, u32[]{:S(2)}) collective-permute-start(bf16[8,64,128]{2,1,0:T(8,128)(2,1)S(1)} %up8.1.own_ref), channel_id=1, source_target_pairs={{1,0},{2,1},{3,2},{4,3},{5,4},{6,5},{7,6},{8,7},{9,8},{10,9},{11,1... | collective-permute-start | bytes 393224 | tf_op jit(solution)/shard_map/ppermute | solution.py:28
  272.8 4.7 %prolong32.1 = (f32[32,64,128]{2,1,0:T(8,128)S(1)}, bf16[4,64,128]{2,1,0:T(8,128)(2,1)S(1)}, bf16[4,64,128]{2,1,0:T(8,128)(2,1)S(1)}) custom-call(s32[16,1,256]{2,1,0:T(1,128)S(1)} %bitcast.95, bf16[8,64,128]{2,1,0:T(8,128)(2,1)S(1)} %collective-permute-done.26.lo_ref, bf16[8,64,128]{2,1,0:T(8,128)(2,1)S(1)} %up8.1.own_ref, ...), custom_call_target="tpu_custom_call" | custom-call | flops 1610612736 | bytes 2097152 | tf_op jit(solution)/shard_map/prolong32/pallas_call | solution.py:239
  279.5 8.0 %collective-permute-start.29 = (bf16[4,64,128]{2,1,0:T(8,128)(2,1)S(1)}, bf16[4,64,128]{2,1,0:T(8,128)(2,1)S(1)}, u32[]{:S(2)}, u32[]{:S(2)}) collective-permute-start(bf16[4,64,128]{2,1,0:T(8,128)(2,1)S(1)} %get-tuple-element.32), channel_id=1, source_target_pairs={{1,0},{2,1},{3,2},{4,3},{5,4},{6,5},{7,6},{8,7},{9,8},{10,9},{11,1... | collective-permute-start | bytes 196616 | tf_op jit(solution)/shard_map/ppermute | solution.py:28
  289.4 5.6 %up32.1 = f32[32,64,128]{2,1,0:T(8,128)} custom-call(s32[108]{0:T(128)S(1)} %copy-done.19, f32[32,64,128]{2,1,0:T(8,128)S(1)} %get-tuple-element.30.x_ref, bf16[4,64,128]{2,1,0:T(8,128)(2,1)S(1)} %collective-permute-done.28.xlo_ref, bf16[4,64,128]{2,1,0:T(8,128)(2,1)S(1)} %collective-permute-done.29.xhi_ref, bf16[32,64,128]{2,1,0:T(8,128)(2,1)S(1)} %copy-done.4, ...), custom_call_target="tpu_custom_call" | custom-call | flops 402653184 | bytes 3145728 | tf_op jit(solution)/shard_map/up32/pallas_call | solution.py:310
  (192 shorter events, 126.1 us)
Async XLA Ops:
  6.7 35.6 %collective-permute-start = (bf16[1040,128]{1,0:T(8,128)(2,1)}, bf16[1040,128]{1,0:T(8,128)(2,1)S(1)}, u32[]{:S(2)}, u32[]{:S(2)}) collective-permute-start(bf16[1040,128]{1,0:T(8,128)(2,1)} %concatenate.33), channel_id=1, source_target_pairs={{0,1},{1,2},{2,3},{3,4},{4,5},{5,6},{6,7},{7,8},{8,9},{9,10},{10,1... | collective-permute-start | bytes 798728 | tf_op jit(solution)/shard_map/ppermute | solution.py:28
  13.2 29.0 %collective-permute-start.1 = (bf16[1040,128]{1,0:T(8,128)(2,1)}, bf16[1040,128]{1,0:T(8,128)(2,1)S(1)}, u32[]{:S(2)}, u32[]{:S(2)}) collective-permute-start(bf16[1040,128]{1,0:T(8,128)(2,1)} %concatenate.34), channel_id=1, source_target_pairs={{1,0},{2,1},{3,2},{4,3},{5,4},{6,5},{7,6},{8,7},{9,8},{10,9},{11,1... | collective-permute-start | bytes 798728 | tf_op jit(solution)/shard_map/ppermute | solution.py:28
  26.6 38.2 %collective-permute-start.2 = (bf16[784,128]{1,0:T(8,128)(2,1)}, bf16[784,128]{1,0:T(8,128)(2,1)S(1)}, u32[]{:S(2)}, u32[]{:S(2)}) collective-permute-start(bf16[784,128]{1,0:T(8,128)(2,1)} %fusion.17), channel_id=1, source_target_pairs={{0,1},{1,2},{2,3},{3,4},{4,5},{5,6},{6,7},{7,8},{8,9},{9,10},{10,1... | collective-permute-start | bytes 602120 | tf_op jit(solution)/shard_map/ppermute | solution.py:28
  32.4 32.4 %collective-permute-start.3 = (bf16[784,128]{1,0:T(8,128)(2,1)}, bf16[784,128]{1,0:T(8,128)(2,1)S(1)}, u32[]{:S(2)}, u32[]{:S(2)}) collective-permute-start(bf16[784,128]{1,0:T(8,128)(2,1)} %fusion.18), channel_id=1, source_target_pairs={{1,0},{2,1},{3,2},{4,3},{5,4},{6,5},{7,6},{8,7},{9,8},{10,9},{11,1... | collective-permute-start | bytes 602120 | tf_op jit(solution)/shard_map/ppermute | solution.py:28
  54.5 11.8 %collective-permute-start.4 = (bf16[8,64,128]{2,1,0:T(8,128)(2,1)}, bf16[8,64,128]{2,1,0:T(8,128)(2,1)}, u32[]{:S(2)}, u32[]{:S(2)}) collective-permute-start(bf16[8,64,128]{2,1,0:T(8,128)(2,1)} %get-tuple-element.20), channel_id=1, source_target_pairs={{0,1},{1,2},{2,3},{3,4},{4,5},{5,6},{6,7},{7,8},{8,9},{9,10},{10,1... | collective-permute-start | bytes 393224 | tf_op jit(solution)/shard_map/ppermute | solution.py:28
  56.4 10.4 %collective-permute-start.5 = (bf16[8,64,128]{2,1,0:T(8,128)(2,1)S(1)}, bf16[8,64,128]{2,1,0:T(8,128)(2,1)}, u32[]{:S(2)}, u32[]{:S(2)}) collective-permute-start(bf16[8,64,128]{2,1,0:T(8,128)(2,1)S(1)} %get-tuple-element.21), channel_id=1, source_target_pairs={{1,0},{2,1},{3,2},{4,3},{5,4},{6,5},{7,6},{8,7},{9,8},{10,9},{11,1... | collective-permute-start | bytes 393224 | tf_op jit(solution)/shard_map/ppermute | solution.py:28
  68.6 14.1 %collective-permute-start.6 = (bf16[256,128]{1,0:T(8,128)(2,1)}, bf16[256,128]{1,0:T(8,128)(2,1)}, u32[]{:S(2)}, u32[]{:S(2)}) collective-permute-start(bf16[256,128]{1,0:T(8,128)(2,1)} %bitcast.9), channel_id=1, source_target_pairs={{0,1},{1,2},{2,3},{3,4},{4,5},{5,6},{6,7},{7,8},{8,9},{9,10},{10,1... | collective-permute-start | bytes 196616 | tf_op jit(solution)/shard_map/ppermute | solution.py:28
  70.5 12.2 %collective-permute-start.7 = (bf16[256,128]{1,0:T(8,128)(2,1)}, bf16[256,128]{1,0:T(8,128)(2,1)}, u32[]{:S(2)}, u32[]{:S(2)}) collective-permute-start(bf16[256,128]{1,0:T(8,128)(2,1)} %bitcast.10), channel_id=1, source_target_pairs={{1,0},{2,1},{3,2},{4,3},{5,4},{6,5},{7,6},{8,7},{9,8},{10,9},{11,1... | collective-permute-start | bytes 196616 | tf_op jit(solution)/shard_map/ppermute | solution.py:28
  90.4 12.5 %collective-permute-start.8 = (bf16[2,64,128]{2,1,0:T(8,128)(2,1)}, bf16[2,64,128]{2,1,0:T(8,128)(2,1)}, u32[]{:S(2)}, u32[]{:S(2)}) collective-permute-start(bf16[2,64,128]{2,1,0:T(8,128)(2,1)} %get-tuple-element.23), channel_id=1, source_target_pairs={{0,1},{1,2},{2,3},{3,4},{4,5},{5,6},{6,7},{7,8},{8,9},{9,10},{10,1... | collective-permute-start | bytes 98312 | tf_op jit(solution)/shard_map/ppermute | solution.py:28
  92.3 10.6 %collective-permute-start.9 = (bf16[2,64,128]{2,1,0:T(8,128)(2,1)}, bf16[2,64,128]{2,1,0:T(8,128)(2,1)}, u32[]{:S(2)}, u32[]{:S(2)}) collective-permute-start(bf16[2,64,128]{2,1,0:T(8,128)(2,1)} %get-tuple-element.24), channel_id=1, source_target_pairs={{1,0},{2,1},{3,2},{4,3},{5,4},{6,5},{7,6},{8,7},{9,8},{10,9},{11,1... | collective-permute-start | bytes 98312 | tf_op jit(solution)/shard_map/ppermute | solution.py:28
  104.4 11.1 %collective-permute-start.10 = (bf16[2,64,128]{2,1,0:T(8,128)(2,1)S(1)}, bf16[2,64,128]{2,1,0:T(8,128)(2,1)S(1)}, u32[]{:S(2)}, u32[]{:S(2)}) collective-permute-start(bf16[2,64,128]{2,1,0:T(8,128)(2,1)S(1)} %get-tuple-element.33), channel_id=1, source_target_pairs={{0,1},{1,2},{2,3},{3,4},{4,5},{5,6},{6,7},{7,8},{8,9},{9,10},{10,1... | collective-permute-start | bytes 98312 | tf_op jit(solution)/shard_map/ppermute | solution.py:28
  120.4 11.1 %collective-permute-start.12 = (bf16[2,64,128]{2,1,0:T(8,128)(2,1)S(1)}, bf16[2,64,128]{2,1,0:T(8,128)(2,1)S(1)}, u32[]{:S(2)}, u32[]{:S(2)}) collective-permute-start(bf16[2,64,128]{2,1,0:T(8,128)(2,1)S(1)} %get-tuple-element.67), channel_id=1, source_target_pairs={{0,1},{1,2},{2,3},{3,4},{4,5},{5,6},{6,7},{7,8},{8,9},{9,10},{10,1... | collective-permute-start | bytes 98312 | tf_op jit(solution)/shard_map/ppermute | solution.py:28
  141.4 9.8 %collective-permute-start.14 = (bf16[128,64]{1,0:T(8,128)(2,1)S(1)}, bf16[128,64]{1,0:T(8,128)(2,1)S(1)}, u32[]{:S(2)}, u32[]{:S(2)}) collective-permute-start(bf16[128,64]{1,0:T(8,128)(2,1)S(1)} %get-tuple-element.57), channel_id=1, source_target_pairs={{0,1},{1,2},{2,3},{3,4},{4,5},{5,6},{6,7},{7,8},{8,9},{9,10},{10,1... | collective-permute-start | bytes 49160 | tf_op jit(solution)/shard_map/ppermute | solution.py:28
  157.4 17.1 %all-to-all-start = ((bf16[32,64,128]{2,1,0:T(8,128)(2,1)}), bf16[32,64,128]{2,1,0:T(8,128)(2,1)}, u32[]{:S(2)}, u32[]{:S(2)}) async-start(bf16[32,64,128]{2,1,0:T(8,128)(2,1)} %broadcast_in_dim.8), calls=%async_computation | async-start | bytes 1048576 | tf_op jit(solution)/shard_map/all_to_all | solution.py:357
  176.0 13.1 %collective-permute-start.16 = (bf16[128,64]{0,1:T(8,128)(2,1)S(1)}, bf16[128,64]{0,1:T(8,128)(2,1)S(1)}, u32[]{:S(2)}, u32[]{:S(2)}) collective-permute-start(bf16[128,64]{0,1:T(8,128)(2,1)S(1)} %fusion.12), channel_id=1, source_target_pairs={{0,1},{1,2},{2,3},{3,4},{4,5},{5,6},{6,7},{7,8},{8,9},{9,10},{10,1... | collective-permute-start | bytes 49160 | tf_op jit(solution)/shard_map/ppermute | solution.py:28
  196.5 9.8 %collective-permute-start.18 = (bf16[2,64,128]{2,1,0:T(8,128)(2,1)S(1)}, bf16[2,64,128]{2,1,0:T(8,128)(2,1)S(1)}, u32[]{:S(2)}, u32[]{:S(2)}) collective-permute-start(bf16[2,64,128]{2,1,0:T(8,128)(2,1)S(1)} %fusion.25), channel_id=1, source_target_pairs={{0,1},{1,2},{2,3},{3,4},{4,5},{5,6},{6,7},{7,8},{8,9},{9,10},{10,1... | collective-permute-start | bytes 98312 | tf_op jit(solution)/shard_map/ppermute | solution.py:28
  212.6 9.8 %collective-permute-start.20 = (bf16[2,64,128]{2,1,0:T(8,128)(2,1)S(1)}, bf16[2,64,128]{2,1,0:T(8,128)(2,1)S(1)}, u32[]{:S(2)}, u32[]{:S(2)}) collective-permute-start(bf16[2,64,128]{2,1,0:T(8,128)(2,1)S(1)} %get-tuple-element.69), channel_id=1, source_target_pairs={{0,1},{1,2},{2,3},{3,4},{4,5},{5,6},{6,7},{7,8},{8,9},{9,10},{10,1... | collective-permute-start | bytes 98312 | tf_op jit(solution)/shard_map/ppermute | solution.py:28
  228.0 9.8 %collective-permute-start.22 = (bf16[2,64,128]{2,1,0:T(8,128)(2,1)S(1)}, bf16[2,64,128]{2,1,0:T(8,128)(2,1)S(1)}, u32[]{:S(2)}, u32[]{:S(2)}) collective-permute-start(bf16[2,64,128]{2,1,0:T(8,128)(2,1)S(1)} %add_convert_fusion.own_ref), channel_id=1, source_target_pairs={{0,1},{1,2},{2,3},{3,4},{4,5},{5,6},{6,7},{7,8},{8,9},{9,10},{10,1... | collective-permute-start | bytes 98312 | tf_op jit(solution)/shard_map/ppermute | solution.py:28
  241.9 10.1 %collective-permute-start.24 = (bf16[4,64,128]{2,1,0:T(8,128)(2,1)S(1)}, bf16[4,64,128]{2,1,0:T(8,128)(2,1)S(1)}, u32[]{:S(2)}, u32[]{:S(2)}) collective-permute-start(bf16[4,64,128]{2,1,0:T(8,128)(2,1)S(1)} %get-tuple-element.27), channel_id=1, source_target_pairs={{0,1},{1,2},{2,3},{3,4},{4,5},{5,6},{6,7},{7,8},{8,9},{9,10},{10,1... | collective-permute-start | bytes 196616 | tf_op jit(solution)/shard_map/ppermute | solution.py:28
  243.8 9.8 %collective-permute-start.25 = (bf16[4,64,128]{2,1,0:T(8,128)(2,1)S(1)}, bf16[4,64,128]{2,1,0:T(8,128)(2,1)S(1)}, u32[]{:S(2)}, u32[]{:S(2)}) collective-permute-start(bf16[4,64,128]{2,1,0:T(8,128)(2,1)S(1)} %get-tuple-element.28), channel_id=1, source_target_pairs={{1,0},{2,1},{3,2},{4,3},{5,4},{6,5},{7,6},{8,7},{9,8},{10,9},{11,1... | collective-permute-start | bytes 196616 | tf_op jit(solution)/shard_map/ppermute | solution.py:28
  258.3 10.9 %collective-permute-start.26 = (bf16[8,64,128]{2,1,0:T(8,128)(2,1)S(1)}, bf16[8,64,128]{2,1,0:T(8,128)(2,1)S(1)}, u32[]{:S(2)}, u32[]{:S(2)}) collective-permute-start(bf16[8,64,128]{2,1,0:T(8,128)(2,1)S(1)} %up8.1.own_ref), channel_id=1, source_target_pairs={{0,1},{1,2},{2,3},{3,4},{4,5},{5,6},{6,7},{7,8},{8,9},{9,10},{10,1... | collective-permute-start | bytes 393224 | tf_op jit(solution)/shard_map/ppermute | solution.py:28
  260.5 10.4 %collective-permute-start.27 = (bf16[8,64,128]{2,1,0:T(8,128)(2,1)S(1)}, bf16[8,64,128]{2,1,0:T(8,128)(2,1)S(1)}, u32[]{:S(2)}, u32[]{:S(2)}) collective-permute-start(bf16[8,64,128]{2,1,0:T(8,128)(2,1)S(1)} %up8.1.own_ref), channel_id=1, source_target_pairs={{1,0},{2,1},{3,2},{4,3},{5,4},{6,5},{7,6},{8,7},{9,8},{10,9},{11,1... | collective-permute-start | bytes 393224 | tf_op jit(solution)/shard_map/ppermute | solution.py:28
  277.6 10.0 %collective-permute-start.28 = (bf16[4,64,128]{2,1,0:T(8,128)(2,1)S(1)}, bf16[4,64,128]{2,1,0:T(8,128)(2,1)S(1)}, u32[]{:S(2)}, u32[]{:S(2)}) collective-permute-start(bf16[4,64,128]{2,1,0:T(8,128)(2,1)S(1)} %get-tuple-element.31), channel_id=1, source_target_pairs={{0,1},{1,2},{2,3},{3,4},{4,5},{5,6},{6,7},{7,8},{8,9},{9,10},{10,1... | collective-permute-start | bytes 196616 | tf_op jit(solution)/shard_map/ppermute | solution.py:28
  279.5 9.9 %collective-permute-start.29 = (bf16[4,64,128]{2,1,0:T(8,128)(2,1)S(1)}, bf16[4,64,128]{2,1,0:T(8,128)(2,1)S(1)}, u32[]{:S(2)}, u32[]{:S(2)}) collective-permute-start(bf16[4,64,128]{2,1,0:T(8,128)(2,1)S(1)} %get-tuple-element.32), channel_id=1, source_target_pairs={{1,0},{2,1},{3,2},{4,3},{5,4},{6,5},{7,6},{8,7},{9,8},{10,9},{11,1... | collective-permute-start | bytes 196616 | tf_op jit(solution)/shard_map/ppermute | solution.py:28
  (39 other events, 698.9 us)

commit v2 on v1

v2 whole, which is shorter than its diff:
```python
import functools

import jax
import jax.numpy as jnp
from jax import lax
from jax.experimental import pallas as pl
from jax.experimental.pallas import tpu as pltpu
from jax.sharding import PartitionSpec as P

BS = 128
R = 64
K = 3
HB = 2
NB2 = 2
NB1 = 8
NB0 = 32
C3 = 128
AXES = ("row", "col")
EDGE = 2 * HB
ROWS = K * BS
damping = 0.8
bf16 = jnp.bfloat16
f32 = jnp.float32
i32 = jnp.int32
INV = 1.0 / (K * BS)

F_ROWS = EDGE * R
W_ROWS = HB * ROWS
TAIL = 16
EDGE1 = F_ROWS + W_ROWS + TAIL
EDGE2 = W_ROWS + TAIL
THIRD = NB2 * ROWS + TAIL
FIXED = EDGE2 + THIRD
FAR = NB2 * ROWS + 3 * TAIL


def passed_along(value, steps):
    count = lax.axis_size(AXES)
    return lax.ppermute(value, AXES, [(s, (s + steps) % count) for s in range(count)])


def both_ways(up, down, steps=1):
    return passed_along(up, steps), passed_along(down, -steps)


def in_hbm(x):
    return pltpu.with_memory_space_constraint(x, pltpu.HBM)


def vmem():
    return pl.BlockSpec(memory_space=pltpu.VMEM)


def smem():
    return pl.BlockSpec(memory_space=pltpu.SMEM)


def hbm():
    return pl.BlockSpec(memory_space=pltpu.HBM)


def shape(dims, dtype):
    return jax.ShapeDtypeStruct(dims, dtype)


def call(kernel, name, outs, in_specs, out_specs, scratch=(), mib=6, flops=0, nbytes=0):
    return pl.pallas_call(
        kernel,
        out_shape=outs,
        in_specs=in_specs,
        out_specs=out_specs,
        scratch_shapes=list(scratch),
        compiler_params=pltpu.CompilerParams(vmem_limit_bytes=mib * 1024 * 1024),
        cost_estimate=pl.CostEstimate(flops=flops, transcendentals=0, bytes_accessed=nbytes),
        name=name,
    )


def device_index():
    return lax.axis_index(AXES)


def near_row(values):
    lane = lax.broadcasted_iota(i32, (1, BS), 1)
    row = jnp.zeros((1, BS), f32)
    for i, v in enumerate(values):
        row = jnp.where(lane == i, v.astype(f32), row)
    return row


def read_near(row):
    lane = lax.broadcasted_iota(i32, (1, BS), 1)
    row = row.astype(f32)
    return [jnp.sum(jnp.where(lane == i, row, 0.0)).astype(i32) for i in range(HB * K)]


def near_of(col_ref, first, b, k):
    return col_ref[k, b] - (first + b - HB)


def column_sum(w):
    return jnp.sum(w.astype(f32), axis=0, keepdims=True)


def diagonal_rows(ref, at, stride, i):
    return ref[at + i : at + i + 1, :].astype(f32) + ref[at + stride + i : at + stride + i + 1, :].astype(f32)


def inverse(g):
    return jnp.where(g > 0, damping / g, 0.0)


def joined(v_ref, indices):
    return jnp.concatenate([v_ref[i] for i in indices], axis=1)


def product(v_ref, indices, w):
    return jnp.dot(joined(v_ref, indices), w, preferred_element_type=f32) * INV


def tail_rows(gs, nears, extra=()):
    high = [g.astype(bf16).astype(f32) for g in gs]
    low = [g - h for g, h in zip(gs, high)]
    rows = high + low + [near_row(nears)] + list(extra)
    rows = rows + [jnp.zeros((1, BS), f32)] * (TAIL - len(rows))
    return jnp.concatenate(rows, axis=0).astype(bf16)


def edge_kernel(f_hbm, w_hbm, deg_ref, col_ref, up_ref, down_ref, w_ref, sem):
    n = NB0
    first = device_index() * n
    copies = [
        pltpu.make_async_copy(w_hbm.at[pl.ds((n - EDGE) * ROWS, EDGE * ROWS)], w_ref.at[1], sem.at[0]),
        pltpu.make_async_copy(w_hbm.at[pl.ds(0, EDGE * ROWS)], w_ref.at[0], sem.at[1]),
        pltpu.make_async_copy(f_hbm.at[pl.ds((n - EDGE) * R, F_ROWS)], up_ref.at[pl.ds(0, F_ROWS)], sem.at[2]),
        pltpu.make_async_copy(f_hbm.at[pl.ds(0, F_ROWS)], down_ref.at[pl.ds(0, F_ROWS)], sem.at[3]),
        pltpu.make_async_copy(
            w_hbm.at[pl.ds((n - HB) * ROWS, W_ROWS)], up_ref.at[pl.ds(F_ROWS, W_ROWS)], sem.at[4]
        ),
        pltpu.make_async_copy(w_hbm.at[pl.ds(0, W_ROWS)], down_ref.at[pl.ds(F_ROWS, W_ROWS)], sem.at[5]),
    ]
    for c in copies:
        c.start()
    for side, ref, start, near_start in ((1, up_ref, n - EDGE, n - HB), (0, down_ref, 0, 0)):
        copies[1 - side].wait()
        gs = [
            deg_ref[start + i : start + i + 1, :] + column_sum(w_ref[side, i * ROWS : (i + 1) * ROWS, :]) * INV
            for i in range(EDGE)
        ]
        nears = [near_of(col_ref, first, near_start + i, k) for i in range(HB) for k in range(K)]
        ref[F_ROWS + W_ROWS :, :] = tail_rows(gs, nears)
    for c in copies[2:]:
        c.wait()


def first_edges(f, w, deg, col):
    return call(
        edge_kernel, "edges",
        (shape((EDGE1, BS), bf16),) * 2,
        [hbm(), hbm(), vmem(), smem()],
        (vmem(),) * 2,
        [pltpu.VMEM((2, EDGE * ROWS, BS), bf16), pltpu.SemaphoreType.DMA((6,))],
        flops=2**20, nbytes=2**21,
    )(f, w, deg, col)


def fixed_kernel(
    w1_hbm, w2_hbm, w3_hbm, deg1_ref, deg2_ref, deg3_ref, col2_ref, col3_ref, own3_ref, slot3_ref,
    g1_ref, g2_ref, g3_ref, up_ref, down_ref, w3_ref, tail_ref, w1_ref, w2_ref, sem,
):
    device = device_index()
    chunks = 4
    size = NB0 // chunks
    last3 = pltpu.make_async_copy(w3_hbm, w3_ref, sem.at[0])
    last2 = pltpu.make_async_copy(w2_hbm, w2_ref, sem.at[1])
    copies = [
        pltpu.make_async_copy(
            w2_hbm.at[pl.ds((NB1 - HB) * ROWS, W_ROWS)], up_ref.at[pl.ds(0, W_ROWS)], sem.at[2]
        ),
        pltpu.make_async_copy(w2_hbm.at[pl.ds(0, W_ROWS)], down_ref.at[pl.ds(0, W_ROWS)], sem.at[3]),
        pltpu.make_async_copy(w3_hbm, up_ref.at[pl.ds(EDGE2, W_ROWS)], sem.at[4]),
        pltpu.make_async_copy(w3_hbm, down_ref.at[pl.ds(EDGE2, W_ROWS)], sem.at[5]),
    ]
    bulk = [
        pltpu.make_async_copy(
            w1_hbm.at[pl.ds(c * size * ROWS, size * ROWS)], w1_ref.at[pl.ds(c * size * ROWS, size * ROWS)], sem.at[6 + c]
        )
        for c in range(chunks)
    ]
    for c in [last3, last2] + copies + bulk:
        c.start()
    last3.wait()
    g3 = [deg3_ref[i : i + 1, :] + column_sum(w3_ref[i * ROWS : (i + 1) * ROWS, :]) * INV for i in range(NB2)]
    for i in range(NB2):
        g3_ref[i : i + 1, :] = g3[i]
    nears = [near_of(col3_ref, device * NB2, i, k) for i in range(NB2) for k in range(K)]
    extra = [(own3_ref[i : i + 1, :] - device).astype(f32) for i in range(NB2)]
    extra = extra + [slot3_ref[i : i + 1, :].astype(f32) for i in range(NB2)]
    tail = tail_rows(g3, nears, extra)
    tail_ref[...] = tail
    up_ref[EDGE2 + W_ROWS :, :] = tail
    down_ref[EDGE2 + W_ROWS :, :] = tail
    last2.wait()
    g2 = [deg2_ref[i : i + 1, :] + column_sum(w2_ref[i * ROWS : (i + 1) * ROWS, :]) * INV for i in range(NB1)]
    for i in range(NB1):
        g2_ref[i : i + 1, :] = g2[i]
    first = device * NB1
    up_ref[W_ROWS : W_ROWS + TAIL, :] = tail_rows(
        g2[NB1 - EDGE :], [near_of(col2_ref, first, NB1 - HB + i, k) for i in range(HB) for k in range(K)]
    )
    down_ref[W_ROWS : W_ROWS + TAIL, :] = tail_rows(
        g2[:EDGE], [near_of(col2_ref, first, i, k) for i in range(HB) for k in range(K)]
    )

    def one(b, carry):
        at = pl.multiple_of(b * ROWS, ROWS)
        g1_ref[pl.ds(b, 1), :] = deg1_ref[pl.ds(b, 1), :] + column_sum(w1_ref[pl.ds(at, ROWS), :]) * INV
        return carry

    for c in range(chunks):
        bulk[c].wait()
        lax.fori_loop(c * size, (c + 1) * size, one, 0, unroll=2)
    for c in copies:
        c.wait()


def fixed_data(w1, w2, w3, deg1, deg2, deg3, col2, col3, own3, slot3):
    return call(
        fixed_kernel, "fixed",
        (
            shape((NB0, BS), f32), shape((NB1, BS), f32), shape((NB2, BS), f32),
            shape((FIXED, BS), bf16), shape((FIXED, BS), bf16),
            shape((NB2 * ROWS, BS), bf16), shape((TAIL, BS), bf16),
        ),
        [hbm()] * 3 + [vmem()] * 3 + [smem()] * 2 + [vmem()] * 2,
        (vmem(),) * 7,
        [
            pltpu.VMEM((NB0 * ROWS, BS), bf16),
            pltpu.VMEM((NB1 * ROWS, BS), bf16),
            pltpu.SemaphoreType.DMA((10,)),
        ],
        mib=10, flops=2**30, nbytes=2**22,
    )(w1, w2, w3, deg1, deg2, deg3, col2, col3, own3, slot3)


def far_kernel(w3_ref, tail_ref, lo_ref, hi_ref, out_ref):
    at = NB2 * ROWS
    out_ref[:at, :] = w3_ref[...]
    out_ref[at : at + TAIL, :] = lo_ref[FIXED - TAIL :, :]
    out_ref[at + TAIL : at + 2 * TAIL, :] = tail_ref[...]
    out_ref[at + 2 * TAIL :, :] = hi_ref[FIXED - TAIL :, :]


def far_data(w3, tail, lo, hi):
    return call(
        far_kernel, "far", shape((FAR, BS), bf16), [vmem()] * 4, vmem(), flops=2**20, nbytes=2**19
    )(w3, tail, lo, hi)


def weight_copies(w_hbm, w_ref, sem, n, chunks):
    size = n // chunks * ROWS
    return [
        pltpu.make_async_copy(w_hbm.at[pl.ds(c * size, size)], w_ref.at[pl.ds(c * size, size)], sem.at[c])
        for c in range(chunks)
    ]


def weight_of(w_ref, b):
    return w_ref[pl.ds(pl.multiple_of(b * ROWS, ROWS), ROWS), :]


def edge_starts(base, f_ref, s_ref):
    if base:
        rhs = lambda i: f_ref[i * R : (i + 1) * R, :].astype(f32)
    else:
        rhs = lambda i: f_ref[i].astype(f32)
    inv = [inverse(diagonal_rows(s_ref, base + W_ROWS, EDGE, i)) for i in range(EDGE)]
    return rhs, inv


def down_kernel(
    n, nc, base, chunks,
    col_ref, f_ref, g_ref, own_ref, slot_ref, flo_ref, fhi_ref, slo_ref, shi_ref, w_hbm,
    x_out, down_ref, mid_ref, up_ref,
    w_ref, v0_ref, v1_ref, x_ref, r_ref, acc_ref, sem,
):
    copies = weight_copies(w_hbm, w_ref, sem, n, chunks)
    for c in copies:
        c.start()
    size = n // chunks
    device = device_index()
    start = device * n

    def scale(b):
        return damping / g_ref[pl.ds(b, 1), :]

    def fill(b, carry):
        v0_ref[b + EDGE] = (f_ref[b].astype(f32) * scale(b)).astype(bf16)
        return carry

    lax.fori_loop(0, n, fill, 0, unroll=2)
    sides = []
    for side, fr, sr in ((0, flo_ref, slo_ref), (1, fhi_ref, shi_ref)):
        rhs, inv = edge_starts(base, fr, sr)
        starts = [rhs(i) * inv[i] for i in range(EDGE)]
        for i in range(EDGE):
            v0_ref[i + side * (n + EDGE)] = starts[i].astype(bf16)
        near = read_near(sr[base + W_ROWS + 2 * EDGE : base + W_ROWS + 2 * EDGE + 1, :])
        sides.append((side, sr, starts, inv, near))
    for side, sr, starts, inv, near in sides:
        for i in range(HB):
            e = i + HB * (1 - side)
            j = i + side * (n + HB)
            w = sr[base + i * ROWS : base + (i + 1) * ROWS, :]
            p = product(v0_ref, [j + near[i * K + k] for k in range(K)], w)
            v1_ref[j] = (1.2 * starts[e] + inv[e] * p).astype(bf16)

    def first(b, carry):
        p = product(v0_ref, [b + HB + near_of(col_ref, start, b, k) for k in range(K)], weight_of(w_ref, b))
        s = scale(b)
        x = 1.2 * (f_ref[b].astype(f32) * s) + s * p
        x_ref[b] = x
        v1_ref[b + HB] = x.astype(bf16)
        return carry

    for c in range(chunks):
        copies[c].wait()
        lax.fori_loop(c * size, (c + 1) * size, first, 0, unroll=4 if size % 4 == 0 else 2)
    saved = pltpu.make_async_copy(x_ref, x_out, sem.at[chunks])
    saved.start()

    def residual(b):
        p = product(v1_ref, [b + near_of(col_ref, start, b, k) for k in range(K)], weight_of(w_ref, b))
        return f_ref[b].astype(f32) - g_ref[pl.ds(b, 1), :] * x_ref[b] + p

    def second(q, carry):
        r_ref[q] = jnp.concatenate([residual(2 * q), residual(2 * q + 1)], axis=1).astype(bf16)
        return carry

    lax.fori_loop(0, n // 2, second, 0, unroll=2)

    highs = 3 * nc // 2
    group = 4
    acc_ref[...] = jnp.zeros_like(acc_ref)

    def gather(q, carry):
        left = []
        right = []
        for i in range(group):
            t = pair_targets(own_ref, slot_ref, device, nc, q * group + i)
            r = r_ref[q * group + i]
            high = t // 256
            left.append(
                jnp.concatenate([r * jnp.where(high == h, 1.0, 0.0).astype(bf16) for h in range(highs)], axis=0)
            )
            rows = lax.broadcasted_iota(i32, (256, 256), 0)
            right.append(jnp.where(rows == t % 256, 1.0, 0.0).astype(bf16))
        acc_ref[...] += lax.dot_general(
            jnp.concatenate(left, axis=1),
            jnp.concatenate(right, axis=1),
            (((1,), (1,)), ((), ())),
            preferred_element_type=f32,
        )
        return carry

    lax.fori_loop(0, n // 2 // group, gather, 0)

    for b in range(3 * nc):
        part = acc_ref[(b // 2) * R : (b // 2 + 1) * R, (b % 2) * BS : (b % 2 + 1) * BS]
        where = b // nc
        ref = (down_ref, mid_ref, up_ref)[where]
        ref[b - where * nc] = part.astype(ref.dtype)
    saved.wait()


def pair_targets(own_ref, slot_ref, device, nc, q):
    row = lambda b: (own_ref[pl.ds(b, 1), :] - device + 1) * (nc * BS) + slot_ref[pl.ds(b, 1), :]
    return jnp.concatenate([row(2 * q), row(2 * q + 1)], axis=1)


def go_down(n, nc, base, col, f, g, own, slot, f_edges, fixed, weights, mib):
    chunks = 4
    highs = 3 * nc // 2
    return call(
        functools.partial(down_kernel, n, nc, base, chunks), f"down{n}",
        (
            shape((n, R, BS), f32), shape((nc, R, BS), bf16), shape((nc, R, BS), f32), shape((nc, R, BS), bf16)
        ),
        [smem()] + [vmem()] * 8 + [hbm()],
        (hbm(), vmem(), vmem(), vmem()),
        [
            pltpu.VMEM((n * ROWS, BS), bf16),
            pltpu.VMEM((n + 2 * EDGE, R, BS), bf16),
            pltpu.VMEM((n + EDGE, R, BS), bf16),
            pltpu.VMEM((n, R, BS), f32),
            pltpu.VMEM((n // 2, R, 2 * BS), bf16),
            pltpu.VMEM((highs * R, 2 * BS), f32),
            pltpu.SemaphoreType.DMA((chunks + 1,)),
        ],
        mib=mib, flops=4 * n * R * ROWS * BS, nbytes=n * ROWS * BS * 2,
    )(col, f, g, own, slot, *f_edges, *fixed, weights)


def rhs_kernel(mid_ref, lo_ref, hi_ref, out_ref, up_ref, down_ref):
    out_ref[...] = mid_ref[...] + lo_ref[...].astype(f32) + hi_ref[...].astype(f32)
    up_ref[...] = out_ref[NB1 - EDGE :].astype(bf16)
    down_ref[...] = out_ref[:EDGE].astype(bf16)


def second_rhs(mid, lo, hi):
    return call(
        rhs_kernel, "rhs8",
        (shape((NB1, R, BS), f32), shape((EDGE, R, BS), bf16), shape((EDGE, R, BS), bf16)),
        [vmem()] * 3, (vmem(),) * 3, flops=2**18, nbytes=2**19,
    )(mid, lo, hi)


def spread(n, nc, e_ref, own_ref, slot_ref, device, x_ref, out_ref):
    highs = 3 * nc // 2

    def step(q, carry):
        t = pair_targets(own_ref, slot_ref, device, nc, q)
        rows = lax.broadcasted_iota(i32, (256, 256), 0)
        pick = jnp.where(rows == t % 256, 1.0, 0.0).astype(bf16)
        found = jnp.dot(e_ref[...], pick, preferred_element_type=f32)
        high = t // 256
        y = jnp.zeros((R, 256), f32)
        for h in range(highs):
            y = y + jnp.where(high == h, found[h * R : (h + 1) * R], 0.0)
        out_ref[2 * q] = x_ref[2 * q] + y[:, :BS]
        out_ref[2 * q + 1] = x_ref[2 * q + 1] + y[:, BS:]
        return carry

    lax.fori_loop(0, n // 2, step, 0)


def place(e_ref, b, value):
    e_ref[(b // 2) * R : (b // 2 + 1) * R, (b % 2) * BS : (b % 2 + 1) * BS] = value


def prolong_kernel(
    n, nc, own_ref, slot_ref, lo_ref, mid_ref, hi_ref, x_hbm, out_ref, first_ref, last_ref, e_ref, x_ref, sem
):
    copy = pltpu.make_async_copy(x_hbm, x_ref, sem.at[0])
    copy.start()
    for b in range(3 * nc):
        place(e_ref, b, (lo_ref, mid_ref, hi_ref)[b // nc][b % nc])
    copy.wait()
    spread(n, nc, e_ref, own_ref, slot_ref, device_index(), x_ref, out_ref)
    first_ref[...] = out_ref[:EDGE].astype(bf16)
    last_ref[...] = out_ref[n - EDGE :].astype(bf16)


def prolong(n, nc, own, slot, lo, mid, hi, x):
    return call(
        functools.partial(prolong_kernel, n, nc), f"prolong{n}",
        (shape((n, R, BS), f32), shape((EDGE, R, BS), bf16), shape((EDGE, R, BS), bf16)),
        [vmem()] * 5 + [hbm()],
        (vmem(),) * 3,
        [
            pltpu.VMEM((3 * nc // 2 * R, 2 * BS), bf16),
            pltpu.VMEM((n, R, BS), f32),
            pltpu.SemaphoreType.DMA((1,)),
        ],
        mib=12, flops=2 * n * BS * 3 * nc * BS * R, nbytes=2 * n * R * BS * 4,
    )(own, slot, lo, mid, hi, x)


def up_kernel(
    n, base, chunks,
    col_ref, x_ref, xlo_ref, xhi_ref, f_ref, g_ref, flo_ref, fhi_ref, slo_ref, shi_ref, w_hbm,
    out_ref,
    w_ref, v0_ref, v1_ref, keep_ref, sem,
):
    copies = weight_copies(w_hbm, w_ref, sem, n, chunks)
    for c in copies:
        c.start()
    size = n // chunks
    start = device_index() * n

    def fill(b, carry):
        v0_ref[b + EDGE] = x_ref[b].astype(bf16)
        return carry

    lax.fori_loop(0, n, fill, 0, unroll=2)
    v0_ref[:EDGE] = xlo_ref[...]
    v0_ref[n + EDGE :] = xhi_ref[...]
    sides = []
    for side, fr, sr, xr in ((0, flo_ref, slo_ref, xlo_ref), (1, fhi_ref, shi_ref, xhi_ref)):
        near = read_near(sr[base + W_ROWS + 2 * EDGE : base + W_ROWS + 2 * EDGE + 1, :])
        sides.append((side, sr, xr, *edge_starts(base, fr, sr), near))
    for side, sr, xr, rhs, inv, near in sides:
        for i in range(HB):
            e = i + HB * (1 - side)
            j = i + side * (n + HB)
            w = sr[base + i * ROWS : base + (i + 1) * ROWS, :]
            p = product(v0_ref, [j + near[i * K + k] for k in range(K)], w)
            v1_ref[j] = (0.2 * xr[e].astype(f32) + inv[e] * (rhs(e) + p)).astype(bf16)

    def sweep(b, x, p):
        return 0.2 * x + (damping / g_ref[pl.ds(b, 1), :]) * (f_ref[b].astype(f32) + p)

    def near(b, base):
        return [b + base + near_of(col_ref, start, b, k) for k in range(K)]

    def first(b, carry):
        x = sweep(b, x_ref[b], product(v0_ref, near(b, HB), weight_of(w_ref, b)))
        keep_ref[b] = x
        v1_ref[b + HB] = x.astype(bf16)
        return carry

    for c in range(chunks):
        copies[c].wait()
        lax.fori_loop(c * size, (c + 1) * size, first, 0, unroll=4 if size % 4 == 0 else 2)

    def second(b, carry):
        p = product(v1_ref, near(b, 0), weight_of(w_ref, b))
        out_ref[b] = sweep(b, keep_ref[b], p).astype(out_ref.dtype)
        return carry

    lax.fori_loop(0, n, second, 0, unroll=4)


def go_up(n, base, col, x, x_edges, f, g, f_edges, fixed, weights, dtype, mib):
    chunks = 4
    return call(
        functools.partial(up_kernel, n, base, chunks), f"up{n}",
        shape((n, R, BS), dtype),
        [smem()] + [vmem()] * 9 + [hbm()],
        vmem(),
        [
            pltpu.VMEM((n * ROWS, BS), bf16),
            pltpu.VMEM((n + 2 * EDGE, R, BS), bf16),
            pltpu.VMEM((n + EDGE, R, BS), bf16),
            pltpu.VMEM((n, R, BS), f32),
            pltpu.SemaphoreType.DMA((chunks,)),
        ],
        mib=mib, flops=4 * n * R * ROWS * BS, nbytes=n * ROWS * BS * 2,
    )(col, x, *x_edges, f, g, *f_edges, *fixed, weights)


def parts_kernel(low_ref, mid_ref, high_ref, out_ref):
    out_ref[:NB2] = low_ref[...]
    out_ref[NB2 : 2 * NB2] = mid_ref[...].astype(bf16)
    out_ref[2 * NB2 :] = high_ref[...]


def parts_of(low, mid, high):
    return call(
        parts_kernel, "parts", shape((3 * NB2, R, BS), bf16), [vmem()] * 3, vmem(), flops=2**17, nbytes=2**17
    )(low, mid, high)


def window_kernel(mid_ref, p_ref, lo_ref, hi_ref, f_ref, up_ref, down_ref):
    a, b = NB2, 2 * NB2
    f_ref[...] = mid_ref[...] + lo_ref[b:].astype(f32) + hi_ref[:a].astype(f32)
    own = f_ref[...].astype(bf16)
    up_ref[:a] = own
    up_ref[a:b] = (hi_ref[a:b].astype(f32) + p_ref[b:].astype(f32)).astype(bf16)
    up_ref[b:] = hi_ref[b:]
    down_ref[:a] = own
    down_ref[a:b] = (lo_ref[a:b].astype(f32) + p_ref[:a].astype(f32)).astype(bf16)
    down_ref[b:] = lo_ref[:a]


def third_window(mid, p, lo, hi):
    return call(
        window_kernel, "window",
        (shape((NB2, R, BS), f32), shape((3 * NB2, R, BS), bf16), shape((3 * NB2, R, BS), bf16)),
        [vmem()] * 4, (vmem(),) * 3, flops=2**18, nbytes=2**18,
    )(mid, p, lo, hi)


REACH = 3


def third_fixed(w3_ref, tail_ref, slo_ref, shi_ref, rlo_ref, rhi_ref):
    at = NB2 * ROWS
    tails = {0: (tail_ref, 0), -1: (slo_ref, FIXED - TAIL), 1: (shi_ref, FIXED - TAIL)}
    tails[-3], tails[-2] = (rlo_ref, at), (rlo_ref, at + TAIL)
    tails[2], tails[3] = (rhi_ref, at + TAIL), (rhi_ref, at + 2 * TAIL)
    matrices = {0: (w3_ref, 0), -1: (slo_ref, EDGE2), 1: (shi_ref, EDGE2), -2: (rlo_ref, 0), 2: (rhi_ref, 0)}
    diagonal = []
    for d in range(-REACH, REACH + 1):
        ref, at = tails[d]
        diagonal += [diagonal_rows(ref, at, NB2, i) for i in range(NB2)]
    near = {}
    for d in range(-2, 3):
        ref, at = tails[d]
        near[d] = read_near(ref[at + 2 * NB2 : at + 2 * NB2 + 1, :])

    def weights(j):
        ref, at = matrices[j // NB2 - 2]
        return ref[at + (j % NB2) * ROWS : at + (j % NB2 + 1) * ROWS, :]

    def columns(j):
        return near[j // NB2 - 2][(j % NB2) * K : (j % NB2 + 1) * K]

    def row(d, kind):
        ref, at = tails[d]
        at = at + 2 * NB2 + 1 + kind * NB2
        return jnp.concatenate([ref[at + i : at + i + 1, :] for i in range(NB2)], axis=1).astype(f32).astype(i32)

    return diagonal, weights, columns, row


def third_down_kernel(
    f_ref, p_ref, lo_ref, hi_ref, dlo_ref, dhi_ref, w3_ref, tail_ref, slo_ref, shi_ref, rlo_ref, rhi_ref,
    c_ref, z_ref,
    v0_ref, v1_ref, v2_ref,
):
    diagonal, weights, columns, row = third_fixed(w3_ref, tail_ref, slo_ref, shi_ref, rlo_ref, rhi_ref)
    a, b = NB2, 2 * NB2
    wide = lambda ref, s, i: ref[s + i].astype(f32)
    f = []
    f += [wide(dlo_ref, 0, i) for i in range(a)]
    f += [wide(dlo_ref, a, i) + wide(lo_ref, 0, i) for i in range(a)]
    f += [wide(dlo_ref, b, i) + wide(lo_ref, a, i) + wide(p_ref, 0, i) for i in range(a)]
    f += [f_ref[i] for i in range(a)]
    f += [wide(dhi_ref, b, i) + wide(hi_ref, a, i) + wide(p_ref, b, i) for i in range(a)]
    f += [wide(dhi_ref, a, i) + wide(hi_ref, b, i) for i in range(a)]
    f += [wide(dhi_ref, 0, i) for i in range(a)]
    count = len(f)
    inv = [damping / g for g in diagonal]
    start = [f[i] * inv[i] for i in range(count)]
    for i in range(count):
        v0_ref[i] = start[i].astype(bf16)
    x1 = []
    for j in range(count - 4):
        p = product(v0_ref, [j + c for c in columns(j)], weights(j))
        x1.append(1.2 * start[j + 2] + inv[j + 2] * p)
        v1_ref[j] = x1[j].astype(bf16)
    res = []
    x2 = []
    for j in range(count - 8):
        p = product(v1_ref, [j + c for c in columns(j + 2)], weights(j + 2))
        r = f[j + 4] - diagonal[j + 4] * x1[j + 2] + p
        res.append(r)
        x2.append(x1[j + 2] + inv[j + 4] * r)
        v2_ref[j] = x2[j].astype(bf16)
    left = []
    right = []
    for d in (-1, 0, 1):
        r = jnp.concatenate(res[(d + 1) * a : (d + 2) * a], axis=1)
        left.append(jnp.where(row(d, 0) == -d, r, 0.0).astype(bf16))
        rows = lax.broadcasted_iota(i32, (C3, NB2 * BS), 0)
        right.append(jnp.where(rows == row(d, 1), 1.0, 0.0).astype(bf16))
    c = lax.dot_general(
        jnp.concatenate(left, axis=1), jnp.concatenate(right, axis=1),
        (((1,), (1,)), ((), ())), preferred_element_type=f32,
    ).astype(bf16)
    for i in range(c_ref.shape[0]):
        c_ref[i] = c
    for i in range(a):
        p = product(v2_ref, [i + c for c in columns(i + 4)], weights(i + 4))
        z_ref[i] = 0.2 * x2[i + 2] + start[i + 6] + inv[i + 6] * p


def third_down(copies, *args):
    count = 2 * NB2 * REACH + NB2
    return call(
        third_down_kernel, "down2",
        (shape((copies, R, C3), bf16), shape((NB2, R, BS), f32)),
        [vmem()] * 12, (vmem(),) * 2,
        [
            pltpu.VMEM((count, R, BS), bf16), pltpu.VMEM((count - 4, R, BS), bf16), pltpu.VMEM((count - 8, R, BS), bf16)
        ],
        mib=12, flops=2**27, nbytes=2**21,
    )(*args)


def coarse_kernel(got_ref, z_ref, s_hbm, out_ref, s_ref, sem):
    count = got_ref.shape[0]
    chunks = 4
    size = count // chunks
    copies = [
        pltpu.make_async_copy(s_hbm.at[:, pl.ds(c * size * BS, size * BS)], s_ref.at[c], sem.at[c])
        for c in range(chunks)
    ]
    for c in copies:
        c.start()
    u = jnp.zeros((R, C3), f32)
    for c in range(chunks):
        copies[c].wait()
        u = u + lax.dot_general(
            joined(got_ref, range(c * size, (c + 1) * size)), s_ref[c],
            (((1,), (1,)), ((), ())), preferred_element_type=f32,
        )
    out_ref[0] = u.astype(bf16)
    out_ref[1:] = z_ref[...].astype(bf16)


def coarse_solve(got, z, inverse_rows):
    count = got.shape[0]
    return call(
        coarse_kernel, "coarse", shape((1 + NB2, R, BS), bf16),
        [vmem(), vmem(), hbm()], vmem(),
        [pltpu.VMEM((4, C3, count // 4 * BS), bf16), pltpu.SemaphoreType.DMA((4,))],
        flops=2**26, nbytes=2**21,
    )(got, z, inverse_rows)


def three_kernel(lo_ref, own_ref, hi_ref, out_ref):
    out_ref[0] = lo_ref[0]
    out_ref[1] = own_ref[0]
    out_ref[2] = hi_ref[0]


def three_of(lo, own, hi):
    return call(
        three_kernel, "three", shape((3, R, BS), bf16), [vmem()] * 3, vmem(), flops=2**15, nbytes=2**16
    )(lo, own, hi)


def third_up_kernel(
    own_ref, lo_ref, hi_ref, ulo_ref, uhi_ref, z_ref, w3_ref, tail_ref, slo_ref, shi_ref, rlo_ref, rhi_ref,
    own2_ref, slot2_ref, x_hbm,
    out_ref, first_ref, last_ref,
    v0_ref, v1_ref, e_ref, x_ref, sem,
):
    copy = pltpu.make_async_copy(x_hbm, x_ref, sem.at[0])
    copy.start()
    diagonal, weights, columns, row = third_fixed(w3_ref, tail_ref, slo_ref, shi_ref, rlo_ref, rhi_ref)
    inv = [damping / g for g in diagonal]
    u = [ulo_ref[0], ulo_ref[1], ulo_ref[2], lo_ref[0], own_ref[0], hi_ref[0], uhi_ref[0], uhi_ref[1], uhi_ref[2]]
    y = []
    for d in range(-REACH, REACH + 1):
        rows = lax.broadcasted_iota(i32, (C3, NB2 * BS), 0)
        pick = jnp.where(rows == row(d, 1), 1.0, 0.0).astype(bf16)
        at = d + REACH
        found = jnp.dot(jnp.concatenate(u[at : at + 3], axis=0), pick, preferred_element_type=f32)
        owner = row(d, 0)
        got = jnp.zeros((R, NB2 * BS), f32)
        for i in range(3):
            got = got + jnp.where(owner == i - 1, found[i * R : (i + 1) * R], 0.0)
        y += [got[:, i * BS : (i + 1) * BS] for i in range(NB2)]
    count = len(y)
    for i in range(count):
        v0_ref[i] = y[i].astype(bf16)
    y1 = []
    for j in range(count - 4):
        p = product(v0_ref, [j + c for c in columns(j)], weights(j))
        y1.append(0.2 * y[j + 2] + inv[j + 2] * p)
        v1_ref[j] = y1[j].astype(bf16)
    for j in range(count - 8):
        p = product(v1_ref, [j + c for c in columns(j + 2)], weights(j + 2))
        y2 = 0.2 * y1[j + 2] + inv[j + 4] * p
        i = j % NB2
        z = (lambda: lo_ref[1 + i].astype(f32), lambda: z_ref[i], lambda: hi_ref[1 + i].astype(f32))[j // NB2]()
        place(e_ref, j, (z + y2).astype(bf16))
    copy.wait()
    spread(NB1, NB2, e_ref, own2_ref, slot2_ref, device_index(), x_ref, out_ref)
    first_ref[...] = out_ref[:EDGE].astype(bf16)
    last_ref[...] = out_ref[NB1 - EDGE :].astype(bf16)


def third_up(*args):
    count = 2 * NB2 * REACH + NB2
    return call(
        third_up_kernel, "up2",
        (shape((NB1, R, BS), f32), shape((EDGE, R, BS), bf16), shape((EDGE, R, BS), bf16)),
        [vmem()] * 14 + [hbm()], (vmem(),) * 3,
        [
            pltpu.VMEM((count, R, BS), bf16), pltpu.VMEM((count - 4, R, BS), bf16),
            pltpu.VMEM((3 * NB2 // 2 * R, 2 * BS), bf16), pltpu.VMEM((NB1, R, BS), f32),
            pltpu.SemaphoreType.DMA((1,)),
        ],
        mib=12, flops=2**27, nbytes=2**21,
    )(*args)


def on_device(
    right_sides,
    weights_fine, columns_fine, degree_fine, owners_fine, slots_fine,
    weights_second, columns_second, degree_second, owners_second, slots_second,
    weights_third, columns_third, degree_third, owners_third, slots_third,
    coarse_inverse,
):
    flat = lambda a: a.reshape(-1, BS)
    f = right_sides
    columns_fine, columns_second, columns_third = columns_fine.T, columns_second.T, columns_third.T
    w1, w2, w3 = (in_hbm(flat(w)) for w in (weights_fine, weights_second, weights_third))
    coarse_inverse = in_hbm(coarse_inverse)
    edges1 = both_ways(*first_edges(in_hbm(flat(f)), w1, degree_fine, columns_fine))
    g1, g2, _, up, down, w3, tail = fixed_data(
        w1, w2, w3, degree_fine, degree_second, degree_third, columns_second, columns_third, owners_third, slots_third
    )
    fixed = both_ways(up, down)
    far = far_data(w3, tail, *fixed)
    far = both_ways(far, far, 2)
    third = (w3, tail, *fixed, *far)

    x1, low, mid, high = go_down(
        NB0, NB1, F_ROWS, columns_fine, f, g1, owners_fine, slots_fine, edges1, edges1, w1, 20
    )
    lo, hi = both_ways(high, low)
    f2, up, down = second_rhs(mid, lo, hi)
    f_edges = both_ways(up, down)
    x2, low, mid, high = go_down(
        NB1, NB2, 0, columns_second, f2, g2, owners_second, slots_second, f_edges, fixed, w2, 12
    )
    parts = parts_of(low, mid, high)
    plo, phi = both_ways(parts, parts)
    f3, up, down = third_window(mid, parts, plo, phi)
    dlo, dhi = both_ways(up, down, 3)
    c, z = third_down(lax.axis_size("col"), f3, parts, plo, phi, dlo, dhi, *third)
    got = lax.all_to_all(c, "col", 0, 0, tiled=True)
    own = coarse_solve(got, z, coarse_inverse)
    lo, hi = both_ways(own, own)
    near = three_of(lo, own, hi)
    ulo, uhi = both_ways(near, near, 3)
    x2, first, last = third_up(own, lo, hi, ulo, uhi, z, *third, owners_second, slots_second, x2)
    x_edges = both_ways(last, first)
    x2 = go_up(NB1, 0, columns_second, x2, x_edges, f2, g2, f_edges, fixed, w2, bf16, 12)
    lo, hi = both_ways(x2, x2)
    x1, first, last = prolong(NB0, NB1, owners_fine, slots_fine, lo, x2, hi, x1)
    x_edges = both_ways(last, first)
    return go_up(NB0, F_ROWS, columns_fine, x1, x_edges, f, g1, edges1, edges1, w1, f32, 20)


def solution(mesh):
    block = P(AXES, None, None)
    pair = P(AXES, None)
    four = P(AXES, None, None, None)
    level = (four, pair, pair, pair, pair)
    return jax.shard_map(
        on_device, mesh=mesh, in_specs=(block, *level, *level, *level, pair), out_specs=block, check_vma=False
    )
```

time: 297 us -> 184 us (0.62)
  the two profiles are of different devices: /device:TPU:6 before, /device:TPU:0 now
where the time goes in v2:
time: 184 us
  starting transfers between devices  82.5 us (45%)
  waiting for transfers between devices  45.7 us (25%)
  Pallas kernels  35.5 us (19%)
  blocking collectives  18 us (10%)
    ppermute x24, starting transfers between devices, passed_along(): lax.ppermute(value, AXES, [(s, (s + steps) % count) for s in range(count)])  82.5 us
    ppermute x24, waiting for transfers between devices, passed_along(): lax.ppermute(value, AXES, [(s, (s + steps) % count) for s in range(count)])  45.7 us
    all_to_all x1, blocking collectives, on_device(): got = lax.all_to_all(c, 'col', 0, 0, tiled=True)  18 us
    pallas_call x2, Pallas kernels, go_down(): call(functools.partial(down_kernel, n, nc, base, chunks), f'down{n}', (sh...  11 us
    pallas_call x2, Pallas kernels, go_up(): call(functools.partial(up_kernel, n, base, chunks), f'up{n}', shape((n, R...  8.93 us
    pallas_call x1, Pallas kernels, prolong(): call(functools.partial(prolong_kernel, n, nc), f'prolong{n}', (shape((n,...  5.01 us
    pallas_call x1, Pallas kernels, fixed_data(): call(fixed_kernel, 'fixed', (shape((NB0, BS), f32), shape((NB1, BS), f32)...  3.97 us
  transfers between devices with their start and end apart: 24, of which 12 were waited for; matrix products, arithmetic and copies ran while one was open for 0% of the time, Pallas kernels for 8%

profile of v2, /device:TPU:0, one launch (start us, length us, event | category | flops | bytes accessed | tf_op | source)
XLA Modules:
  0.0 183.9 jit_solution(4502558025445964708)
XLA Ops:
  3.7 8.1 %collective-permute-start.1 = (bf16[1040,128]{1,0:T(8,128)(2,1)S(1)}, bf16[1040,128]{1,0:T(8,128)(2,1)S(1)}, u32[]{:S(2)}, u32[]{:S(2)}) collective-permute-start(bf16[1040,128]{1,0:T(8,128)(2,1)S(1)} %get-tuple-element.37), channel_id=1, source_target_pairs={{0,255},{1,0},{2,1},{3,2},{4,3},{5,4},{6,5},{7,6},{8,7},{9,8},{10,... | collective-permute-start | bytes 798728 | tf_op jit(solution)/shard_map/ppermute | solution.py:39
  12.0 4.0 %fixed.1 = (f32[32,128]{1,0:T(8,128)S(1)}, f32[8,128]{1,0:T(8,128)S(1)}, f32[2,128]{1,0:T(2,128)}, bf16[1568,128]{1,0:T(8,128)(2,1)S(1)}, bf16[1568,128]{1,0:T(8...) custom-call(bf16[12288,128]{1,0:T(8,128)(2,1)} %bitcast.16, bf16[3072,128]{1,0:T(8,128)(2,1)} %bitcast.19, ...), custom_call_target="tpu_custom_call" | custom-call | flops 1073741824 | bytes 4194304 | tf_op jit(solution)/shard_map/fixed/pallas_call | solution.py:228
  16.1 7.2 %collective-permute-start.7 = (bf16[1568,128]{1,0:T(8,128)(2,1)S(1)}, bf16[1568,128]{1,0:T(8,128)(2,1)S(1)}, u32[]{:S(2)}, u32[]{:S(2)}) collective-permute-start(bf16[1568,128]{1,0:T(8,128)(2,1)S(1)} %get-tuple-element.46), channel_id=1, source_target_pairs={{0,255},{1,0},{2,1},{3,2},{4,3},{5,4},{6,5},{7,6},{8,7},{9,8},{10,... | collective-permute-start | bytes 1204232 | tf_op jit(solution)/shard_map/ppermute | solution.py:39
  23.3 7.9 %down32.1 = (f32[32,64,128]{2,1,0:T(8,128)S(1)}, bf16[8,64,128]{2,1,0:T(8,128)(2,1)S(1)}, f32[8,64,128]{2,1,0:T(8,128)S(1)}, bf16[8,64,128]{2,1,0:T(8,128)(2,1)S(1)}) custom-call(s32[3,32]{1,0:T(4,128)S(1)} %bitcast.9, bf16[32,64,128]{2,1,0:T(8,128)(2,1)S(1)} %copy-done, f32[32,128]{1,0:T(8,128)S(1)} %get-tuple-element.35.g_ref, s32[32,128]{1,0:T(8,128)S(1)} %copy-done.6, ...), custom_call_target="tpu_custom_call" | custom-call | flops 402653184 | bytes 3145728 | tf_op jit(solution)/shard_map/down32/pallas_call | solution.py:384
  31.3 7.2 %collective-permute-start.3 = (bf16[8,64,128]{2,1,0:T(8,128)(2,1)S(1)}, bf16[8,64,128]{2,1,0:T(8,128)(2,1)S(1)}, u32[]{:S(2)}, u32[]{:S(2)}) collective-permute-start(bf16[8,64,128]{2,1,0:T(8,128)(2,1)S(1)} %get-tuple-element.40), channel_id=1, source_target_pairs={{0,255},{1,0},{2,1},{3,2},{4,3},{5,4},{6,5},{7,6},{8,7},{9,8},{10,... | collective-permute-start | bytes 393224 | tf_op jit(solution)/shard_map/ppermute | solution.py:39
  38.5 2.6 %collective-permute-done.2.lo_ref = bf16[8,64,128]{2,1,0:T(8,128)(2,1)S(1)} collective-permute-done((bf16[8,64,128]{2,1,0:T(8,128)(2,1)S(1)}, bf16[8,64,128]{2,1,0:T(8,128)(2,1)S(1)}, u32[]{:S(2)}, u32[]{:S(2)}) %collective-permute-start.2) | collective-permute-done | bytes 131104 | tf_op jit(solution)/shard_map/ppermute | solution.py:39
  41.3 7.2 %collective-permute-start.5 = (bf16[4,64,128]{2,1,0:T(8,128)(2,1)S(1)}, bf16[4,64,128]{2,1,0:T(8,128)(2,1)S(1)}, u32[]{:S(2)}, u32[]{:S(2)}) collective-permute-start(bf16[4,64,128]{2,1,0:T(8,128)(2,1)S(1)} %get-tuple-element.44), channel_id=1, source_target_pairs={{0,255},{1,0},{2,1},{3,2},{4,3},{5,4},{6,5},{7,6},{8,7},{9,8},{10,... | collective-permute-start | bytes 196616 | tf_op jit(solution)/shard_map/ppermute | solution.py:39
  51.6 3.1 %down8.1 = (f32[8,64,128]{2,1,0:T(8,128)S(1)}, bf16[2,64,128]{2,1,0:T(8,128)(2,1)S(1)}, f32[2,64,128]{2,1,0:T(8,128)S(1)}, bf16[2,64,128]{2,1,0:T(8,128)(2,1)S(1)}) custom-call(s32[3,8]{1,0:T(4,128)S(1)} %bitcast.12, f32[8,64,128]{2,1,0:T(8,128)S(1)} %get-tuple-element.41.f_ref, f32[8,128]{1,0:T(8,128)S(1)} %get-tuple-element.42.g_ref, ...), custom_call_target="tpu_custom_call" | custom-call | flops 100663296 | bytes 786432 | tf_op jit(solution)/shard_map/down8/pallas_call | solution.py:384
  54.7 6.6 %collective-permute-start.9 = (bf16[6,64,128]{2,1,0:T(8,128)(2,1)S(1)}, bf16[6,64,128]{2,1,0:T(8,128)(2,1)S(1)}, u32[]{:S(2)}, u32[]{:S(2)}) collective-permute-start(bf16[6,64,128]{2,1,0:T(8,128)(2,1)S(1)} %parts.1.p_ref), channel_id=1, source_target_pairs={{0,255},{1,0},{2,1},{3,2},{4,3},{5,4},{6,5},{7,6},{8,7},{9,8},{10,... | collective-permute-start | bytes 294920 | tf_op jit(solution)/shard_map/ppermute | solution.py:39
  61.3 2.6 %collective-permute-done.9.hi_ref = bf16[6,64,128]{2,1,0:T(8,128)(2,1)S(1)} collective-permute-done((bf16[6,64,128]{2,1,0:T(8,128)(2,1)S(1)}, bf16[6,64,128]{2,1,0:T(8,128)(2,1)S(1)}, u32[]{:S(2)}, u32[]{:S(2)}) %collective-permute-start.9) | collective-permute-done | bytes 98336 | tf_op jit(solution)/shard_map/ppermute | solution.py:39
  63.8 7.7 %collective-permute-done.8.lo_ref = bf16[6,64,128]{2,1,0:T(8,128)(2,1)S(1)} collective-permute-done((bf16[6,64,128]{2,1,0:T(8,128)(2,1)S(1)}, bf16[6,64,128]{2,1,0:T(8,128)(2,1)S(1)}, u32[]{:S(2)}, u32[]{:S(2)}) %collective-permute-start.8) | collective-permute-done | bytes 98336 | tf_op jit(solution)/shard_map/ppermute | solution.py:39
  71.7 9.0 %collective-permute-start.11 = (bf16[6,64,128]{2,1,0:T(8,128)(2,1)S(1)}, bf16[6,64,128]{2,1,0:T(8,128)(2,1)S(1)}, u32[]{:S(2)}, u32[]{:S(2)}) collective-permute-start(bf16[6,64,128]{2,1,0:T(8,128)(2,1)S(1)} %get-tuple-element.52), channel_id=1, source_target_pairs={{0,253},{1,254},{2,255},{3,0},{4,1},{5,2},{6,3},{7,4},{8,5},{9,6},... | collective-permute-start | bytes 294920 | tf_op jit(solution)/shard_map/ppermute | solution.py:39
  83.9 18.0 %all_to_all.5.got_ref = bf16[32,64,128]{2,1,0:T(8,128)(2,1)S(1)} all-to-all(bf16[32,64,128]{2,1,0:T(8,128)(2,1)S(1)} %get-tuple-element.55), channel_id=1, replica_groups=mesh['row'=8,'col'=32] {'col'}, dimensions={0} | all-to-all | bytes 1048576 | tf_op jit(solution)/shard_map/all_to_all | solution.py:807
  103.8 7.3 %collective-permute-start.15 = (bf16[3,64,128]{2,1,0:T(8,128)(2,1)S(1)}, bf16[3,64,128]{2,1,0:T(8,128)(2,1)S(1)}, u32[]{:S(2)}, u32[]{:S(2)}) collective-permute-start(bf16[3,64,128]{2,1,0:T(8,128)(2,1)S(1)} %coarse.1.own_ref), channel_id=1, source_target_pairs={{0,255},{1,0},{2,1},{3,2},{4,3},{5,4},{6,5},{7,6},{8,7},{9,8},{10,... | collective-permute-start | bytes 147464 | tf_op jit(solution)/shard_map/ppermute | solution.py:39
  112.9 7.2 %collective-permute-done.14.lo_ref = bf16[3,64,128]{2,1,0:T(8,128)(2,1)S(1)} collective-permute-done((bf16[3,64,128]{2,1,0:T(8,128)(2,1)S(1)}, bf16[3,64,128]{2,1,0:T(8,128)(2,1)S(1)}, u32[]{:S(2)}, u32[]{:S(2)}) %collective-permute-start.14) | collective-permute-done | bytes 49184 | tf_op jit(solution)/shard_map/ppermute | solution.py:39
  120.1 3.8 %collective-permute-start.16 = (bf16[3,64,128]{2,1,0:T(8,128)(2,1)S(1)}, bf16[3,64,128]{2,1,0:T(8,128)(2,1)S(1)}, u32[]{:S(2)}, u32[]{:S(2)}) collective-permute-start(bf16[3,64,128]{2,1,0:T(8,128)(2,1)S(1)} %three.1), channel_id=1, source_target_pairs={{0,3},{1,4},{2,5},{3,6},{4,7},{5,8},{6,9},{7,10},{8,11},{9,12},{10... | collective-permute-start | bytes 147464 | tf_op jit(solution)/shard_map/ppermute | solution.py:39
  126.0 5.1 %collective-permute-done.16.ulo_ref = bf16[3,64,128]{2,1,0:T(8,128)(2,1)S(1)} collective-permute-done((bf16[3,64,128]{2,1,0:T(8,128)(2,1)S(1)}, bf16[3,64,128]{2,1,0:T(8,128)(2,1)S(1)}, u32[]{:S(2)}, u32[]{:S(2)}) %collective-permute-start.16) | collective-permute-done | bytes 49184 | tf_op jit(solution)/shard_map/ppermute | solution.py:39
  133.0 7.2 %collective-permute-start.19 = (bf16[4,64,128]{2,1,0:T(8,128)(2,1)S(1)}, bf16[4,64,128]{2,1,0:T(8,128)(2,1)S(1)}, u32[]{:S(2)}, u32[]{:S(2)}) collective-permute-start(bf16[4,64,128]{2,1,0:T(8,128)(2,1)S(1)} %get-tuple-element.60), channel_id=1, source_target_pairs={{0,255},{1,0},{2,1},{3,2},{4,3},{5,4},{6,5},{7,6},{8,7},{9,8},{10,... | collective-permute-start | bytes 196616 | tf_op jit(solution)/shard_map/ppermute | solution.py:39
  142.1 2.7 %up8.1.mid_ref = bf16[8,64,128]{2,1,0:T(8,128)(2,1)S(1)} custom-call(s32[3,8]{1,0:T(4,128)S(1)} %bitcast.13, f32[8,64,128]{2,1,0:T(8,128)S(1)} %get-tuple-element.58.x_ref, bf16[4,64,128]{2,1,0:T(8,128)(2,1)S(1)} %collective-permute-done.18.xlo_ref, bf16[4,64,128]{2,1,0:T(8,128)(2,1)S(1)} %collective-permute-done.19.xhi_ref, ...), custom_call_target="tpu_custom_call" | custom-call | flops 100663296 | bytes 786432 | tf_op jit(solution)/shard_map/up8/pallas_call | solution.py:526
  144.8 8.0 %collective-permute-start.21 = (bf16[8,64,128]{2,1,0:T(8,128)(2,1)S(1)}, bf16[8,64,128]{2,1,0:T(8,128)(2,1)S(1)}, u32[]{:S(2)}, u32[]{:S(2)}) collective-permute-start(bf16[8,64,128]{2,1,0:T(8,128)(2,1)S(1)} %up8.1.mid_ref), channel_id=1, source_target_pairs={{0,255},{1,0},{2,1},{3,2},{4,3},{5,4},{6,5},{7,6},{8,7},{9,8},{10,... | collective-permute-start | bytes 393224 | tf_op jit(solution)/shard_map/ppermute | solution.py:39
  155.3 8.0 %collective-permute-done.20.lo_ref = bf16[8,64,128]{2,1,0:T(8,128)(2,1)S(1)} collective-permute-done((bf16[8,64,128]{2,1,0:T(8,128)(2,1)S(1)}, bf16[8,64,128]{2,1,0:T(8,128)(2,1)S(1)}, u32[]{:S(2)}, u32[]{:S(2)}) %collective-permute-start.20) | collective-permute-done | bytes 131104 | tf_op jit(solution)/shard_map/ppermute | solution.py:39
  163.3 5.0 %prolong32.1 = (f32[32,64,128]{2,1,0:T(8,128)S(1)}, bf16[4,64,128]{2,1,0:T(8,128)(2,1)S(1)}, bf16[4,64,128]{2,1,0:T(8,128)(2,1)S(1)}) custom-call(s32[32,128]{1,0:T(8,128)S(1)} %copy-done.6, s32[32,128]{1,0:T(8,128)S(1)} %copy-done.7, bf16[8,64,128]{2,1,0:T(8,128)(2,1)S(1)} %collective-permute-done.20.lo_ref, bf16[8,64,128]{2,1,0:T(8,128)(2,1)S(1)} %up8.1.mid_ref, ...), custom_call_target="tpu_custom_call" | custom-call | flops 1610612736 | bytes 2097152 | tf_op jit(solution)/shard_map/prolong32/pallas_call | solution.py:455
  168.4 7.2 %collective-permute-start.23 = (bf16[4,64,128]{2,1,0:T(8,128)(2,1)S(1)}, bf16[4,64,128]{2,1,0:T(8,128)(2,1)S(1)}, u32[]{:S(2)}, u32[]{:S(2)}) collective-permute-start(bf16[4,64,128]{2,1,0:T(8,128)(2,1)S(1)} %get-tuple-element.64), channel_id=1, source_target_pairs={{0,255},{1,0},{2,1},{3,2},{4,3},{5,4},{6,5},{7,6},{8,7},{9,8},{10,... | collective-permute-start | bytes 196616 | tf_op jit(solution)/shard_map/ppermute | solution.py:39
  177.5 6.2 %up32.1 = f32[32,64,128]{2,1,0:T(8,128)} custom-call(s32[3,32]{1,0:T(4,128)S(1)} %bitcast.10, f32[32,64,128]{2,1,0:T(8,128)S(1)} %get-tuple-element.62.x_ref, bf16[4,64,128]{2,1,0:T(8,128)(2,1)S(1)} %collective-permute-done.22.xlo_ref, bf16[4,64,128]{2,1,0:T(8,128)(2,1)S(1)} %collective-permute-done.23.xhi_ref, bf16[32,64,128]{2,1,0:T(8,128)(2,1)S(1)} %copy-done, ...), custom_call_target="tpu_custom_call" | custom-call | flops 402653184 | bytes 3145728 | tf_op jit(solution)/shard_map/up32/pallas_call | solution.py:526
  (71 shorter events, 24.6 us)
Async XLA Ops:
  3.4 19.8 %collective-permute-start = (bf16[1040,128]{1,0:T(8,128)(2,1)S(1)}, bf16[1040,128]{1,0:T(8,128)(2,1)S(1)}, u32[]{:S(2)}, u32[]{:S(2)}) collective-permute-start(bf16[1040,128]{1,0:T(8,128)(2,1)S(1)} %get-tuple-element.36), channel_id=1, source_target_pairs={{0,1},{1,2},{2,3},{3,4},{4,5},{5,6},{6,7},{7,8},{8,9},{9,10},{10,1... | collective-permute-start | bytes 798728 | tf_op jit(solution)/shard_map/ppermute | solution.py:39
  3.7 19.5 %collective-permute-start.1 = (bf16[1040,128]{1,0:T(8,128)(2,1)S(1)}, bf16[1040,128]{1,0:T(8,128)(2,1)S(1)}, u32[]{:S(2)}, u32[]{:S(2)}) collective-permute-start(bf16[1040,128]{1,0:T(8,128)(2,1)S(1)} %get-tuple-element.37), channel_id=1, source_target_pairs={{0,255},{1,0},{2,1},{3,2},{4,3},{5,4},{6,5},{7,6},{8,7},{9,8},{10,... | collective-permute-start | bytes 798728 | tf_op jit(solution)/shard_map/ppermute | solution.py:39
  16.0 32.6 %collective-permute-start.6 = (bf16[1568,128]{1,0:T(8,128)(2,1)S(1)}, bf16[1568,128]{1,0:T(8,128)(2,1)S(1)}, u32[]{:S(2)}, u32[]{:S(2)}) collective-permute-start(bf16[1568,128]{1,0:T(8,128)(2,1)S(1)} %get-tuple-element.45), channel_id=1, source_target_pairs={{0,1},{1,2},{2,3},{3,4},{4,5},{5,6},{6,7},{7,8},{8,9},{9,10},{10,1... | collective-permute-start | bytes 1204232 | tf_op jit(solution)/shard_map/ppermute | solution.py:39
  16.1 32.5 %collective-permute-start.7 = (bf16[1568,128]{1,0:T(8,128)(2,1)S(1)}, bf16[1568,128]{1,0:T(8,128)(2,1)S(1)}, u32[]{:S(2)}, u32[]{:S(2)}) collective-permute-start(bf16[1568,128]{1,0:T(8,128)(2,1)S(1)} %get-tuple-element.46), channel_id=1, source_target_pairs={{0,255},{1,0},{2,1},{3,2},{4,3},{5,4},{6,5},{7,6},{8,7},{9,8},{10,... | collective-permute-start | bytes 1204232 | tf_op jit(solution)/shard_map/ppermute | solution.py:39
  31.2 9.9 %collective-permute-start.2 = (bf16[8,64,128]{2,1,0:T(8,128)(2,1)S(1)}, bf16[8,64,128]{2,1,0:T(8,128)(2,1)S(1)}, u32[]{:S(2)}, u32[]{:S(2)}) collective-permute-start(bf16[8,64,128]{2,1,0:T(8,128)(2,1)S(1)} %get-tuple-element.39), channel_id=1, source_target_pairs={{0,1},{1,2},{2,3},{3,4},{4,5},{5,6},{6,7},{7,8},{8,9},{9,10},{10,1... | collective-permute-start | bytes 393224 | tf_op jit(solution)/shard_map/ppermute | solution.py:39
  31.3 9.8 %collective-permute-start.3 = (bf16[8,64,128]{2,1,0:T(8,128)(2,1)S(1)}, bf16[8,64,128]{2,1,0:T(8,128)(2,1)S(1)}, u32[]{:S(2)}, u32[]{:S(2)}) collective-permute-start(bf16[8,64,128]{2,1,0:T(8,128)(2,1)S(1)} %get-tuple-element.40), channel_id=1, source_target_pairs={{0,255},{1,0},{2,1},{3,2},{4,3},{5,4},{6,5},{7,6},{8,7},{9,8},{10,... | collective-permute-start | bytes 393224 | tf_op jit(solution)/shard_map/ppermute | solution.py:39
  41.2 10.4 %collective-permute-start.4 = (bf16[4,64,128]{2,1,0:T(8,128)(2,1)S(1)}, bf16[4,64,128]{2,1,0:T(8,128)(2,1)S(1)}, u32[]{:S(2)}, u32[]{:S(2)}) collective-permute-start(bf16[4,64,128]{2,1,0:T(8,128)(2,1)S(1)} %get-tuple-element.43), channel_id=1, source_target_pairs={{0,1},{1,2},{2,3},{3,4},{4,5},{5,6},{6,7},{7,8},{8,9},{9,10},{10,1... | collective-permute-start | bytes 196616 | tf_op jit(solution)/shard_map/ppermute | solution.py:39
  41.3 10.3 %collective-permute-start.5 = (bf16[4,64,128]{2,1,0:T(8,128)(2,1)S(1)}, bf16[4,64,128]{2,1,0:T(8,128)(2,1)S(1)}, u32[]{:S(2)}, u32[]{:S(2)}) collective-permute-start(bf16[4,64,128]{2,1,0:T(8,128)(2,1)S(1)} %get-tuple-element.44), channel_id=1, source_target_pairs={{0,255},{1,0},{2,1},{3,2},{4,3},{5,4},{6,5},{7,6},{8,7},{9,8},{10,... | collective-permute-start | bytes 196616 | tf_op jit(solution)/shard_map/ppermute | solution.py:39
  48.5 32.1 %collective-permute-start.13 = (bf16[816,128]{1,0:T(8,128)(2,1)S(1)}, bf16[816,128]{1,0:T(8,128)(2,1)S(1)}, u32[]{:S(2)}, u32[]{:S(2)}) collective-permute-start(bf16[816,128]{1,0:T(8,128)(2,1)S(1)} %far.1), channel_id=1, source_target_pairs={{0,254},{1,255},{2,0},{3,1},{4,2},{5,3},{6,4},{7,5},{8,6},{9,7},{1... | collective-permute-start | bytes 626696 | tf_op jit(solution)/shard_map/ppermute | solution.py:39
  49.7 30.9 %collective-permute-start.12 = (bf16[816,128]{1,0:T(8,128)(2,1)S(1)}, bf16[816,128]{1,0:T(8,128)(2,1)S(1)}, u32[]{:S(2)}, u32[]{:S(2)}) collective-permute-start(bf16[816,128]{1,0:T(8,128)(2,1)S(1)} %far.1), channel_id=1, source_target_pairs={{0,2},{1,3},{2,4},{3,5},{4,6},{5,7},{6,8},{7,9},{8,10},{9,11},{10,... | collective-permute-start | bytes 626696 | tf_op jit(solution)/shard_map/ppermute | solution.py:39
  54.7 9.2 %collective-permute-start.9 = (bf16[6,64,128]{2,1,0:T(8,128)(2,1)S(1)}, bf16[6,64,128]{2,1,0:T(8,128)(2,1)S(1)}, u32[]{:S(2)}, u32[]{:S(2)}) collective-permute-start(bf16[6,64,128]{2,1,0:T(8,128)(2,1)S(1)} %parts.1.p_ref), channel_id=1, source_target_pairs={{0,255},{1,0},{2,1},{3,2},{4,3},{5,4},{6,5},{7,6},{8,7},{9,8},{10,... | collective-permute-start | bytes 294920 | tf_op jit(solution)/shard_map/ppermute | solution.py:39
  61.3 10.3 %collective-permute-start.8 = (bf16[6,64,128]{2,1,0:T(8,128)(2,1)S(1)}, bf16[6,64,128]{2,1,0:T(8,128)(2,1)S(1)}, u32[]{:S(2)}, u32[]{:S(2)}) collective-permute-start(bf16[6,64,128]{2,1,0:T(8,128)(2,1)S(1)} %parts.1.p_ref), channel_id=1, source_target_pairs={{0,1},{1,2},{2,3},{3,4},{4,5},{5,6},{6,7},{7,8},{8,9},{9,10},{10,1... | collective-permute-start | bytes 294920 | tf_op jit(solution)/shard_map/ppermute | solution.py:39
  71.6 11.4 %collective-permute-start.10 = (bf16[6,64,128]{2,1,0:T(8,128)(2,1)S(1)}, bf16[6,64,128]{2,1,0:T(8,128)(2,1)S(1)}, u32[]{:S(2)}, u32[]{:S(2)}) collective-permute-start(bf16[6,64,128]{2,1,0:T(8,128)(2,1)S(1)} %get-tuple-element.51), channel_id=1, source_target_pairs={{0,3},{1,4},{2,5},{3,6},{4,7},{5,8},{6,9},{7,10},{8,11},{9,12},{10... | collective-permute-start | bytes 294920 | tf_op jit(solution)/shard_map/ppermute | solution.py:39
  71.7 11.3 %collective-permute-start.11 = (bf16[6,64,128]{2,1,0:T(8,128)(2,1)S(1)}, bf16[6,64,128]{2,1,0:T(8,128)(2,1)S(1)}, u32[]{:S(2)}, u32[]{:S(2)}) collective-permute-start(bf16[6,64,128]{2,1,0:T(8,128)(2,1)S(1)} %get-tuple-element.52), channel_id=1, source_target_pairs={{0,253},{1,254},{2,255},{3,0},{4,1},{5,2},{6,3},{7,4},{8,5},{9,6},... | collective-permute-start | bytes 294920 | tf_op jit(solution)/shard_map/ppermute | solution.py:39
  103.8 9.1 %collective-permute-start.15 = (bf16[3,64,128]{2,1,0:T(8,128)(2,1)S(1)}, bf16[3,64,128]{2,1,0:T(8,128)(2,1)S(1)}, u32[]{:S(2)}, u32[]{:S(2)}) collective-permute-start(bf16[3,64,128]{2,1,0:T(8,128)(2,1)S(1)} %coarse.1.own_ref), channel_id=1, source_target_pairs={{0,255},{1,0},{2,1},{3,2},{4,3},{5,4},{6,5},{7,6},{8,7},{9,8},{10,... | collective-permute-start | bytes 147464 | tf_op jit(solution)/shard_map/ppermute | solution.py:39
  111.2 8.9 %collective-permute-start.14 = (bf16[3,64,128]{2,1,0:T(8,128)(2,1)S(1)}, bf16[3,64,128]{2,1,0:T(8,128)(2,1)S(1)}, u32[]{:S(2)}, u32[]{:S(2)}) collective-permute-start(bf16[3,64,128]{2,1,0:T(8,128)(2,1)S(1)} %coarse.1.own_ref), channel_id=1, source_target_pairs={{0,1},{1,2},{2,3},{3,4},{4,5},{5,6},{6,7},{7,8},{8,9},{9,10},{10,1... | collective-permute-start | bytes 147464 | tf_op jit(solution)/shard_map/ppermute | solution.py:39
  120.1 5.9 %collective-permute-start.17 = (bf16[3,64,128]{2,1,0:T(8,128)(2,1)S(1)}, bf16[3,64,128]{2,1,0:T(8,128)(2,1)S(1)}, u32[]{:S(2)}, u32[]{:S(2)}) collective-permute-start(bf16[3,64,128]{2,1,0:T(8,128)(2,1)S(1)} %three.1), channel_id=1, source_target_pairs={{0,253},{1,254},{2,255},{3,0},{4,1},{5,2},{6,3},{7,4},{8,5},{9,6},... | collective-permute-start | bytes 147464 | tf_op jit(solution)/shard_map/ppermute | solution.py:39
  120.1 11.0 %collective-permute-start.16 = (bf16[3,64,128]{2,1,0:T(8,128)(2,1)S(1)}, bf16[3,64,128]{2,1,0:T(8,128)(2,1)S(1)}, u32[]{:S(2)}, u32[]{:S(2)}) collective-permute-start(bf16[3,64,128]{2,1,0:T(8,128)(2,1)S(1)} %three.1), channel_id=1, source_target_pairs={{0,3},{1,4},{2,5},{3,6},{4,7},{5,8},{6,9},{7,10},{8,11},{9,12},{10... | collective-permute-start | bytes 147464 | tf_op jit(solution)/shard_map/ppermute | solution.py:39
  132.9 9.2 %collective-permute-start.18 = (bf16[4,64,128]{2,1,0:T(8,128)(2,1)S(1)}, bf16[4,64,128]{2,1,0:T(8,128)(2,1)S(1)}, u32[]{:S(2)}, u32[]{:S(2)}) collective-permute-start(bf16[4,64,128]{2,1,0:T(8,128)(2,1)S(1)} %get-tuple-element.59), channel_id=1, source_target_pairs={{0,1},{1,2},{2,3},{3,4},{4,5},{5,6},{6,7},{7,8},{8,9},{9,10},{10,1... | collective-permute-start | bytes 196616 | tf_op jit(solution)/shard_map/ppermute | solution.py:39
  133.0 9.1 %collective-permute-start.19 = (bf16[4,64,128]{2,1,0:T(8,128)(2,1)S(1)}, bf16[4,64,128]{2,1,0:T(8,128)(2,1)S(1)}, u32[]{:S(2)}, u32[]{:S(2)}) collective-permute-start(bf16[4,64,128]{2,1,0:T(8,128)(2,1)S(1)} %get-tuple-element.60), channel_id=1, source_target_pairs={{0,255},{1,0},{2,1},{3,2},{4,3},{5,4},{6,5},{7,6},{8,7},{9,8},{10,... | collective-permute-start | bytes 196616 | tf_op jit(solution)/shard_map/ppermute | solution.py:39
  144.8 10.5 %collective-permute-start.21 = (bf16[8,64,128]{2,1,0:T(8,128)(2,1)S(1)}, bf16[8,64,128]{2,1,0:T(8,128)(2,1)S(1)}, u32[]{:S(2)}, u32[]{:S(2)}) collective-permute-start(bf16[8,64,128]{2,1,0:T(8,128)(2,1)S(1)} %up8.1.mid_ref), channel_id=1, source_target_pairs={{0,255},{1,0},{2,1},{3,2},{4,3},{5,4},{6,5},{7,6},{8,7},{9,8},{10,... | collective-permute-start | bytes 393224 | tf_op jit(solution)/shard_map/ppermute | solution.py:39
  152.8 10.5 %collective-permute-start.20 = (bf16[8,64,128]{2,1,0:T(8,128)(2,1)S(1)}, bf16[8,64,128]{2,1,0:T(8,128)(2,1)S(1)}, u32[]{:S(2)}, u32[]{:S(2)}) collective-permute-start(bf16[8,64,128]{2,1,0:T(8,128)(2,1)S(1)} %up8.1.mid_ref), channel_id=1, source_target_pairs={{0,1},{1,2},{2,3},{3,4},{4,5},{5,6},{6,7},{7,8},{8,9},{9,10},{10,1... | collective-permute-start | bytes 393224 | tf_op jit(solution)/shard_map/ppermute | solution.py:39
  168.3 9.2 %collective-permute-start.22 = (bf16[4,64,128]{2,1,0:T(8,128)(2,1)S(1)}, bf16[4,64,128]{2,1,0:T(8,128)(2,1)S(1)}, u32[]{:S(2)}, u32[]{:S(2)}) collective-permute-start(bf16[4,64,128]{2,1,0:T(8,128)(2,1)S(1)} %get-tuple-element.63), channel_id=1, source_target_pairs={{0,1},{1,2},{2,3},{3,4},{4,5},{5,6},{6,7},{7,8},{8,9},{9,10},{10,1... | collective-permute-start | bytes 196616 | tf_op jit(solution)/shard_map/ppermute | solution.py:39
  168.4 9.1 %collective-permute-start.23 = (bf16[4,64,128]{2,1,0:T(8,128)(2,1)S(1)}, bf16[4,64,128]{2,1,0:T(8,128)(2,1)S(1)}, u32[]{:S(2)}, u32[]{:S(2)}) collective-permute-start(bf16[4,64,128]{2,1,0:T(8,128)(2,1)S(1)} %get-tuple-element.64), channel_id=1, source_target_pairs={{0,255},{1,0},{2,1},{3,2},{4,3},{5,4},{6,5},{7,6},{8,7},{9,8},{10,... | collective-permute-start | bytes 196616 | tf_op jit(solution)/shard_map/ppermute | solution.py:39
  (15 other events, 224.3 us)

commit v3 on v2

--- a/solution.py
+++ b/solution.py
@@ -243,17 +243,18 @@
     )(w1, w2, w3, deg1, deg2, deg3, col2, col3, own3, slot3)
 
 
-def far_kernel(w3_ref, tail_ref, lo_ref, hi_ref, out_ref):
+def far_kernel(w3_ref, tail_ref, lo_ref, hi_ref, out_ref, copy_ref):
     at = NB2 * ROWS
     out_ref[:at, :] = w3_ref[...]
     out_ref[at : at + TAIL, :] = lo_ref[FIXED - TAIL :, :]
     out_ref[at + TAIL : at + 2 * TAIL, :] = tail_ref[...]
     out_ref[at + 2 * TAIL :, :] = hi_ref[FIXED - TAIL :, :]
+    copy_ref[...] = out_ref[...]
 
 
 def far_data(w3, tail, lo, hi):
     return call(
-        far_kernel, "far", shape((FAR, BS), bf16), [vmem()] * 4, vmem(), flops=2**20, nbytes=2**19
+        far_kernel, "far", (shape((FAR, BS), bf16),) * 2, [vmem()] * 4, (vmem(),) * 2, flops=2**20, nbytes=2**19
     )(w3, tail, lo, hi)
 
 
@@ -469,9 +470,10 @@
 def up_kernel(
     n, base, chunks,
     col_ref, x_ref, xlo_ref, xhi_ref, f_ref, g_ref, flo_ref, fhi_ref, slo_ref, shi_ref, w_hbm,
-    out_ref,
-    w_ref, v0_ref, v1_ref, keep_ref, sem,
+    *outs_and_scratch,
 ):
+    *outs, w_ref, v0_ref, v1_ref, keep_ref, sem = outs_and_scratch
+    out_ref = outs[0]
     copies = weight_copies(w_hbm, w_ref, sem, n, chunks)
     for c in copies:
         c.start()
@@ -515,19 +517,21 @@
 
     def second(b, carry):
         p = product(v1_ref, near(b, 0), weight_of(w_ref, b))
-        out_ref[b] = sweep(b, keep_ref[b], p).astype(out_ref.dtype)
+        x = sweep(b, keep_ref[b], p).astype(out_ref.dtype)
+        for ref in outs:
+            ref[b] = x
         return carry
 
     lax.fori_loop(0, n, second, 0, unroll=4)
 
 
-def go_up(n, base, col, x, x_edges, f, g, f_edges, fixed, weights, dtype, mib):
+def go_up(n, base, col, x, x_edges, f, g, f_edges, fixed, weights, dtype, mib, outs=1):
     chunks = 4
     return call(
         functools.partial(up_kernel, n, base, chunks), f"up{n}",
-        shape((n, R, BS), dtype),
+        (shape((n, R, BS), dtype),) * outs,
         [smem()] + [vmem()] * 9 + [hbm()],
-        vmem(),
+        (vmem(),) * outs,
         [
             pltpu.VMEM((n * ROWS, BS), bf16),
             pltpu.VMEM((n + 2 * EDGE, R, BS), bf16),
@@ -539,15 +543,17 @@
     )(col, x, *x_edges, f, g, *f_edges, *fixed, weights)
 
 
-def parts_kernel(low_ref, mid_ref, high_ref, out_ref):
+def parts_kernel(low_ref, mid_ref, high_ref, out_ref, copy_ref):
     out_ref[:NB2] = low_ref[...]
     out_ref[NB2 : 2 * NB2] = mid_ref[...].astype(bf16)
     out_ref[2 * NB2 :] = high_ref[...]
+    copy_ref[...] = out_ref[...]
 
 
 def parts_of(low, mid, high):
     return call(
-        parts_kernel, "parts", shape((3 * NB2, R, BS), bf16), [vmem()] * 3, vmem(), flops=2**17, nbytes=2**17
+        parts_kernel, "parts", (shape((3 * NB2, R, BS), bf16),) * 2, [vmem()] * 3, (vmem(),) * 2,
+        flops=2**17, nbytes=2**17,
     )(low, mid, high)
 
 
@@ -669,7 +675,7 @@
     )(*args)
 
 
-def coarse_kernel(got_ref, z_ref, s_hbm, out_ref, s_ref, sem):
+def coarse_kernel(got_ref, z_ref, s_hbm, out_ref, copy_ref, s_ref, sem):
     count = got_ref.shape[0]
     chunks = 4
     size = count // chunks
@@ -688,27 +694,30 @@
         )
     out_ref[0] = u.astype(bf16)
     out_ref[1:] = z_ref[...].astype(bf16)
+    copy_ref[...] = out_ref[...]
 
 
 def coarse_solve(got, z, inverse_rows):
     count = got.shape[0]
     return call(
-        coarse_kernel, "coarse", shape((1 + NB2, R, BS), bf16),
-        [vmem(), vmem(), hbm()], vmem(),
+        coarse_kernel, "coarse", (shape((1 + NB2, R, BS), bf16),) * 2,
+        [vmem(), vmem(), hbm()], (vmem(),) * 2,
         [pltpu.VMEM((4, C3, count // 4 * BS), bf16), pltpu.SemaphoreType.DMA((4,))],
         flops=2**26, nbytes=2**21,
     )(got, z, inverse_rows)
 
 
-def three_kernel(lo_ref, own_ref, hi_ref, out_ref):
+def three_kernel(lo_ref, own_ref, hi_ref, out_ref, copy_ref):
     out_ref[0] = lo_ref[0]
     out_ref[1] = own_ref[0]
     out_ref[2] = hi_ref[0]
+    copy_ref[...] = out_ref[...]
 
 
 def three_of(lo, own, hi):
     return call(
-        three_kernel, "three", shape((3, R, BS), bf16), [vmem()] * 3, vmem(), flops=2**15, nbytes=2**16
+        three_kernel, "three", (shape((3, R, BS), bf16),) * 2, [vmem()] * 3, (vmem(),) * 2,
+        flops=2**15, nbytes=2**16,
     )(lo, own, hi)
 
 
@@ -786,8 +795,7 @@
         w1, w2, w3, degree_fine, degree_second, degree_third, columns_second, columns_third, owners_third, slots_third
     )
     fixed = both_ways(up, down)
-    far = far_data(w3, tail, *fixed)
-    far = both_ways(far, far, 2)
+    far = both_ways(*far_data(w3, tail, *fixed), 2)
     third = (w3, tail, *fixed, *far)
 
     x1, low, mid, high = go_down(
@@ -799,23 +807,23 @@
     x2, low, mid, high = go_down(
         NB1, NB2, 0, columns_second, f2, g2, owners_second, slots_second, f_edges, fixed, w2, 12
     )
-    parts = parts_of(low, mid, high)
-    plo, phi = both_ways(parts, parts)
+    parts, copy = parts_of(low, mid, high)
+    plo, phi = both_ways(copy, parts)
     f3, up, down = third_window(mid, parts, plo, phi)
     dlo, dhi = both_ways(up, down, 3)
     c, z = third_down(lax.axis_size("col"), f3, parts, plo, phi, dlo, dhi, *third)
     got = lax.all_to_all(c, "col", 0, 0, tiled=True)
-    own = coarse_solve(got, z, coarse_inverse)
-    lo, hi = both_ways(own, own)
-    near = three_of(lo, own, hi)
-    ulo, uhi = both_ways(near, near, 3)
+    own, copy = coarse_solve(got, z, coarse_inverse)
+    lo, hi = both_ways(copy, own)
+    near, copy = three_of(lo, own, hi)
+    ulo, uhi = both_ways(near, copy, 3)
     x2, first, last = third_up(own, lo, hi, ulo, uhi, z, *third, owners_second, slots_second, x2)
     x_edges = both_ways(last, first)
-    x2 = go_up(NB1, 0, columns_second, x2, x_edges, f2, g2, f_edges, fixed, w2, bf16, 12)
-    lo, hi = both_ways(x2, x2)
+    x2, copy = go_up(NB1, 0, columns_second, x2, x_edges, f2, g2, f_edges, fixed, w2, bf16, 12, 2)
+    lo, hi = both_ways(copy, x2)
     x1, first, last = prolong(NB0, NB1, owners_fine, slots_fine, lo, x2, hi, x1)
     x_edges = both_ways(last, first)
-    return go_up(NB0, F_ROWS, columns_fine, x1, x_edges, f, g1, edges1, edges1, w1, f32, 20)
+    return go_up(NB0, F_ROWS, columns_fine, x1, x_edges, f, g1, edges1, edges1, w1, f32, 20)[0]
 
 
 def solution(mesh):

time: 184 us -> 168 us (0.913)
  waiting for transfers between devices: 45.7 us -> 19.2 us
  starting transfers between devices: 82.5 us -> 93 us
    ppermute x24, waiting for transfers between devices: 45.7 us -> 19.2 us  [passed_along(): lax.ppermute(value, AXES, [(s, (s + steps) % count) for s in range(count)])]
    ppermute x24, starting transfers between devices: 82.5 us -> 93 us  [passed_along(): lax.ppermute(value, AXES, [(s, (s + steps) % count) for s in range(count)])]
  transfers between devices with their start and end apart: 24 -> 24, of which waited for: 12 -> 11; matrix products, arithmetic and copies ran while one was open for 0% -> 0% of each run, Pallas kernels for 8% -> 9%
where the time goes in v3:
time: 168 us; the launch traced here: 167 us
  starting transfers between devices  93 us (55%)
  Pallas kernels  35.6 us (21%)
  waiting for transfers between devices  19.2 us (11%)
  blocking collectives  17.5 us (10%)
    ppermute x24, starting transfers between devices, passed_along(): lax.ppermute(value, AXES, [(s, (s + steps) % count) for s in range(count)])  93 us
    ppermute x24, waiting for transfers between devices, passed_along(): lax.ppermute(value, AXES, [(s, (s + steps) % count) for s in range(count)])  19.2 us
    all_to_all x1, blocking collectives, on_device(): got = lax.all_to_all(c, 'col', 0, 0, tiled=True)  17.5 us
    pallas_call x2, Pallas kernels, go_down(): call(functools.partial(down_kernel, n, nc, base, chunks), f'down{n}', (sh...  11 us
    pallas_call x2, Pallas kernels, go_up(): call(functools.partial(up_kernel, n, base, chunks), f'up{n}', (shape((n,...  8.93 us
    pallas_call x1, Pallas kernels, prolong(): call(functools.partial(prolong_kernel, n, nc), f'prolong{n}', (shape((n,...  5.02 us
    pallas_call x1, Pallas kernels, fixed_data(): call(fixed_kernel, 'fixed', (shape((NB0, BS), f32), shape((NB1, BS), f32)...  3.97 us
  transfers between devices with their start and end apart: 24, of which 11 were waited for; matrix products, arithmetic and copies ran while one was open for 0% of the time, Pallas kernels for 9%

profile of v3, /device:TPU:0, one launch (start us, length us, event | category | flops | bytes accessed | tf_op | source)
XLA Modules:
  0.0 167.4 jit_solution(2992800681343297402)
XLA Ops:
  3.7 8.1 %collective-permute-start.1 = (bf16[1040,128]{1,0:T(8,128)(2,1)S(1)}, bf16[1040,128]{1,0:T(8,128)(2,1)S(1)}, u32[]{:S(2)}, u32[]{:S(2)}) collective-permute-start(bf16[1040,128]{1,0:T(8,128)(2,1)S(1)} %get-tuple-element.47), channel_id=1, source_target_pairs={{0,255},{1,0},{2,1},{3,2},{4,3},{5,4},{6,5},{7,6},{8,7},{9,8},{10,... | collective-permute-start | bytes 798728 | tf_op jit(solution)/shard_map/ppermute | solution.py:39
  12.0 4.0 %fixed.1 = (f32[32,128]{1,0:T(8,128)S(1)}, f32[8,128]{1,0:T(8,128)S(1)}, f32[2,128]{1,0:T(2,128)}, bf16[1568,128]{1,0:T(8,128)(2,1)S(1)}, bf16[1568,128]{1,0:T(8...) custom-call(bf16[12288,128]{1,0:T(8,128)(2,1)} %bitcast.16, bf16[3072,128]{1,0:T(8,128)(2,1)} %bitcast.19, ...), custom_call_target="tpu_custom_call" | custom-call | flops 1073741824 | bytes 4194304 | tf_op jit(solution)/shard_map/fixed/pallas_call | solution.py:228
  16.1 7.2 %collective-permute-start.7 = (bf16[1568,128]{1,0:T(8,128)(2,1)S(1)}, bf16[1568,128]{1,0:T(8,128)(2,1)S(1)}, u32[]{:S(2)}, u32[]{:S(2)}) collective-permute-start(bf16[1568,128]{1,0:T(8,128)(2,1)S(1)} %get-tuple-element.56), channel_id=1, source_target_pairs={{0,255},{1,0},{2,1},{3,2},{4,3},{5,4},{6,5},{7,6},{8,7},{9,8},{10,... | collective-permute-start | bytes 1204232 | tf_op jit(solution)/shard_map/ppermute | solution.py:39
  23.3 7.9 %down32.1 = (f32[32,64,128]{2,1,0:T(8,128)S(1)}, bf16[8,64,128]{2,1,0:T(8,128)(2,1)S(1)}, f32[8,64,128]{2,1,0:T(8,128)S(1)}, bf16[8,64,128]{2,1,0:T(8,128)(2,1)S(1)}) custom-call(s32[3,32]{1,0:T(4,128)S(1)} %bitcast.9, bf16[32,64,128]{2,1,0:T(8,128)(2,1)S(1)} %copy-done, f32[32,128]{1,0:T(8,128)S(1)} %get-tuple-element.45.g_ref, s32[32,128]{1,0:T(8,128)S(1)} %copy-done.6, ...), custom_call_target="tpu_custom_call" | custom-call | flops 402653184 | bytes 3145728 | tf_op jit(solution)/shard_map/down32/pallas_call | solution.py:385
  31.3 7.2 %collective-permute-start.3 = (bf16[8,64,128]{2,1,0:T(8,128)(2,1)S(1)}, bf16[8,64,128]{2,1,0:T(8,128)(2,1)S(1)}, u32[]{:S(2)}, u32[]{:S(2)}) collective-permute-start(bf16[8,64,128]{2,1,0:T(8,128)(2,1)S(1)} %get-tuple-element.50), channel_id=1, source_target_pairs={{0,255},{1,0},{2,1},{3,2},{4,3},{5,4},{6,5},{7,6},{8,7},{9,8},{10,... | collective-permute-start | bytes 393224 | tf_op jit(solution)/shard_map/ppermute | solution.py:39
  38.5 2.6 %collective-permute-done.2.lo_ref = bf16[8,64,128]{2,1,0:T(8,128)(2,1)S(1)} collective-permute-done((bf16[8,64,128]{2,1,0:T(8,128)(2,1)S(1)}, bf16[8,64,128]{2,1,0:T(8,128)(2,1)S(1)}, u32[]{:S(2)}, u32[]{:S(2)}) %collective-permute-start.2) | collective-permute-done | bytes 131104 | tf_op jit(solution)/shard_map/ppermute | solution.py:39
  41.3 7.2 %collective-permute-start.5 = (bf16[4,64,128]{2,1,0:T(8,128)(2,1)S(1)}, bf16[4,64,128]{2,1,0:T(8,128)(2,1)S(1)}, u32[]{:S(2)}, u32[]{:S(2)}) collective-permute-start(bf16[4,64,128]{2,1,0:T(8,128)(2,1)S(1)} %get-tuple-element.54), channel_id=1, source_target_pairs={{0,255},{1,0},{2,1},{3,2},{4,3},{5,4},{6,5},{7,6},{8,7},{9,8},{10,... | collective-permute-start | bytes 196616 | tf_op jit(solution)/shard_map/ppermute | solution.py:39
  48.7 8.1 %collective-permute-start.13 = (bf16[816,128]{1,0:T(8,128)(2,1)S(1)}, bf16[816,128]{1,0:T(8,128)(2,1)S(1)}, u32[]{:S(2)}, u32[]{:S(2)}) collective-permute-start(bf16[816,128]{1,0:T(8,128)(2,1)S(1)} %get-tuple-element.68), channel_id=1, source_target_pairs={{0,254},{1,255},{2,0},{3,1},{4,2},{5,3},{6,4},{7,5},{8,6},{9,7},{1... | collective-permute-start | bytes 626696 | tf_op jit(solution)/shard_map/ppermute | solution.py:39
  56.7 3.1 %down8.1 = (f32[8,64,128]{2,1,0:T(8,128)S(1)}, bf16[2,64,128]{2,1,0:T(8,128)(2,1)S(1)}, f32[2,64,128]{2,1,0:T(8,128)S(1)}, bf16[2,64,128]{2,1,0:T(8,128)(2,1)S(1)}) custom-call(s32[3,8]{1,0:T(4,128)S(1)} %bitcast.12, f32[8,64,128]{2,1,0:T(8,128)S(1)} %get-tuple-element.51.f_ref, f32[8,128]{1,0:T(8,128)S(1)} %get-tuple-element.52.g_ref, ...), custom_call_target="tpu_custom_call" | custom-call | flops 100663296 | bytes 786432 | tf_op jit(solution)/shard_map/down8/pallas_call | solution.py:385
  59.9 7.2 %collective-permute-start.9 = (bf16[6,64,128]{2,1,0:T(8,128)(2,1)S(1)}, bf16[6,64,128]{2,1,0:T(8,128)(2,1)S(1)}, u32[]{:S(2)}, u32[]{:S(2)}) collective-permute-start(bf16[6,64,128]{2,1,0:T(8,128)(2,1)S(1)} %get-tuple-element.60.p_ref), channel_id=1, source_target_pairs={{0,255},{1,0},{2,1},{3,2},{4,3},{5,4},{6,5},{7,6},{8,7},{9,8},{10,... | collective-permute-start | bytes 294920 | tf_op jit(solution)/shard_map/ppermute | solution.py:39
  67.1 2.3 %collective-permute-done.8.lo_ref = bf16[6,64,128]{2,1,0:T(8,128)(2,1)S(1)} collective-permute-done((bf16[6,64,128]{2,1,0:T(8,128)(2,1)S(1)}, bf16[6,64,128]{2,1,0:T(8,128)(2,1)S(1)}, u32[]{:S(2)}, u32[]{:S(2)}) %collective-permute-start.8) | collective-permute-done | bytes 98336 | tf_op jit(solution)/shard_map/ppermute | solution.py:39
  69.6 9.0 %collective-permute-start.11 = (bf16[6,64,128]{2,1,0:T(8,128)(2,1)S(1)}, bf16[6,64,128]{2,1,0:T(8,128)(2,1)S(1)}, u32[]{:S(2)}, u32[]{:S(2)}) collective-permute-start(bf16[6,64,128]{2,1,0:T(8,128)(2,1)S(1)} %get-tuple-element.64), channel_id=1, source_target_pairs={{0,253},{1,254},{2,255},{3,0},{4,1},{5,2},{6,3},{7,4},{8,5},{9,6},... | collective-permute-start | bytes 294920 | tf_op jit(solution)/shard_map/ppermute | solution.py:39
  82.7 17.5 %all_to_all.5.got_ref = bf16[32,64,128]{2,1,0:T(8,128)(2,1)S(1)} all-to-all(bf16[32,64,128]{2,1,0:T(8,128)(2,1)S(1)} %get-tuple-element.69), channel_id=1, replica_groups=mesh['row'=8,'col'=32] {'col'}, dimensions={0} | all-to-all | bytes 1048576 | tf_op jit(solution)/shard_map/all_to_all | solution.py:815
  102.1 2.8 %collective-permute-start.14 = (bf16[3,64,128]{2,1,0:T(8,128)(2,1)S(1)}, bf16[3,64,128]{2,1,0:T(8,128)(2,1)S(1)}, u32[]{:S(2)}, u32[]{:S(2)}) collective-permute-start(bf16[3,64,128]{2,1,0:T(8,128)(2,1)S(1)} %get-tuple-element.72), channel_id=1, source_target_pairs={{0,1},{1,2},{2,3},{3,4},{4,5},{5,6},{6,7},{7,8},{8,9},{9,10},{10,1... | collective-permute-start | bytes 147464 | tf_op jit(solution)/shard_map/ppermute | solution.py:39
  104.9 4.6 %collective-permute-start.15 = (bf16[3,64,128]{2,1,0:T(8,128)(2,1)S(1)}, bf16[3,64,128]{2,1,0:T(8,128)(2,1)S(1)}, u32[]{:S(2)}, u32[]{:S(2)}) collective-permute-start(bf16[3,64,128]{2,1,0:T(8,128)(2,1)S(1)} %get-tuple-element.71.own_ref), channel_id=1, source_target_pairs={{0,255},{1,0},{2,1},{3,2},{4,3},{5,4},{6,5},{7,6},{8,7},{9,8},{10,... | collective-permute-start | bytes 147464 | tf_op jit(solution)/shard_map/ppermute | solution.py:39
  111.4 9.0 %collective-permute-start.17 = (bf16[3,64,128]{2,1,0:T(8,128)(2,1)S(1)}, bf16[3,64,128]{2,1,0:T(8,128)(2,1)S(1)}, u32[]{:S(2)}, u32[]{:S(2)}) collective-permute-start(bf16[3,64,128]{2,1,0:T(8,128)(2,1)S(1)} %get-tuple-element.74), channel_id=1, source_target_pairs={{0,253},{1,254},{2,255},{3,0},{4,1},{5,2},{6,3},{7,4},{8,5},{9,6},... | collective-permute-start | bytes 147464 | tf_op jit(solution)/shard_map/ppermute | solution.py:39
  124.4 7.2 %collective-permute-start.19 = (bf16[4,64,128]{2,1,0:T(8,128)(2,1)S(1)}, bf16[4,64,128]{2,1,0:T(8,128)(2,1)S(1)}, u32[]{:S(2)}, u32[]{:S(2)}) collective-permute-start(bf16[4,64,128]{2,1,0:T(8,128)(2,1)S(1)} %get-tuple-element.78), channel_id=1, source_target_pairs={{0,255},{1,0},{2,1},{3,2},{4,3},{5,4},{6,5},{7,6},{8,7},{9,8},{10,... | collective-permute-start | bytes 196616 | tf_op jit(solution)/shard_map/ppermute | solution.py:39
  131.6 2.5 %collective-permute-done.18.xlo_ref = bf16[4,64,128]{2,1,0:T(8,128)(2,1)S(1)} collective-permute-done((bf16[4,64,128]{2,1,0:T(8,128)(2,1)S(1)}, bf16[4,64,128]{2,1,0:T(8,128)(2,1)S(1)}, u32[]{:S(2)}, u32[]{:S(2)}) %collective-permute-start.18) | collective-permute-done | bytes 65568 | tf_op jit(solution)/shard_map/ppermute | solution.py:39
  134.1 2.7 %up8.1 = (bf16[8,64,128]{2,1,0:T(8,128)(2,1)S(1)}, bf16[8,64,128]{2,1,0:T(8,128)(2,1)S(1)}) custom-call(s32[3,8]{1,0:T(4,128)S(1)} %bitcast.13, f32[8,64,128]{2,1,0:T(8,128)S(1)} %get-tuple-element.76.x_ref, bf16[4,64,128]{2,1,0:T(8,128)(2,1)S(1)} %collective-permute-done.18.xlo_ref, bf16[4,64,128]{2,1,0:T(8,128)(2,1)S(1)} %collective-permute-done.19.xhi_ref, ...), custom_call_target="tpu_custom_call" | custom-call | flops 100663296 | bytes 786432 | tf_op jit(solution)/shard_map/up8/pallas_call | solution.py:530
  136.9 7.2 %collective-permute-start.21 = (bf16[8,64,128]{2,1,0:T(8,128)(2,1)S(1)}, bf16[8,64,128]{2,1,0:T(8,128)(2,1)S(1)}, u32[]{:S(2)}, u32[]{:S(2)}) collective-permute-start(bf16[8,64,128]{2,1,0:T(8,128)(2,1)S(1)} %get-tuple-element.80.mid_ref), channel_id=1, source_target_pairs={{0,255},{1,0},{2,1},{3,2},{4,3},{5,4},{6,5},{7,6},{8,7},{9,8},{10,... | collective-permute-start | bytes 393224 | tf_op jit(solution)/shard_map/ppermute | solution.py:39
  144.1 2.6 %collective-permute-done.20.lo_ref = bf16[8,64,128]{2,1,0:T(8,128)(2,1)S(1)} collective-permute-done((bf16[8,64,128]{2,1,0:T(8,128)(2,1)S(1)}, bf16[8,64,128]{2,1,0:T(8,128)(2,1)S(1)}, u32[]{:S(2)}, u32[]{:S(2)}) %collective-permute-start.20) | collective-permute-done | bytes 131104 | tf_op jit(solution)/shard_map/ppermute | solution.py:39
  146.7 5.0 %prolong32.1 = (f32[32,64,128]{2,1,0:T(8,128)S(1)}, bf16[4,64,128]{2,1,0:T(8,128)(2,1)S(1)}, bf16[4,64,128]{2,1,0:T(8,128)(2,1)S(1)}) custom-call(s32[32,128]{1,0:T(8,128)S(1)} %copy-done.6, s32[32,128]{1,0:T(8,128)S(1)} %copy-done.7, bf16[8,64,128]{2,1,0:T(8,128)(2,1)S(1)} %collective-permute-done.20.lo_ref, ...), custom_call_target="tpu_custom_call" | custom-call | flops 1610612736 | bytes 2097152 | tf_op jit(solution)/shard_map/prolong32/pallas_call | solution.py:456
  151.9 7.2 %collective-permute-start.23 = (bf16[4,64,128]{2,1,0:T(8,128)(2,1)S(1)}, bf16[4,64,128]{2,1,0:T(8,128)(2,1)S(1)}, u32[]{:S(2)}, u32[]{:S(2)}) collective-permute-start(bf16[4,64,128]{2,1,0:T(8,128)(2,1)S(1)} %get-tuple-element.84), channel_id=1, source_target_pairs={{0,255},{1,0},{2,1},{3,2},{4,3},{5,4},{6,5},{7,6},{8,7},{9,8},{10,... | collective-permute-start | bytes 196616 | tf_op jit(solution)/shard_map/ppermute | solution.py:39
  161.0 6.2 %up32.1 = f32[32,64,128]{2,1,0:T(8,128)} custom-call(s32[3,32]{1,0:T(4,128)S(1)} %bitcast.10, f32[32,64,128]{2,1,0:T(8,128)S(1)} %get-tuple-element.82.x_ref, bf16[4,64,128]{2,1,0:T(8,128)(2,1)S(1)} %collective-permute-done.22.xlo_ref, bf16[4,64,128]{2,1,0:T(8,128)(2,1)S(1)} %collective-permute-done.23.xhi_ref, bf16[32,64,128]{2,1,0:T(8,128)(2,1)S(1)} %copy-done, ...), custom_call_target="tpu_custom_call" | custom-call | flops 402653184 | bytes 3145728 | tf_op jit(solution)/shard_map/up32/pallas_call | solution.py:530
  (71 shorter events, 18.5 us)
Async XLA Ops:
  3.4 19.8 %collective-permute-start = (bf16[1040,128]{1,0:T(8,128)(2,1)S(1)}, bf16[1040,128]{1,0:T(8,128)(2,1)S(1)}, u32[]{:S(2)}, u32[]{:S(2)}) collective-permute-start(bf16[1040,128]{1,0:T(8,128)(2,1)S(1)} %get-tuple-element.46), channel_id=1, source_target_pairs={{0,1},{1,2},{2,3},{3,4},{4,5},{5,6},{6,7},{7,8},{8,9},{9,10},{10,1... | collective-permute-start | bytes 798728 | tf_op jit(solution)/shard_map/ppermute | solution.py:39
  3.7 19.5 %collective-permute-start.1 = (bf16[1040,128]{1,0:T(8,128)(2,1)S(1)}, bf16[1040,128]{1,0:T(8,128)(2,1)S(1)}, u32[]{:S(2)}, u32[]{:S(2)}) collective-permute-start(bf16[1040,128]{1,0:T(8,128)(2,1)S(1)} %get-tuple-element.47), channel_id=1, source_target_pairs={{0,255},{1,0},{2,1},{3,2},{4,3},{5,4},{6,5},{7,6},{8,7},{9,8},{10,... | collective-permute-start | bytes 798728 | tf_op jit(solution)/shard_map/ppermute | solution.py:39
  16.0 32.6 %collective-permute-start.6 = (bf16[1568,128]{1,0:T(8,128)(2,1)S(1)}, bf16[1568,128]{1,0:T(8,128)(2,1)S(1)}, u32[]{:S(2)}, u32[]{:S(2)}) collective-permute-start(bf16[1568,128]{1,0:T(8,128)(2,1)S(1)} %get-tuple-element.55), channel_id=1, source_target_pairs={{0,1},{1,2},{2,3},{3,4},{4,5},{5,6},{6,7},{7,8},{8,9},{9,10},{10,1... | collective-permute-start | bytes 1204232 | tf_op jit(solution)/shard_map/ppermute | solution.py:39
  16.1 32.5 %collective-permute-start.7 = (bf16[1568,128]{1,0:T(8,128)(2,1)S(1)}, bf16[1568,128]{1,0:T(8,128)(2,1)S(1)}, u32[]{:S(2)}, u32[]{:S(2)}) collective-permute-start(bf16[1568,128]{1,0:T(8,128)(2,1)S(1)} %get-tuple-element.56), channel_id=1, source_target_pairs={{0,255},{1,0},{2,1},{3,2},{4,3},{5,4},{6,5},{7,6},{8,7},{9,8},{10,... | collective-permute-start | bytes 1204232 | tf_op jit(solution)/shard_map/ppermute | solution.py:39
  31.2 9.9 %collective-permute-start.2 = (bf16[8,64,128]{2,1,0:T(8,128)(2,1)S(1)}, bf16[8,64,128]{2,1,0:T(8,128)(2,1)S(1)}, u32[]{:S(2)}, u32[]{:S(2)}) collective-permute-start(bf16[8,64,128]{2,1,0:T(8,128)(2,1)S(1)} %get-tuple-element.49), channel_id=1, source_target_pairs={{0,1},{1,2},{2,3},{3,4},{4,5},{5,6},{6,7},{7,8},{8,9},{9,10},{10,1... | collective-permute-start | bytes 393224 | tf_op jit(solution)/shard_map/ppermute | solution.py:39
  31.3 9.8 %collective-permute-start.3 = (bf16[8,64,128]{2,1,0:T(8,128)(2,1)S(1)}, bf16[8,64,128]{2,1,0:T(8,128)(2,1)S(1)}, u32[]{:S(2)}, u32[]{:S(2)}) collective-permute-start(bf16[8,64,128]{2,1,0:T(8,128)(2,1)S(1)} %get-tuple-element.50), channel_id=1, source_target_pairs={{0,255},{1,0},{2,1},{3,2},{4,3},{5,4},{6,5},{7,6},{8,7},{9,8},{10,... | collective-permute-start | bytes 393224 | tf_op jit(solution)/shard_map/ppermute | solution.py:39
  41.2 15.5 %collective-permute-start.4 = (bf16[4,64,128]{2,1,0:T(8,128)(2,1)S(1)}, bf16[4,64,128]{2,1,0:T(8,128)(2,1)S(1)}, u32[]{:S(2)}, u32[]{:S(2)}) collective-permute-start(bf16[4,64,128]{2,1,0:T(8,128)(2,1)S(1)} %get-tuple-element.53), channel_id=1, source_target_pairs={{0,1},{1,2},{2,3},{3,4},{4,5},{5,6},{6,7},{7,8},{8,9},{9,10},{10,1... | collective-permute-start | bytes 196616 | tf_op jit(solution)/shard_map/ppermute | solution.py:39
  41.3 15.5 %collective-permute-start.5 = (bf16[4,64,128]{2,1,0:T(8,128)(2,1)S(1)}, bf16[4,64,128]{2,1,0:T(8,128)(2,1)S(1)}, u32[]{:S(2)}, u32[]{:S(2)}) collective-permute-start(bf16[4,64,128]{2,1,0:T(8,128)(2,1)S(1)} %get-tuple-element.54), channel_id=1, source_target_pairs={{0,255},{1,0},{2,1},{3,2},{4,3},{5,4},{6,5},{7,6},{8,7},{9,8},{10,... | collective-permute-start | bytes 196616 | tf_op jit(solution)/shard_map/ppermute | solution.py:39
  48.6 30.0 %collective-permute-start.12 = (bf16[816,128]{1,0:T(8,128)(2,1)S(1)}, bf16[816,128]{1,0:T(8,128)(2,1)S(1)}, u32[]{:S(2)}, u32[]{:S(2)}) collective-permute-start(bf16[816,128]{1,0:T(8,128)(2,1)S(1)} %get-tuple-element.67), channel_id=1, source_target_pairs={{0,2},{1,3},{2,4},{3,5},{4,6},{5,7},{6,8},{7,9},{8,10},{9,11},{10,... | collective-permute-start | bytes 626696 | tf_op jit(solution)/shard_map/ppermute | solution.py:39
  48.7 29.9 %collective-permute-start.13 = (bf16[816,128]{1,0:T(8,128)(2,1)S(1)}, bf16[816,128]{1,0:T(8,128)(2,1)S(1)}, u32[]{:S(2)}, u32[]{:S(2)}) collective-permute-start(bf16[816,128]{1,0:T(8,128)(2,1)S(1)} %get-tuple-element.68), channel_id=1, source_target_pairs={{0,254},{1,255},{2,0},{3,1},{4,2},{5,3},{6,4},{7,5},{8,6},{9,7},{1... | collective-permute-start | bytes 626696 | tf_op jit(solution)/shard_map/ppermute | solution.py:39
  59.8 9.6 %collective-permute-start.8 = (bf16[6,64,128]{2,1,0:T(8,128)(2,1)S(1)}, bf16[6,64,128]{2,1,0:T(8,128)(2,1)S(1)}, u32[]{:S(2)}, u32[]{:S(2)}) collective-permute-start(bf16[6,64,128]{2,1,0:T(8,128)(2,1)S(1)} %get-tuple-element.61), channel_id=1, source_target_pairs={{0,1},{1,2},{2,3},{3,4},{4,5},{5,6},{6,7},{7,8},{8,9},{9,10},{10,1... | collective-permute-start | bytes 294920 | tf_op jit(solution)/shard_map/ppermute | solution.py:39
  59.9 9.5 %collective-permute-start.9 = (bf16[6,64,128]{2,1,0:T(8,128)(2,1)S(1)}, bf16[6,64,128]{2,1,0:T(8,128)(2,1)S(1)}, u32[]{:S(2)}, u32[]{:S(2)}) collective-permute-start(bf16[6,64,128]{2,1,0:T(8,128)(2,1)S(1)} %get-tuple-element.60.p_ref), channel_id=1, source_target_pairs={{0,255},{1,0},{2,1},{3,2},{4,3},{5,4},{6,5},{7,6},{8,7},{9,8},{10,... | collective-permute-start | bytes 294920 | tf_op jit(solution)/shard_map/ppermute | solution.py:39
  69.5 11.4 %collective-permute-start.10 = (bf16[6,64,128]{2,1,0:T(8,128)(2,1)S(1)}, bf16[6,64,128]{2,1,0:T(8,128)(2,1)S(1)}, u32[]{:S(2)}, u32[]{:S(2)}) collective-permute-start(bf16[6,64,128]{2,1,0:T(8,128)(2,1)S(1)} %get-tuple-element.63), channel_id=1, source_target_pairs={{0,3},{1,4},{2,5},{3,6},{4,7},{5,8},{6,9},{7,10},{8,11},{9,12},{10... | collective-permute-start | bytes 294920 | tf_op jit(solution)/shard_map/ppermute | solution.py:39
  69.6 12.2 %collective-permute-start.11 = (bf16[6,64,128]{2,1,0:T(8,128)(2,1)S(1)}, bf16[6,64,128]{2,1,0:T(8,128)(2,1)S(1)}, u32[]{:S(2)}, u32[]{:S(2)}) collective-permute-start(bf16[6,64,128]{2,1,0:T(8,128)(2,1)S(1)} %get-tuple-element.64), channel_id=1, source_target_pairs={{0,253},{1,254},{2,255},{3,0},{4,1},{5,2},{6,3},{7,4},{8,5},{9,6},... | collective-permute-start | bytes 294920 | tf_op jit(solution)/shard_map/ppermute | solution.py:39
  102.1 9.1 %collective-permute-start.14 = (bf16[3,64,128]{2,1,0:T(8,128)(2,1)S(1)}, bf16[3,64,128]{2,1,0:T(8,128)(2,1)S(1)}, u32[]{:S(2)}, u32[]{:S(2)}) collective-permute-start(bf16[3,64,128]{2,1,0:T(8,128)(2,1)S(1)} %get-tuple-element.72), channel_id=1, source_target_pairs={{0,1},{1,2},{2,3},{3,4},{4,5},{5,6},{6,7},{7,8},{8,9},{9,10},{10,1... | collective-permute-start | bytes 147464 | tf_op jit(solution)/shard_map/ppermute | solution.py:39
  104.9 6.4 %collective-permute-start.15 = (bf16[3,64,128]{2,1,0:T(8,128)(2,1)S(1)}, bf16[3,64,128]{2,1,0:T(8,128)(2,1)S(1)}, u32[]{:S(2)}, u32[]{:S(2)}) collective-permute-start(bf16[3,64,128]{2,1,0:T(8,128)(2,1)S(1)} %get-tuple-element.71.own_ref), channel_id=1, source_target_pairs={{0,255},{1,0},{2,1},{3,2},{4,3},{5,4},{6,5},{7,6},{8,7},{9,8},{10,... | collective-permute-start | bytes 147464 | tf_op jit(solution)/shard_map/ppermute | solution.py:39
  111.3 10.8 %collective-permute-start.16 = (bf16[3,64,128]{2,1,0:T(8,128)(2,1)S(1)}, bf16[3,64,128]{2,1,0:T(8,128)(2,1)S(1)}, u32[]{:S(2)}, u32[]{:S(2)}) collective-permute-start(bf16[3,64,128]{2,1,0:T(8,128)(2,1)S(1)} %get-tuple-element.73), channel_id=1, source_target_pairs={{0,3},{1,4},{2,5},{3,6},{4,7},{5,8},{6,9},{7,10},{8,11},{9,12},{10... | collective-permute-start | bytes 147464 | tf_op jit(solution)/shard_map/ppermute | solution.py:39
  111.4 11.1 %collective-permute-start.17 = (bf16[3,64,128]{2,1,0:T(8,128)(2,1)S(1)}, bf16[3,64,128]{2,1,0:T(8,128)(2,1)S(1)}, u32[]{:S(2)}, u32[]{:S(2)}) collective-permute-start(bf16[3,64,128]{2,1,0:T(8,128)(2,1)S(1)} %get-tuple-element.74), channel_id=1, source_target_pairs={{0,253},{1,254},{2,255},{3,0},{4,1},{5,2},{6,3},{7,4},{8,5},{9,6},... | collective-permute-start | bytes 147464 | tf_op jit(solution)/shard_map/ppermute | solution.py:39
  124.3 9.8 %collective-permute-start.18 = (bf16[4,64,128]{2,1,0:T(8,128)(2,1)S(1)}, bf16[4,64,128]{2,1,0:T(8,128)(2,1)S(1)}, u32[]{:S(2)}, u32[]{:S(2)}) collective-permute-start(bf16[4,64,128]{2,1,0:T(8,128)(2,1)S(1)} %get-tuple-element.77), channel_id=1, source_target_pairs={{0,1},{1,2},{2,3},{3,4},{4,5},{5,6},{6,7},{7,8},{8,9},{9,10},{10,1... | collective-permute-start | bytes 196616 | tf_op jit(solution)/shard_map/ppermute | solution.py:39
  124.4 9.7 %collective-permute-start.19 = (bf16[4,64,128]{2,1,0:T(8,128)(2,1)S(1)}, bf16[4,64,128]{2,1,0:T(8,128)(2,1)S(1)}, u32[]{:S(2)}, u32[]{:S(2)}) collective-permute-start(bf16[4,64,128]{2,1,0:T(8,128)(2,1)S(1)} %get-tuple-element.78), channel_id=1, source_target_pairs={{0,255},{1,0},{2,1},{3,2},{4,3},{5,4},{6,5},{7,6},{8,7},{9,8},{10,... | collective-permute-start | bytes 196616 | tf_op jit(solution)/shard_map/ppermute | solution.py:39
  136.8 9.9 %collective-permute-start.20 = (bf16[8,64,128]{2,1,0:T(8,128)(2,1)S(1)}, bf16[8,64,128]{2,1,0:T(8,128)(2,1)S(1)}, u32[]{:S(2)}, u32[]{:S(2)}) collective-permute-start(bf16[8,64,128]{2,1,0:T(8,128)(2,1)S(1)} %get-tuple-element.79), channel_id=1, source_target_pairs={{0,1},{1,2},{2,3},{3,4},{4,5},{5,6},{6,7},{7,8},{8,9},{9,10},{10,1... | collective-permute-start | bytes 393224 | tf_op jit(solution)/shard_map/ppermute | solution.py:39
  136.9 9.8 %collective-permute-start.21 = (bf16[8,64,128]{2,1,0:T(8,128)(2,1)S(1)}, bf16[8,64,128]{2,1,0:T(8,128)(2,1)S(1)}, u32[]{:S(2)}, u32[]{:S(2)}) collective-permute-start(bf16[8,64,128]{2,1,0:T(8,128)(2,1)S(1)} %get-tuple-element.80.mid_ref), channel_id=1, source_target_pairs={{0,255},{1,0},{2,1},{3,2},{4,3},{5,4},{6,5},{7,6},{8,7},{9,8},{10,... | collective-permute-start | bytes 393224 | tf_op jit(solution)/shard_map/ppermute | solution.py:39
  151.8 9.2 %collective-permute-start.22 = (bf16[4,64,128]{2,1,0:T(8,128)(2,1)S(1)}, bf16[4,64,128]{2,1,0:T(8,128)(2,1)S(1)}, u32[]{:S(2)}, u32[]{:S(2)}) collective-permute-start(bf16[4,64,128]{2,1,0:T(8,128)(2,1)S(1)} %get-tuple-element.83), channel_id=1, source_target_pairs={{0,1},{1,2},{2,3},{3,4},{4,5},{5,6},{6,7},{7,8},{8,9},{9,10},{10,1... | collective-permute-start | bytes 196616 | tf_op jit(solution)/shard_map/ppermute | solution.py:39
  151.9 9.2 %collective-permute-start.23 = (bf16[4,64,128]{2,1,0:T(8,128)(2,1)S(1)}, bf16[4,64,128]{2,1,0:T(8,128)(2,1)S(1)}, u32[]{:S(2)}, u32[]{:S(2)}) collective-permute-start(bf16[4,64,128]{2,1,0:T(8,128)(2,1)S(1)} %get-tuple-element.84), channel_id=1, source_target_pairs={{0,255},{1,0},{2,1},{3,2},{4,3},{5,4},{6,5},{7,6},{8,7},{9,8},{10,... | collective-permute-start | bytes 196616 | tf_op jit(solution)/shard_map/ppermute | solution.py:39
  (15 other events, 234.6 us)

commit v4 on v3

--- a/solution.py
+++ b/solution.py
@@ -126,8 +126,12 @@
     return jnp.concatenate(rows, axis=0).astype(bf16)
 
 
-def edge_kernel(f_hbm, w_hbm, deg_ref, col_ref, up_ref, down_ref, w_ref, sem):
+def edge_kernel(f_hbm, w_hbm, deg_hbm, col_hbm, up_ref, down_ref, w_ref, deg_ref, col_ref, sem):
     n = NB0
+    small = [
+        pltpu.make_async_copy(deg_hbm, deg_ref, sem.at[6]),
+        pltpu.make_async_copy(col_hbm, col_ref, sem.at[7]),
+    ]
     first = device_index() * n
     copies = [
         pltpu.make_async_copy(w_hbm.at[pl.ds((n - EDGE) * ROWS, EDGE * ROWS)], w_ref.at[1], sem.at[0]),
@@ -139,8 +143,10 @@
         ),
         pltpu.make_async_copy(w_hbm.at[pl.ds(0, W_ROWS)], down_ref.at[pl.ds(F_ROWS, W_ROWS)], sem.at[5]),
     ]
-    for c in copies:
+    for c in small + copies:
         c.start()
+    for c in small:
+        c.wait()
     for side, ref, start, near_start in ((1, up_ref, n - EDGE, n - HB), (0, down_ref, 0, 0)):
         copies[1 - side].wait()
         gs = [
@@ -157,9 +163,14 @@
     return call(
         edge_kernel, "edges",
         (shape((EDGE1, BS), bf16),) * 2,
-        [hbm(), hbm(), vmem(), smem()],
+        [hbm()] * 4,
         (vmem(),) * 2,
-        [pltpu.VMEM((2, EDGE * ROWS, BS), bf16), pltpu.SemaphoreType.DMA((6,))],
+        [
+            pltpu.VMEM((2, EDGE * ROWS, BS), bf16),
+            pltpu.VMEM((NB0, BS), f32),
+            pltpu.SMEM((K, NB0), i32),
+            pltpu.SemaphoreType.DMA((8,)),
+        ],
         flops=2**20, nbytes=2**21,
     )(f, w, deg, col)
 
@@ -230,12 +241,11 @@
         (
             shape((NB0, BS), f32), shape((NB1, BS), f32), shape((NB2, BS), f32),
             shape((FIXED, BS), bf16), shape((FIXED, BS), bf16),
-            shape((NB2 * ROWS, BS), bf16), shape((TAIL, BS), bf16),
+            shape((NB2 * ROWS, BS), bf16), shape((TAIL, BS), bf16), shape((NB0 * ROWS, BS), bf16),
         ),
         [hbm()] * 3 + [vmem()] * 3 + [smem()] * 2 + [vmem()] * 2,
-        (vmem(),) * 7,
+        (vmem(),) * 8,
         [
-            pltpu.VMEM((NB0 * ROWS, BS), bf16),
             pltpu.VMEM((NB1 * ROWS, BS), bf16),
             pltpu.SemaphoreType.DMA((10,)),
         ],
@@ -281,14 +291,17 @@
 
 def down_kernel(
     n, nc, base, chunks,
-    col_ref, f_ref, g_ref, own_ref, slot_ref, flo_ref, fhi_ref, slo_ref, shi_ref, w_hbm,
-    x_out, down_ref, mid_ref, up_ref,
-    w_ref, v0_ref, v1_ref, x_ref, r_ref, acc_ref, sem,
+    col_ref, f_ref, g_ref, own_ref, slot_ref, flo_ref, fhi_ref, slo_ref, shi_ref, *rest,
 ):
-    copies = weight_copies(w_hbm, w_ref, sem, n, chunks)
-    for c in copies:
-        c.start()
-    size = n // chunks
+    inner_ref = None
+    if chunks:
+        w_hbm, x_ref, down_ref, mid_ref, up_ref, v0_ref, v1_ref, r_ref, acc_ref, w_ref, sem = rest
+        copies = weight_copies(w_hbm, w_ref, sem, n, chunks)
+        for c in copies:
+            c.start()
+        size = n // chunks
+    else:
+        w_ref, inner_ref, x_ref, down_ref, mid_ref, up_ref, v0_ref, v1_ref, r_ref, acc_ref = rest
     device = device_index()
     start = device * n
 
@@ -327,8 +340,10 @@
     for c in range(chunks):
         copies[c].wait()
         lax.fori_loop(c * size, (c + 1) * size, first, 0, unroll=4 if size % 4 == 0 else 2)
-    saved = pltpu.make_async_copy(x_ref, x_out, sem.at[chunks])
-    saved.start()
+    if not chunks:
+        take_inner(n, inner_ref, x_ref, v1_ref)
+        for b in edge_blocks(n):
+            first(b, 0)
 
     def residual(b):
         p = product(v1_ref, [b + near_of(col_ref, start, b, k) for k in range(K)], weight_of(w_ref, b))
@@ -371,7 +386,20 @@
         where = b // nc
         ref = (down_ref, mid_ref, up_ref)[where]
         ref[b - where * nc] = part.astype(ref.dtype)
-    saved.wait()
+
+
+def edge_blocks(n):
+    return list(range(HB)) + list(range(n - HB, n))
+
+
+def take_inner(n, inner_ref, x_ref, v_ref):
+    def one(b, carry):
+        x = inner_ref[b]
+        x_ref[b] = x
+        v_ref[b + HB] = x.astype(bf16)
+        return carry
+
+    lax.fori_loop(HB, n - HB, one, 0, unroll=4)
 
 
 def pair_targets(own_ref, slot_ref, device, nc, q):
@@ -379,27 +407,27 @@
     return jnp.concatenate([row(2 * q), row(2 * q + 1)], axis=1)
 
 
-def go_down(n, nc, base, col, f, g, own, slot, f_edges, fixed, weights, mib):
-    chunks = 4
+def go_down(n, nc, base, col, f, g, own, slot, f_edges, fixed, weights, mib, inner=None):
+    chunks = 0 if inner is not None else 4
+    loads = [pltpu.VMEM((n * ROWS, BS), bf16), pltpu.SemaphoreType.DMA((4,))] if chunks else []
+    last = (weights,) if chunks else (weights, inner)
     highs = 3 * nc // 2
     return call(
         functools.partial(down_kernel, n, nc, base, chunks), f"down{n}",
         (
             shape((n, R, BS), f32), shape((nc, R, BS), bf16), shape((nc, R, BS), f32), shape((nc, R, BS), bf16)
         ),
-        [smem()] + [vmem()] * 8 + [hbm()],
-        (hbm(), vmem(), vmem(), vmem()),
+        [smem()] + [vmem()] * 8 + ([hbm()] if chunks else [vmem()] * 2),
+        (vmem(),) * 4,
         [
-            pltpu.VMEM((n * ROWS, BS), bf16),
             pltpu.VMEM((n + 2 * EDGE, R, BS), bf16),
             pltpu.VMEM((n + EDGE, R, BS), bf16),
-            pltpu.VMEM((n, R, BS), f32),
             pltpu.VMEM((n // 2, R, 2 * BS), bf16),
             pltpu.VMEM((highs * R, 2 * BS), f32),
-            pltpu.SemaphoreType.DMA((chunks + 1,)),
+            *loads,
         ],
         mib=mib, flops=4 * n * R * ROWS * BS, nbytes=n * ROWS * BS * 2,
-    )(col, f, g, own, slot, *f_edges, *fixed, weights)
+    )(col, f, g, own, slot, *f_edges, *fixed, *last)
 
 
 def rhs_kernel(mid_ref, lo_ref, hi_ref, out_ref, up_ref, down_ref):
@@ -440,13 +468,10 @@
 
 
 def prolong_kernel(
-    n, nc, own_ref, slot_ref, lo_ref, mid_ref, hi_ref, x_hbm, out_ref, first_ref, last_ref, e_ref, x_ref, sem
+    n, nc, own_ref, slot_ref, lo_ref, mid_ref, hi_ref, x_ref, out_ref, first_ref, last_ref, e_ref
 ):
-    copy = pltpu.make_async_copy(x_hbm, x_ref, sem.at[0])
-    copy.start()
     for b in range(3 * nc):
         place(e_ref, b, (lo_ref, mid_ref, hi_ref)[b // nc][b % nc])
-    copy.wait()
     spread(n, nc, e_ref, own_ref, slot_ref, device_index(), x_ref, out_ref)
     first_ref[...] = out_ref[:EDGE].astype(bf16)
     last_ref[...] = out_ref[n - EDGE :].astype(bf16)
@@ -456,28 +481,28 @@
     return call(
         functools.partial(prolong_kernel, n, nc), f"prolong{n}",
         (shape((n, R, BS), f32), shape((EDGE, R, BS), bf16), shape((EDGE, R, BS), bf16)),
-        [vmem()] * 5 + [hbm()],
+        [vmem()] * 6,
         (vmem(),) * 3,
-        [
-            pltpu.VMEM((3 * nc // 2 * R, 2 * BS), bf16),
-            pltpu.VMEM((n, R, BS), f32),
-            pltpu.SemaphoreType.DMA((1,)),
-        ],
+        [pltpu.VMEM((3 * nc // 2 * R, 2 * BS), bf16)],
         mib=12, flops=2 * n * BS * 3 * nc * BS * R, nbytes=2 * n * R * BS * 4,
     )(own, slot, lo, mid, hi, x)
 
 
 def up_kernel(
     n, base, chunks,
-    col_ref, x_ref, xlo_ref, xhi_ref, f_ref, g_ref, flo_ref, fhi_ref, slo_ref, shi_ref, w_hbm,
-    *outs_and_scratch,
+    col_ref, x_ref, xlo_ref, xhi_ref, f_ref, g_ref, flo_ref, fhi_ref, slo_ref, shi_ref, w_ref, *rest,
 ):
-    *outs, w_ref, v0_ref, v1_ref, keep_ref, sem = outs_and_scratch
+    inner_ref = None
+    if chunks:
+        *outs, v0_ref, v1_ref, keep_ref, kept_ref, sem = rest
+        copies = weight_copies(w_ref, kept_ref, sem, n, chunks)
+        w_ref = kept_ref
+        for c in copies:
+            c.start()
+        size = n // chunks
+    else:
+        inner_ref, *outs, v0_ref, v1_ref, keep_ref = rest
     out_ref = outs[0]
-    copies = weight_copies(w_hbm, w_ref, sem, n, chunks)
-    for c in copies:
-        c.start()
-    size = n // chunks
     start = device_index() * n
 
     def fill(b, carry):
@@ -514,6 +539,10 @@
     for c in range(chunks):
         copies[c].wait()
         lax.fori_loop(c * size, (c + 1) * size, first, 0, unroll=4 if size % 4 == 0 else 2)
+    if not chunks:
+        take_inner(n, inner_ref, keep_ref, v1_ref)
+        for b in edge_blocks(n):
+            first(b, 0)
 
     def second(b, carry):
         p = product(v1_ref, near(b, 0), weight_of(w_ref, b))
@@ -525,22 +554,58 @@
     lax.fori_loop(0, n, second, 0, unroll=4)
 
 
-def go_up(n, base, col, x, x_edges, f, g, f_edges, fixed, weights, dtype, mib, outs=1):
-    chunks = 4
+def go_up(n, base, col, x, x_edges, f, g, f_edges, fixed, weights, dtype, mib, outs=1, inner=None):
+    chunks = 0 if inner is not None else 4
+    loads = [pltpu.VMEM((n * ROWS, BS), bf16), pltpu.SemaphoreType.DMA((4,))] if chunks else []
+    last = (weights,) if chunks else (weights, inner)
     return call(
         functools.partial(up_kernel, n, base, chunks), f"up{n}",
         (shape((n, R, BS), dtype),) * outs,
-        [smem()] + [vmem()] * 9 + [hbm()],
+        [smem()] + [vmem()] * 9 + ([hbm()] if chunks else [vmem()] * 2),
         (vmem(),) * outs,
         [
-            pltpu.VMEM((n * ROWS, BS), bf16),
             pltpu.VMEM((n + 2 * EDGE, R, BS), bf16),
             pltpu.VMEM((n + EDGE, R, BS), bf16),
             pltpu.VMEM((n, R, BS), f32),
-            pltpu.SemaphoreType.DMA((chunks,)),
+            *loads,
         ],
         mib=mib, flops=4 * n * R * ROWS * BS, nbytes=n * ROWS * BS * 2,
-    )(col, x, *x_edges, f, g, *f_edges, *fixed, weights)
+    )(col, x, *x_edges, f, g, *f_edges, *fixed, *last)
+
+
+def inner_kernel(n, first_sweep, col_ref, x_ref, f_ref, g_ref, w_ref, out_ref, v_ref):
+    start = device_index() * n
+
+    def scale(b):
+        return damping / g_ref[pl.ds(b, 1), :]
+
+    def fill(b, carry):
+        x = f_ref[b].astype(f32) * scale(b) if first_sweep else x_ref[b]
+        v_ref[b] = x.astype(bf16)
+        return carry
+
+    lax.fori_loop(0, n, fill, 0, unroll=4)
+
+    def one(b, carry):
+        p = product(v_ref, [b - HB + near_of(col_ref, start, b, k) for k in range(K)], weight_of(w_ref, b))
+        s = scale(b)
+        f = f_ref[b].astype(f32)
+        out_ref[b] = 1.2 * (f * s) + s * p if first_sweep else 0.2 * x_ref[b] + s * (f + p)
+        return carry
+
+    lax.fori_loop(HB, n - HB, one, 0, unroll=4)
+    blank = jnp.zeros((R, BS), f32)
+    for b in list(range(HB)) + list(range(n - HB, n)):
+        out_ref[b] = blank
+
+
+def inner_sweep(n, first_sweep, col, x, f, g, w):
+    return call(
+        functools.partial(inner_kernel, n, first_sweep), "inner" + ("down" if first_sweep else "up"),
+        shape((n, R, BS), f32),
+        [smem()] + [vmem()] * 4, vmem(), [pltpu.VMEM((n, R, BS), bf16)],
+        mib=12, flops=2 * n * R * ROWS * BS, nbytes=2**20,
+    )(col, x, f, g, w)
 
 
 def parts_kernel(low_ref, mid_ref, high_ref, out_ref, copy_ref):
@@ -675,21 +740,14 @@
     )(*args)
 
 
-def coarse_kernel(got_ref, z_ref, s_hbm, out_ref, copy_ref, s_ref, sem):
+def coarse_kernel(got_ref, z_ref, s_ref, out_ref, copy_ref):
     count = got_ref.shape[0]
     chunks = 4
     size = count // chunks
-    copies = [
-        pltpu.make_async_copy(s_hbm.at[:, pl.ds(c * size * BS, size * BS)], s_ref.at[c], sem.at[c])
-        for c in range(chunks)
-    ]
-    for c in copies:
-        c.start()
     u = jnp.zeros((R, C3), f32)
     for c in range(chunks):
-        copies[c].wait()
         u = u + lax.dot_general(
-            joined(got_ref, range(c * size, (c + 1) * size)), s_ref[c],
+            joined(got_ref, range(c * size, (c + 1) * size)), s_ref[:, c * size * BS : (c + 1) * size * BS],
             (((1,), (1,)), ((), ())), preferred_element_type=f32,
         )
     out_ref[0] = u.astype(bf16)
@@ -701,8 +759,7 @@
     count = got.shape[0]
     return call(
         coarse_kernel, "coarse", (shape((1 + NB2, R, BS), bf16),) * 2,
-        [vmem(), vmem(), hbm()], (vmem(),) * 2,
-        [pltpu.VMEM((4, C3, count // 4 * BS), bf16), pltpu.SemaphoreType.DMA((4,))],
+        [vmem()] * 3, (vmem(),) * 2,
         flops=2**26, nbytes=2**21,
     )(got, z, inverse_rows)
 
@@ -723,12 +780,10 @@
 
 def third_up_kernel(
     own_ref, lo_ref, hi_ref, ulo_ref, uhi_ref, z_ref, w3_ref, tail_ref, slo_ref, shi_ref, rlo_ref, rhi_ref,
-    own2_ref, slot2_ref, x_hbm,
+    own2_ref, slot2_ref, x_ref,
     out_ref, first_ref, last_ref,
-    v0_ref, v1_ref, e_ref, x_ref, sem,
+    v0_ref, v1_ref, e_ref,
 ):
-    copy = pltpu.make_async_copy(x_hbm, x_ref, sem.at[0])
-    copy.start()
     diagonal, weights, columns, row = third_fixed(w3_ref, tail_ref, slo_ref, shi_ref, rlo_ref, rhi_ref)
     inv = [damping / g for g in diagonal]
     u = [ulo_ref[0], ulo_ref[1], ulo_ref[2], lo_ref[0], own_ref[0], hi_ref[0], uhi_ref[0], uhi_ref[1], uhi_ref[2]]
@@ -757,7 +812,6 @@
         i = j % NB2
         z = (lambda: lo_ref[1 + i].astype(f32), lambda: z_ref[i], lambda: hi_ref[1 + i].astype(f32))[j // NB2]()
         place(e_ref, j, (z + y2).astype(bf16))
-    copy.wait()
     spread(NB1, NB2, e_ref, own2_ref, slot2_ref, device_index(), x_ref, out_ref)
     first_ref[...] = out_ref[:EDGE].astype(bf16)
     last_ref[...] = out_ref[NB1 - EDGE :].astype(bf16)
@@ -768,11 +822,10 @@
     return call(
         third_up_kernel, "up2",
         (shape((NB1, R, BS), f32), shape((EDGE, R, BS), bf16), shape((EDGE, R, BS), bf16)),
-        [vmem()] * 14 + [hbm()], (vmem(),) * 3,
+        [vmem()] * 15, (vmem(),) * 3,
         [
             pltpu.VMEM((count, R, BS), bf16), pltpu.VMEM((count - 4, R, BS), bf16),
-            pltpu.VMEM((3 * NB2 // 2 * R, 2 * BS), bf16), pltpu.VMEM((NB1, R, BS), f32),
-            pltpu.SemaphoreType.DMA((1,)),
+            pltpu.VMEM((3 * NB2 // 2 * R, 2 * BS), bf16),
         ],
         mib=12, flops=2**27, nbytes=2**21,
     )(*args)
@@ -789,17 +842,17 @@
     f = right_sides
     columns_fine, columns_second, columns_third = columns_fine.T, columns_second.T, columns_third.T
     w1, w2, w3 = (in_hbm(flat(w)) for w in (weights_fine, weights_second, weights_third))
-    coarse_inverse = in_hbm(coarse_inverse)
-    edges1 = both_ways(*first_edges(in_hbm(flat(f)), w1, degree_fine, columns_fine))
-    g1, g2, _, up, down, w3, tail = fixed_data(
+    edges1 = both_ways(*first_edges(in_hbm(flat(f)), w1, in_hbm(degree_fine), in_hbm(columns_fine)))
+    g1, g2, _, up, down, w3, tail, kept1 = fixed_data(
         w1, w2, w3, degree_fine, degree_second, degree_third, columns_second, columns_third, owners_third, slots_third
     )
     fixed = both_ways(up, down)
     far = both_ways(*far_data(w3, tail, *fixed), 2)
     third = (w3, tail, *fixed, *far)
 
+    inner = inner_sweep(NB0, True, columns_fine, f, f, g1, kept1)
     x1, low, mid, high = go_down(
-        NB0, NB1, F_ROWS, columns_fine, f, g1, owners_fine, slots_fine, edges1, edges1, w1, 20
+        NB0, NB1, F_ROWS, columns_fine, f, g1, owners_fine, slots_fine, edges1, edges1, kept1, 20, inner
     )
     lo, hi = both_ways(high, low)
     f2, up, down = second_rhs(mid, lo, hi)
@@ -823,7 +876,8 @@
     lo, hi = both_ways(copy, x2)
     x1, first, last = prolong(NB0, NB1, owners_fine, slots_fine, lo, x2, hi, x1)
     x_edges = both_ways(last, first)
-    return go_up(NB0, F_ROWS, columns_fine, x1, x_edges, f, g1, edges1, edges1, w1, f32, 20)[0]
+    inner = inner_sweep(NB0, False, columns_fine, x1, f, g1, kept1)
+    return go_up(NB0, F_ROWS, columns_fine, x1, x_edges, f, g1, edges1, edges1, kept1, f32, 20, 1, inner)[0]
 
 
 def solution(mesh):

time: 168 us -> 162 us (0.964)
  waiting for transfers between devices: 19.2 us -> 16.9 us
  Pallas kernels: 35.6 us -> 33.9 us
    pallas_call x1 -> x3, Pallas kernels: 1.93 us -> 6 us  [the longest x2 4.56 us: inner_sweep(): call(functools.partial(inner_kernel, n, first_sweep), 'inner' + ('down' i...]
    ppermute x24, waiting for transfers between devices: 19.2 us -> 16.9 us  [passed_along(): lax.ppermute(value, AXES, [(s, (s + steps) % count) for s in range(count)])]
    pallas_call x2, Pallas kernels: 8.93 us -> 6.81 us  [go_up(): call(functools.partial(up_kernel, n, base, chunks), f'up{n}', (shape((n,...]
    pallas_call x2, Pallas kernels: 11 us -> 8.86 us  [go_down(): call(functools.partial(down_kernel, n, nc, base, chunks), f'down{n}', (sh...]
  transfers between devices with their start and end apart: 24 -> 24, of which waited for: 11 -> 9; matrix products, arithmetic and copies ran while one was open for 0% -> 0% of each run, Pallas kernels for 9% -> 11%
where the time goes in v4:
time: 162 us
  starting transfers between devices  93.4 us (58%)
  Pallas kernels  33.9 us (21%)
  blocking collectives  17.5 us (11%)
  waiting for transfers between devices  16.9 us (10%)
    ppermute x24, starting transfers between devices, passed_along(): lax.ppermute(value, AXES, [(s, (s + steps) % count) for s in range(count)])  93.4 us
    all_to_all x1, blocking collectives, on_device(): got = lax.all_to_all(c, 'col', 0, 0, tiled=True)  17.5 us
    ppermute x24, waiting for transfers between devices, passed_along(): lax.ppermute(value, AXES, [(s, (s + steps) % count) for s in range(count)])  16.9 us
    pallas_call x2, Pallas kernels, go_down(): call(functools.partial(down_kernel, n, nc, base, chunks), f'down{n}', (sh...  8.86 us
    pallas_call x2, Pallas kernels, go_up(): call(functools.partial(up_kernel, n, base, chunks), f'up{n}', (shape((n,...  6.81 us
    pallas_call x1, Pallas kernels, prolong(): call(functools.partial(prolong_kernel, n, nc), f'prolong{n}', (shape((n,...  4.93 us
    pallas_call x2, Pallas kernels, inner_sweep(): call(functools.partial(inner_kernel, n, first_sweep), 'inner' + ('down' i...  4.56 us
    pallas_call x1, Pallas kernels, fixed_data(): call(fixed_kernel, 'fixed', (shape((NB0, BS), f32), shape((NB1, BS), f32)...  3.97 us
  transfers between devices with their start and end apart: 24, of which 9 were waited for; matrix products, arithmetic and copies ran while one was open for 0% of the time, Pallas kernels for 11%

profile of v4, /device:TPU:0, one launch (start us, length us, event | category | flops | bytes accessed | tf_op | source)
XLA Modules:
  0.0 162.3 jit_solution(9189116698599046400)
XLA Ops:
  1.8 8.1 %collective-permute-start.1 = (bf16[1040,128]{1,0:T(8,128)(2,1)S(1)}, bf16[1040,128]{1,0:T(8,128)(2,1)S(1)}, u32[]{:S(2)}, u32[]{:S(2)}) collective-permute-start(bf16[1040,128]{1,0:T(8,128)(2,1)S(1)} %get-tuple-element.48), channel_id=1, source_target_pairs={{0,255},{1,0},{2,1},{3,2},{4,3},{5,4},{6,5},{7,6},{8,7},{9,8},{10,... | collective-permute-start | bytes 798728 | tf_op jit(solution)/shard_map/ppermute | solution.py:39
  10.0 4.0 %fixed.1 = (f32[32,128]{1,0:T(8,128)S(1)}, f32[8,128]{1,0:T(8,128)S(1)}, f32[2,128]{1,0:T(2,128)}, bf16[1568,128]{1,0:T(8,128)(2,1)S(1)}, bf16[1568,128]{1,0:T(8...) custom-call(bf16[12288,128]{1,0:T(8,128)(2,1)} %bitcast.18, ...), custom_call_target="tpu_custom_call" | custom-call | flops 1073741824 | bytes 4194304 | tf_op jit(solution)/shard_map/fixed/pallas_call | solution.py:239
  14.1 7.2 %collective-permute-start.7 = (bf16[1568,128]{1,0:T(8,128)(2,1)S(1)}, bf16[1568,128]{1,0:T(8,128)(2,1)S(1)}, u32[]{:S(2)}, u32[]{:S(2)}) collective-permute-start(bf16[1568,128]{1,0:T(8,128)(2,1)S(1)} %get-tuple-element.58), channel_id=1, source_target_pairs={{0,255},{1,0},{2,1},{3,2},{4,3},{5,4},{6,5},{7,6},{8,7},{9,8},{10,... | collective-permute-start | bytes 1204232 | tf_op jit(solution)/shard_map/ppermute | solution.py:39
  23.7 5.8 %down32.1 = (f32[32,64,128]{2,1,0:T(8,128)S(1)}, bf16[8,64,128]{2,1,0:T(8,128)(2,1)S(1)}, f32[8,64,128]{2,1,0:T(8,128)S(1)}, bf16[8,64,128]{2,1,0:T(8,128)(2,1)S(1)}) custom-call(s32[3,32]{1,0:T(4,128)S(1)} %bitcast.10, bf16[32,64,128]{2,1,0:T(8,128)(2,1)S(1)} %copy-done, f32[32,128]{1,0:T(8,128)S(1)} %get-tuple-element.46.g_ref, s32[32,128]{1,0:T(8,128)S(1)} %copy-done.5, ...), custom_call_target="tpu_custom_call" | custom-call | flops 402653184 | bytes 3145728 | tf_op jit(solution)/shard_map/down32/pallas_call | solution.py:415
  29.6 7.2 %collective-permute-start.3 = (bf16[8,64,128]{2,1,0:T(8,128)(2,1)S(1)}, bf16[8,64,128]{2,1,0:T(8,128)(2,1)S(1)}, u32[]{:S(2)}, u32[]{:S(2)}) collective-permute-start(bf16[8,64,128]{2,1,0:T(8,128)(2,1)S(1)} %get-tuple-element.52), channel_id=1, source_target_pairs={{0,255},{1,0},{2,1},{3,2},{4,3},{5,4},{6,5},{7,6},{8,7},{9,8},{10,... | collective-permute-start | bytes 393224 | tf_op jit(solution)/shard_map/ppermute | solution.py:39
  36.8 2.6 %collective-permute-done.2.lo_ref = bf16[8,64,128]{2,1,0:T(8,128)(2,1)S(1)} collective-permute-done((bf16[8,64,128]{2,1,0:T(8,128)(2,1)S(1)}, bf16[8,64,128]{2,1,0:T(8,128)(2,1)S(1)}, u32[]{:S(2)}, u32[]{:S(2)}) %collective-permute-start.2) | collective-permute-done | bytes 131104 | tf_op jit(solution)/shard_map/ppermute | solution.py:39
  39.6 7.2 %collective-permute-start.5 = (bf16[4,64,128]{2,1,0:T(8,128)(2,1)S(1)}, bf16[4,64,128]{2,1,0:T(8,128)(2,1)S(1)}, u32[]{:S(2)}, u32[]{:S(2)}) collective-permute-start(bf16[4,64,128]{2,1,0:T(8,128)(2,1)S(1)} %get-tuple-element.56), channel_id=1, source_target_pairs={{0,255},{1,0},{2,1},{3,2},{4,3},{5,4},{6,5},{7,6},{8,7},{9,8},{10,... | collective-permute-start | bytes 196616 | tf_op jit(solution)/shard_map/ppermute | solution.py:39
  47.0 8.1 %collective-permute-start.13 = (bf16[816,128]{1,0:T(8,128)(2,1)S(1)}, bf16[816,128]{1,0:T(8,128)(2,1)S(1)}, u32[]{:S(2)}, u32[]{:S(2)}) collective-permute-start(bf16[816,128]{1,0:T(8,128)(2,1)S(1)} %get-tuple-element.70), channel_id=1, source_target_pairs={{0,254},{1,255},{2,0},{3,1},{4,2},{5,3},{6,4},{7,5},{8,6},{9,7},{1... | collective-permute-start | bytes 626696 | tf_op jit(solution)/shard_map/ppermute | solution.py:39
  55.1 3.0 %down8.1 = (f32[8,64,128]{2,1,0:T(8,128)S(1)}, bf16[2,64,128]{2,1,0:T(8,128)(2,1)S(1)}, f32[2,64,128]{2,1,0:T(8,128)S(1)}, bf16[2,64,128]{2,1,0:T(8,128)(2,1)S(1)}) custom-call(s32[3,8]{1,0:T(4,128)S(1)} %bitcast.14, f32[8,64,128]{2,1,0:T(8,128)S(1)} %get-tuple-element.53.f_ref, f32[8,128]{1,0:T(8,128)S(1)} %get-tuple-element.54.g_ref, ...), custom_call_target="tpu_custom_call" | custom-call | flops 100663296 | bytes 786432 | tf_op jit(solution)/shard_map/down8/pallas_call | solution.py:415
  58.2 7.2 %collective-permute-start.9 = (bf16[6,64,128]{2,1,0:T(8,128)(2,1)S(1)}, bf16[6,64,128]{2,1,0:T(8,128)(2,1)S(1)}, u32[]{:S(2)}, u32[]{:S(2)}) collective-permute-start(bf16[6,64,128]{2,1,0:T(8,128)(2,1)S(1)} %get-tuple-element.62.p_ref), channel_id=1, source_target_pairs={{0,255},{1,0},{2,1},{3,2},{4,3},{5,4},{6,5},{7,6},{8,7},{9,8},{10,... | collective-permute-start | bytes 294920 | tf_op jit(solution)/shard_map/ppermute | solution.py:39
  65.4 2.4 %collective-permute-done.8.lo_ref = bf16[6,64,128]{2,1,0:T(8,128)(2,1)S(1)} collective-permute-done((bf16[6,64,128]{2,1,0:T(8,128)(2,1)S(1)}, bf16[6,64,128]{2,1,0:T(8,128)(2,1)S(1)}, u32[]{:S(2)}, u32[]{:S(2)}) %collective-permute-start.8) | collective-permute-done | bytes 98336 | tf_op jit(solution)/shard_map/ppermute | solution.py:39
  67.9 9.0 %collective-permute-start.11 = (bf16[6,64,128]{2,1,0:T(8,128)(2,1)S(1)}, bf16[6,64,128]{2,1,0:T(8,128)(2,1)S(1)}, u32[]{:S(2)}, u32[]{:S(2)}) collective-permute-start(bf16[6,64,128]{2,1,0:T(8,128)(2,1)S(1)} %get-tuple-element.66), channel_id=1, source_target_pairs={{0,253},{1,254},{2,255},{3,0},{4,1},{5,2},{6,3},{7,4},{8,5},{9,6},... | collective-permute-start | bytes 294920 | tf_op jit(solution)/shard_map/ppermute | solution.py:39
  81.0 17.5 %all_to_all.5.got_ref = bf16[32,64,128]{2,1,0:T(8,128)(2,1)S(1)} all-to-all(bf16[32,64,128]{2,1,0:T(8,128)(2,1)S(1)} %get-tuple-element.71), channel_id=1, replica_groups=mesh['row'=8,'col'=32] {'col'}, dimensions={0} | all-to-all | bytes 1048576 | tf_op jit(solution)/shard_map/all_to_all | solution.py:868
  99.0 2.8 %collective-permute-start.14 = (bf16[3,64,128]{2,1,0:T(8,128)(2,1)S(1)}, bf16[3,64,128]{2,1,0:T(8,128)(2,1)S(1)}, u32[]{:S(2)}, u32[]{:S(2)}) collective-permute-start(bf16[3,64,128]{2,1,0:T(8,128)(2,1)S(1)} %get-tuple-element.74), channel_id=1, source_target_pairs={{0,1},{1,2},{2,3},{3,4},{4,5},{5,6},{6,7},{7,8},{8,9},{9,10},{10,1... | collective-permute-start | bytes 147464 | tf_op jit(solution)/shard_map/ppermute | solution.py:39
  101.8 4.9 %collective-permute-start.15 = (bf16[3,64,128]{2,1,0:T(8,128)(2,1)S(1)}, bf16[3,64,128]{2,1,0:T(8,128)(2,1)S(1)}, u32[]{:S(2)}, u32[]{:S(2)}) collective-permute-start(bf16[3,64,128]{2,1,0:T(8,128)(2,1)S(1)} %get-tuple-element.73.own_ref), channel_id=1, source_target_pairs={{0,255},{1,0},{2,1},{3,2},{4,3},{5,4},{6,5},{7,6},{8,7},{9,8},{10,... | collective-permute-start | bytes 147464 | tf_op jit(solution)/shard_map/ppermute | solution.py:39
  108.5 9.0 %collective-permute-start.17 = (bf16[3,64,128]{2,1,0:T(8,128)(2,1)S(1)}, bf16[3,64,128]{2,1,0:T(8,128)(2,1)S(1)}, u32[]{:S(2)}, u32[]{:S(2)}) collective-permute-start(bf16[3,64,128]{2,1,0:T(8,128)(2,1)S(1)} %get-tuple-element.76), channel_id=1, source_target_pairs={{0,253},{1,254},{2,255},{3,0},{4,1},{5,2},{6,3},{7,4},{8,5},{9,6},... | collective-permute-start | bytes 147464 | tf_op jit(solution)/shard_map/ppermute | solution.py:39
  117.5 2.4 %collective-permute-done.16.ulo_ref = bf16[3,64,128]{2,1,0:T(8,128)(2,1)S(1)} collective-permute-done((bf16[3,64,128]{2,1,0:T(8,128)(2,1)S(1)}, bf16[3,64,128]{2,1,0:T(8,128)(2,1)S(1)}, u32[]{:S(2)}, u32[]{:S(2)}) %collective-permute-start.16) | collective-permute-done | bytes 49184 | tf_op jit(solution)/shard_map/ppermute | solution.py:39
  121.8 7.2 %collective-permute-start.19 = (bf16[4,64,128]{2,1,0:T(8,128)(2,1)S(1)}, bf16[4,64,128]{2,1,0:T(8,128)(2,1)S(1)}, u32[]{:S(2)}, u32[]{:S(2)}) collective-permute-start(bf16[4,64,128]{2,1,0:T(8,128)(2,1)S(1)} %get-tuple-element.80), channel_id=1, source_target_pairs={{0,255},{1,0},{2,1},{3,2},{4,3},{5,4},{6,5},{7,6},{8,7},{9,8},{10,... | collective-permute-start | bytes 196616 | tf_op jit(solution)/shard_map/ppermute | solution.py:39
  130.9 2.7 %up8.1 = (bf16[8,64,128]{2,1,0:T(8,128)(2,1)S(1)}, bf16[8,64,128]{2,1,0:T(8,128)(2,1)S(1)}) custom-call(s32[3,8]{1,0:T(4,128)S(1)} %bitcast.15, f32[8,64,128]{2,1,0:T(8,128)S(1)} %get-tuple-element.78.x_ref, bf16[4,64,128]{2,1,0:T(8,128)(2,1)S(1)} %collective-permute-done.18.xlo_ref, bf16[4,64,128]{2,1,0:T(8,128)(2,1)S(1)} %collective-permute-done.19.xhi_ref, ...), custom_call_target="tpu_custom_call" | custom-call | flops 100663296 | bytes 786432 | tf_op jit(solution)/shard_map/up8/pallas_call | solution.py:561
  133.7 7.2 %collective-permute-start.21 = (bf16[8,64,128]{2,1,0:T(8,128)(2,1)S(1)}, bf16[8,64,128]{2,1,0:T(8,128)(2,1)S(1)}, u32[]{:S(2)}, u32[]{:S(2)}) collective-permute-start(bf16[8,64,128]{2,1,0:T(8,128)(2,1)S(1)} %get-tuple-element.82.mid_ref), channel_id=1, source_target_pairs={{0,255},{1,0},{2,1},{3,2},{4,3},{5,4},{6,5},{7,6},{8,7},{9,8},{10,... | collective-permute-start | bytes 393224 | tf_op jit(solution)/shard_map/ppermute | solution.py:39
  141.0 2.6 %collective-permute-done.20.lo_ref = bf16[8,64,128]{2,1,0:T(8,128)(2,1)S(1)} collective-permute-done((bf16[8,64,128]{2,1,0:T(8,128)(2,1)S(1)}, bf16[8,64,128]{2,1,0:T(8,128)(2,1)S(1)}, u32[]{:S(2)}, u32[]{:S(2)}) %collective-permute-start.20) | collective-permute-done | bytes 131104 | tf_op jit(solution)/shard_map/ppermute | solution.py:39
  143.5 4.9 %prolong32.1 = (f32[32,64,128]{2,1,0:T(8,128)S(1)}, bf16[4,64,128]{2,1,0:T(8,128)(2,1)S(1)}, bf16[4,64,128]{2,1,0:T(8,128)(2,1)S(1)}) custom-call(s32[32,128]{1,0:T(8,128)S(1)} %copy-done.5, s32[32,128]{1,0:T(8,128)S(1)} %copy-done.6, bf16[8,64,128]{2,1,0:T(8,128)(2,1)S(1)} %collective-permute-done.20.lo_ref, ...), custom_call_target="tpu_custom_call" | custom-call | flops 1610612736 | bytes 2097152 | tf_op jit(solution)/shard_map/prolong32/pallas_call | solution.py:481
  148.6 7.3 %collective-permute-start.23 = (bf16[4,64,128]{2,1,0:T(8,128)(2,1)S(1)}, bf16[4,64,128]{2,1,0:T(8,128)(2,1)S(1)}, u32[]{:S(2)}, u32[]{:S(2)}) collective-permute-start(bf16[4,64,128]{2,1,0:T(8,128)(2,1)S(1)} %get-tuple-element.86), channel_id=1, source_target_pairs={{0,255},{1,0},{2,1},{3,2},{4,3},{5,4},{6,5},{7,6},{8,7},{9,8},{10,... | collective-permute-start | bytes 196616 | tf_op jit(solution)/shard_map/ppermute | solution.py:39
  158.2 4.1 %up32.1 = f32[32,64,128]{2,1,0:T(8,128)} custom-call(s32[3,32]{1,0:T(4,128)S(1)} %bitcast.12, f32[32,64,128]{2,1,0:T(8,128)S(1)} %get-tuple-element.84.x_ref, bf16[4,64,128]{2,1,0:T(8,128)(2,1)S(1)} %collective-permute-done.22.xlo_ref, bf16[4,64,128]{2,1,0:T(8,128)(2,1)S(1)} %collective-permute-done.23.xhi_ref, bf16[32,64,128]{2,1,0:T(8,128)(2,1)S(1)} %copy-done, ...), custom_call_target="tpu_custom_call" | custom-call | flops 402653184 | bytes 3145728 | tf_op jit(solution)/shard_map/up32/pallas_call | solution.py:561
  (71 shorter events, 17.6 us)
Async XLA Ops:
  1.5 22.2 %collective-permute-start = (bf16[1040,128]{1,0:T(8,128)(2,1)S(1)}, bf16[1040,128]{1,0:T(8,128)(2,1)S(1)}, u32[]{:S(2)}, u32[]{:S(2)}) collective-permute-start(bf16[1040,128]{1,0:T(8,128)(2,1)S(1)} %get-tuple-element.47), channel_id=1, source_target_pairs={{0,1},{1,2},{2,3},{3,4},{4,5},{5,6},{6,7},{7,8},{8,9},{9,10},{10,1... | collective-permute-start | bytes 798728 | tf_op jit(solution)/shard_map/ppermute | solution.py:39
  1.8 21.9 %collective-permute-start.1 = (bf16[1040,128]{1,0:T(8,128)(2,1)S(1)}, bf16[1040,128]{1,0:T(8,128)(2,1)S(1)}, u32[]{:S(2)}, u32[]{:S(2)}) collective-permute-start(bf16[1040,128]{1,0:T(8,128)(2,1)S(1)} %get-tuple-element.48), channel_id=1, source_target_pairs={{0,255},{1,0},{2,1},{3,2},{4,3},{5,4},{6,5},{7,6},{8,7},{9,8},{10,... | collective-permute-start | bytes 798728 | tf_op jit(solution)/shard_map/ppermute | solution.py:39
  14.0 32.8 %collective-permute-start.6 = (bf16[1568,128]{1,0:T(8,128)(2,1)S(1)}, bf16[1568,128]{1,0:T(8,128)(2,1)S(1)}, u32[]{:S(2)}, u32[]{:S(2)}) collective-permute-start(bf16[1568,128]{1,0:T(8,128)(2,1)S(1)} %get-tuple-element.57), channel_id=1, source_target_pairs={{0,1},{1,2},{2,3},{3,4},{4,5},{5,6},{6,7},{7,8},{8,9},{9,10},{10,1... | collective-permute-start | bytes 1204232 | tf_op jit(solution)/shard_map/ppermute | solution.py:39
  14.1 32.7 %collective-permute-start.7 = (bf16[1568,128]{1,0:T(8,128)(2,1)S(1)}, bf16[1568,128]{1,0:T(8,128)(2,1)S(1)}, u32[]{:S(2)}, u32[]{:S(2)}) collective-permute-start(bf16[1568,128]{1,0:T(8,128)(2,1)S(1)} %get-tuple-element.58), channel_id=1, source_target_pairs={{0,255},{1,0},{2,1},{3,2},{4,3},{5,4},{6,5},{7,6},{8,7},{9,8},{10,... | collective-permute-start | bytes 1204232 | tf_op jit(solution)/shard_map/ppermute | solution.py:39
  29.5 9.9 %collective-permute-start.2 = (bf16[8,64,128]{2,1,0:T(8,128)(2,1)S(1)}, bf16[8,64,128]{2,1,0:T(8,128)(2,1)S(1)}, u32[]{:S(2)}, u32[]{:S(2)}) collective-permute-start(bf16[8,64,128]{2,1,0:T(8,128)(2,1)S(1)} %get-tuple-element.51), channel_id=1, source_target_pairs={{0,1},{1,2},{2,3},{3,4},{4,5},{5,6},{6,7},{7,8},{8,9},{9,10},{10,1... | collective-permute-start | bytes 393224 | tf_op jit(solution)/shard_map/ppermute | solution.py:39
  29.6 9.8 %collective-permute-start.3 = (bf16[8,64,128]{2,1,0:T(8,128)(2,1)S(1)}, bf16[8,64,128]{2,1,0:T(8,128)(2,1)S(1)}, u32[]{:S(2)}, u32[]{:S(2)}) collective-permute-start(bf16[8,64,128]{2,1,0:T(8,128)(2,1)S(1)} %get-tuple-element.52), channel_id=1, source_target_pairs={{0,255},{1,0},{2,1},{3,2},{4,3},{5,4},{6,5},{7,6},{8,7},{9,8},{10,... | collective-permute-start | bytes 393224 | tf_op jit(solution)/shard_map/ppermute | solution.py:39
  39.5 15.6 %collective-permute-start.4 = (bf16[4,64,128]{2,1,0:T(8,128)(2,1)S(1)}, bf16[4,64,128]{2,1,0:T(8,128)(2,1)S(1)}, u32[]{:S(2)}, u32[]{:S(2)}) collective-permute-start(bf16[4,64,128]{2,1,0:T(8,128)(2,1)S(1)} %get-tuple-element.55), channel_id=1, source_target_pairs={{0,1},{1,2},{2,3},{3,4},{4,5},{5,6},{6,7},{7,8},{8,9},{9,10},{10,1... | collective-permute-start | bytes 196616 | tf_op jit(solution)/shard_map/ppermute | solution.py:39
  39.6 15.5 %collective-permute-start.5 = (bf16[4,64,128]{2,1,0:T(8,128)(2,1)S(1)}, bf16[4,64,128]{2,1,0:T(8,128)(2,1)S(1)}, u32[]{:S(2)}, u32[]{:S(2)}) collective-permute-start(bf16[4,64,128]{2,1,0:T(8,128)(2,1)S(1)} %get-tuple-element.56), channel_id=1, source_target_pairs={{0,255},{1,0},{2,1},{3,2},{4,3},{5,4},{6,5},{7,6},{8,7},{9,8},{10,... | collective-permute-start | bytes 196616 | tf_op jit(solution)/shard_map/ppermute | solution.py:39
  46.9 30.0 %collective-permute-start.12 = (bf16[816,128]{1,0:T(8,128)(2,1)S(1)}, bf16[816,128]{1,0:T(8,128)(2,1)S(1)}, u32[]{:S(2)}, u32[]{:S(2)}) collective-permute-start(bf16[816,128]{1,0:T(8,128)(2,1)S(1)} %get-tuple-element.69), channel_id=1, source_target_pairs={{0,2},{1,3},{2,4},{3,5},{4,6},{5,7},{6,8},{7,9},{8,10},{9,11},{10,... | collective-permute-start | bytes 626696 | tf_op jit(solution)/shard_map/ppermute | solution.py:39
  47.0 29.9 %collective-permute-start.13 = (bf16[816,128]{1,0:T(8,128)(2,1)S(1)}, bf16[816,128]{1,0:T(8,128)(2,1)S(1)}, u32[]{:S(2)}, u32[]{:S(2)}) collective-permute-start(bf16[816,128]{1,0:T(8,128)(2,1)S(1)} %get-tuple-element.70), channel_id=1, source_target_pairs={{0,254},{1,255},{2,0},{3,1},{4,2},{5,3},{6,4},{7,5},{8,6},{9,7},{1... | collective-permute-start | bytes 626696 | tf_op jit(solution)/shard_map/ppermute | solution.py:39
  58.2 9.6 %collective-permute-start.8 = (bf16[6,64,128]{2,1,0:T(8,128)(2,1)S(1)}, bf16[6,64,128]{2,1,0:T(8,128)(2,1)S(1)}, u32[]{:S(2)}, u32[]{:S(2)}) collective-permute-start(bf16[6,64,128]{2,1,0:T(8,128)(2,1)S(1)} %get-tuple-element.63), channel_id=1, source_target_pairs={{0,1},{1,2},{2,3},{3,4},{4,5},{5,6},{6,7},{7,8},{8,9},{9,10},{10,1... | collective-permute-start | bytes 294920 | tf_op jit(solution)/shard_map/ppermute | solution.py:39
  58.2 9.5 %collective-permute-start.9 = (bf16[6,64,128]{2,1,0:T(8,128)(2,1)S(1)}, bf16[6,64,128]{2,1,0:T(8,128)(2,1)S(1)}, u32[]{:S(2)}, u32[]{:S(2)}) collective-permute-start(bf16[6,64,128]{2,1,0:T(8,128)(2,1)S(1)} %get-tuple-element.62.p_ref), channel_id=1, source_target_pairs={{0,255},{1,0},{2,1},{3,2},{4,3},{5,4},{6,5},{7,6},{8,7},{9,8},{10,... | collective-permute-start | bytes 294920 | tf_op jit(solution)/shard_map/ppermute | solution.py:39
  67.8 11.4 %collective-permute-start.10 = (bf16[6,64,128]{2,1,0:T(8,128)(2,1)S(1)}, bf16[6,64,128]{2,1,0:T(8,128)(2,1)S(1)}, u32[]{:S(2)}, u32[]{:S(2)}) collective-permute-start(bf16[6,64,128]{2,1,0:T(8,128)(2,1)S(1)} %get-tuple-element.65), channel_id=1, source_target_pairs={{0,3},{1,4},{2,5},{3,6},{4,7},{5,8},{6,9},{7,10},{8,11},{9,12},{10... | collective-permute-start | bytes 294920 | tf_op jit(solution)/shard_map/ppermute | solution.py:39
  67.9 12.2 %collective-permute-start.11 = (bf16[6,64,128]{2,1,0:T(8,128)(2,1)S(1)}, bf16[6,64,128]{2,1,0:T(8,128)(2,1)S(1)}, u32[]{:S(2)}, u32[]{:S(2)}) collective-permute-start(bf16[6,64,128]{2,1,0:T(8,128)(2,1)S(1)} %get-tuple-element.66), channel_id=1, source_target_pairs={{0,253},{1,254},{2,255},{3,0},{4,1},{5,2},{6,3},{7,4},{8,5},{9,6},... | collective-permute-start | bytes 294920 | tf_op jit(solution)/shard_map/ppermute | solution.py:39
  99.0 9.4 %collective-permute-start.14 = (bf16[3,64,128]{2,1,0:T(8,128)(2,1)S(1)}, bf16[3,64,128]{2,1,0:T(8,128)(2,1)S(1)}, u32[]{:S(2)}, u32[]{:S(2)}) collective-permute-start(bf16[3,64,128]{2,1,0:T(8,128)(2,1)S(1)} %get-tuple-element.74), channel_id=1, source_target_pairs={{0,1},{1,2},{2,3},{3,4},{4,5},{5,6},{6,7},{7,8},{8,9},{9,10},{10,1... | collective-permute-start | bytes 147464 | tf_op jit(solution)/shard_map/ppermute | solution.py:39
  101.8 6.6 %collective-permute-start.15 = (bf16[3,64,128]{2,1,0:T(8,128)(2,1)S(1)}, bf16[3,64,128]{2,1,0:T(8,128)(2,1)S(1)}, u32[]{:S(2)}, u32[]{:S(2)}) collective-permute-start(bf16[3,64,128]{2,1,0:T(8,128)(2,1)S(1)} %get-tuple-element.73.own_ref), channel_id=1, source_target_pairs={{0,255},{1,0},{2,1},{3,2},{4,3},{5,4},{6,5},{7,6},{8,7},{9,8},{10,... | collective-permute-start | bytes 147464 | tf_op jit(solution)/shard_map/ppermute | solution.py:39
  108.4 11.5 %collective-permute-start.16 = (bf16[3,64,128]{2,1,0:T(8,128)(2,1)S(1)}, bf16[3,64,128]{2,1,0:T(8,128)(2,1)S(1)}, u32[]{:S(2)}, u32[]{:S(2)}) collective-permute-start(bf16[3,64,128]{2,1,0:T(8,128)(2,1)S(1)} %get-tuple-element.75), channel_id=1, source_target_pairs={{0,3},{1,4},{2,5},{3,6},{4,7},{5,8},{6,9},{7,10},{8,11},{9,12},{10... | collective-permute-start | bytes 147464 | tf_op jit(solution)/shard_map/ppermute | solution.py:39
  108.5 11.4 %collective-permute-start.17 = (bf16[3,64,128]{2,1,0:T(8,128)(2,1)S(1)}, bf16[3,64,128]{2,1,0:T(8,128)(2,1)S(1)}, u32[]{:S(2)}, u32[]{:S(2)}) collective-permute-start(bf16[3,64,128]{2,1,0:T(8,128)(2,1)S(1)} %get-tuple-element.76), channel_id=1, source_target_pairs={{0,253},{1,254},{2,255},{3,0},{4,1},{5,2},{6,3},{7,4},{8,5},{9,6},... | collective-permute-start | bytes 147464 | tf_op jit(solution)/shard_map/ppermute | solution.py:39
  121.7 9.2 %collective-permute-start.18 = (bf16[4,64,128]{2,1,0:T(8,128)(2,1)S(1)}, bf16[4,64,128]{2,1,0:T(8,128)(2,1)S(1)}, u32[]{:S(2)}, u32[]{:S(2)}) collective-permute-start(bf16[4,64,128]{2,1,0:T(8,128)(2,1)S(1)} %get-tuple-element.79), channel_id=1, source_target_pairs={{0,1},{1,2},{2,3},{3,4},{4,5},{5,6},{6,7},{7,8},{8,9},{9,10},{10,1... | collective-permute-start | bytes 196616 | tf_op jit(solution)/shard_map/ppermute | solution.py:39
  121.8 9.1 %collective-permute-start.19 = (bf16[4,64,128]{2,1,0:T(8,128)(2,1)S(1)}, bf16[4,64,128]{2,1,0:T(8,128)(2,1)S(1)}, u32[]{:S(2)}, u32[]{:S(2)}) collective-permute-start(bf16[4,64,128]{2,1,0:T(8,128)(2,1)S(1)} %get-tuple-element.80), channel_id=1, source_target_pairs={{0,255},{1,0},{2,1},{3,2},{4,3},{5,4},{6,5},{7,6},{8,7},{9,8},{10,... | collective-permute-start | bytes 196616 | tf_op jit(solution)/shard_map/ppermute | solution.py:39
  133.6 9.9 %collective-permute-start.20 = (bf16[8,64,128]{2,1,0:T(8,128)(2,1)S(1)}, bf16[8,64,128]{2,1,0:T(8,128)(2,1)S(1)}, u32[]{:S(2)}, u32[]{:S(2)}) collective-permute-start(bf16[8,64,128]{2,1,0:T(8,128)(2,1)S(1)} %get-tuple-element.81), channel_id=1, source_target_pairs={{0,1},{1,2},{2,3},{3,4},{4,5},{5,6},{6,7},{7,8},{8,9},{9,10},{10,1... | collective-permute-start | bytes 393224 | tf_op jit(solution)/shard_map/ppermute | solution.py:39
  133.7 9.8 %collective-permute-start.21 = (bf16[8,64,128]{2,1,0:T(8,128)(2,1)S(1)}, bf16[8,64,128]{2,1,0:T(8,128)(2,1)S(1)}, u32[]{:S(2)}, u32[]{:S(2)}) collective-permute-start(bf16[8,64,128]{2,1,0:T(8,128)(2,1)S(1)} %get-tuple-element.82.mid_ref), channel_id=1, source_target_pairs={{0,255},{1,0},{2,1},{3,2},{4,3},{5,4},{6,5},{7,6},{8,7},{9,8},{10,... | collective-permute-start | bytes 393224 | tf_op jit(solution)/shard_map/ppermute | solution.py:39
  148.5 9.7 %collective-permute-start.22 = (bf16[4,64,128]{2,1,0:T(8,128)(2,1)S(1)}, bf16[4,64,128]{2,1,0:T(8,128)(2,1)S(1)}, u32[]{:S(2)}, u32[]{:S(2)}) collective-permute-start(bf16[4,64,128]{2,1,0:T(8,128)(2,1)S(1)} %get-tuple-element.85), channel_id=1, source_target_pairs={{0,1},{1,2},{2,3},{3,4},{4,5},{5,6},{6,7},{7,8},{8,9},{9,10},{10,1... | collective-permute-start | bytes 196616 | tf_op jit(solution)/shard_map/ppermute | solution.py:39
  148.6 9.6 %collective-permute-start.23 = (bf16[4,64,128]{2,1,0:T(8,128)(2,1)S(1)}, bf16[4,64,128]{2,1,0:T(8,128)(2,1)S(1)}, u32[]{:S(2)}, u32[]{:S(2)}) collective-permute-start(bf16[4,64,128]{2,1,0:T(8,128)(2,1)S(1)} %get-tuple-element.86), channel_id=1, source_target_pairs={{0,255},{1,0},{2,1},{3,2},{4,3},{5,4},{6,5},{7,6},{8,7},{9,8},{10,... | collective-permute-start | bytes 196616 | tf_op jit(solution)/shard_map/ppermute | solution.py:39
  (14 other events, 246.4 us)

commit v5 on v4

--- a/solution.py
+++ b/solution.py
@@ -242,13 +242,11 @@
             shape((NB0, BS), f32), shape((NB1, BS), f32), shape((NB2, BS), f32),
             shape((FIXED, BS), bf16), shape((FIXED, BS), bf16),
             shape((NB2 * ROWS, BS), bf16), shape((TAIL, BS), bf16), shape((NB0 * ROWS, BS), bf16),
+            shape((NB1 * ROWS, BS), bf16),
         ),
         [hbm()] * 3 + [vmem()] * 3 + [smem()] * 2 + [vmem()] * 2,
-        (vmem(),) * 8,
-        [
-            pltpu.VMEM((NB1 * ROWS, BS), bf16),
-            pltpu.SemaphoreType.DMA((10,)),
-        ],
+        (vmem(),) * 9,
+        [pltpu.SemaphoreType.DMA((10,))],
         mib=10, flops=2**30, nbytes=2**22,
     )(w1, w2, w3, deg1, deg2, deg3, col2, col3, own3, slot3)
 
@@ -460,7 +458,7 @@
         out_ref[2 * q + 1] = x_ref[2 * q + 1] + y[:, BS:]
         return carry
 
-    lax.fori_loop(0, n // 2, step, 0)
+    lax.fori_loop(0, n // 2, step, 0, unroll=2)
 
 
 def place(e_ref, b, value):
@@ -601,7 +599,7 @@
 
 def inner_sweep(n, first_sweep, col, x, f, g, w):
     return call(
-        functools.partial(inner_kernel, n, first_sweep), "inner" + ("down" if first_sweep else "up"),
+        functools.partial(inner_kernel, n, first_sweep), "inner" + ("down" if first_sweep else "up") + str(n),
         shape((n, R, BS), f32),
         [smem()] + [vmem()] * 4, vmem(), [pltpu.VMEM((n, R, BS), bf16)],
         mib=12, flops=2 * n * R * ROWS * BS, nbytes=2**20,
@@ -843,7 +841,7 @@
     columns_fine, columns_second, columns_third = columns_fine.T, columns_second.T, columns_third.T
     w1, w2, w3 = (in_hbm(flat(w)) for w in (weights_fine, weights_second, weights_third))
     edges1 = both_ways(*first_edges(in_hbm(flat(f)), w1, in_hbm(degree_fine), in_hbm(columns_fine)))
-    g1, g2, _, up, down, w3, tail, kept1 = fixed_data(
+    g1, g2, _, up, down, w3, tail, kept1, kept2 = fixed_data(
         w1, w2, w3, degree_fine, degree_second, degree_third, columns_second, columns_third, owners_third, slots_third
     )
     fixed = both_ways(up, down)
@@ -857,8 +855,9 @@
     lo, hi = both_ways(high, low)
     f2, up, down = second_rhs(mid, lo, hi)
     f_edges = both_ways(up, down)
+    inner = inner_sweep(NB1, True, columns_second, f2, f2, g2, kept2)
     x2, low, mid, high = go_down(
-        NB1, NB2, 0, columns_second, f2, g2, owners_second, slots_second, f_edges, fixed, w2, 12
+        NB1, NB2, 0, columns_second, f2, g2, owners_second, slots_second, f_edges, fixed, kept2, 12, inner
     )
     parts, copy = parts_of(low, mid, high)
     plo, phi = both_ways(copy, parts)
@@ -872,7 +871,8 @@
     ulo, uhi = both_ways(near, copy, 3)
     x2, first, last = third_up(own, lo, hi, ulo, uhi, z, *third, owners_second, slots_second, x2)
     x_edges = both_ways(last, first)
-    x2, copy = go_up(NB1, 0, columns_second, x2, x_edges, f2, g2, f_edges, fixed, w2, bf16, 12, 2)
+    inner = inner_sweep(NB1, False, columns_second, x2, f2, g2, kept2)
+    x2, copy = go_up(NB1, 0, columns_second, x2, x_edges, f2, g2, f_edges, fixed, kept2, bf16, 12, 2, inner)
     lo, hi = both_ways(copy, x2)
     x1, first, last = prolong(NB0, NB1, owners_fine, slots_fine, lo, x2, hi, x1)
     x_edges = both_ways(last, first)

time: 162 us -> 160 us (0.988)
  Pallas kernels: 33.9 us -> 30.9 us
    pallas_call x1, Pallas kernels: 4.93 us -> 3.15 us  [prolong(): call(functools.partial(prolong_kernel, n, nc), f'prolong{n}', (shape((n,...]
    pallas_call x2 -> x4, Pallas kernels: 4.56 us -> 6.19 us  [inner_sweep(): call(functools.partial(inner_kernel, n, first_sweep), 'inner' + ('down' i...]
  transfers between devices with their start and end apart: 24 -> 24, of which waited for: 9 -> 11; matrix products, arithmetic and copies ran while one was open for 0% -> 0% of each run, Pallas kernels for 11% -> 11%
where the time goes in v5:
time: 160 us
  starting transfers between devices  93.8 us (59%)
  Pallas kernels  30.9 us (19%)
  blocking collectives  17.4 us (11%)
  waiting for transfers between devices  17.3 us (11%)
    ppermute x24, starting transfers between devices, passed_along(): lax.ppermute(value, AXES, [(s, (s + steps) % count) for s in range(count)])  93.8 us
    all_to_all x1, blocking collectives, on_device(): got = lax.all_to_all(c, 'col', 0, 0, tiled=True)  17.4 us
    ppermute x24, waiting for transfers between devices, passed_along(): lax.ppermute(value, AXES, [(s, (s + steps) % count) for s in range(count)])  17.3 us
    pallas_call x2, Pallas kernels, go_down(): call(functools.partial(down_kernel, n, nc, base, chunks), f'down{n}', (sh...  7.63 us
    pallas_call x4, Pallas kernels, inner_sweep(): call(functools.partial(inner_kernel, n, first_sweep), 'inner' + ('down' i...  6.19 us
    pallas_call x2, Pallas kernels, go_up(): call(functools.partial(up_kernel, n, base, chunks), f'up{n}', (shape((n,...  5.55 us
    pallas_call x1, Pallas kernels, fixed_data(): call(fixed_kernel, 'fixed', (shape((NB0, BS), f32), shape((NB1, BS), f32)...  3.97 us
  transfers between devices with their start and end apart: 24, of which 11 were waited for; matrix products, arithmetic and copies ran while one was open for 0% of the time, Pallas kernels for 11%

profile of v5, /device:TPU:0, one launch (start us, length us, event | category | flops | bytes accessed | tf_op | source)
XLA Modules:
  0.0 159.9 jit_solution(461420660222836881)
XLA Ops:
  1.8 8.1 %collective-permute-start.1 = (bf16[1040,128]{1,0:T(8,128)(2,1)S(1)}, bf16[1040,128]{1,0:T(8,128)(2,1)S(1)}, u32[]{:S(2)}, u32[]{:S(2)}) collective-permute-start(bf16[1040,128]{1,0:T(8,128)(2,1)S(1)} %get-tuple-element.49), channel_id=1, source_target_pairs={{0,255},{1,0},{2,1},{3,2},{4,3},{5,4},{6,5},{7,6},{8,7},{9,8},{10,... | collective-permute-start | bytes 798728 | tf_op jit(solution)/shard_map/ppermute | solution.py:39
  10.0 4.0 %fixed.1 = (f32[32,128]{1,0:T(8,128)S(1)}, f32[8,128]{1,0:T(8,128)S(1)}, f32[2,128]{1,0:T(2,128)}, bf16[1568,128]{1,0:T(8,128)(2,1)S(1)}, bf16[1568,128]{1,0:T(8...) custom-call(bf16[12288,128]{1,0:T(8,128)(2,1)} %bitcast.20, ...), custom_call_target="tpu_custom_call" | custom-call | flops 1073741824 | bytes 4194304 | tf_op jit(solution)/shard_map/fixed/pallas_call | solution.py:239
  14.1 7.2 %collective-permute-start.7 = (bf16[1568,128]{1,0:T(8,128)(2,1)S(1)}, bf16[1568,128]{1,0:T(8,128)(2,1)S(1)}, u32[]{:S(2)}, u32[]{:S(2)}) collective-permute-start(bf16[1568,128]{1,0:T(8,128)(2,1)S(1)} %get-tuple-element.59), channel_id=1, source_target_pairs={{0,255},{1,0},{2,1},{3,2},{4,3},{5,4},{6,5},{7,6},{8,7},{9,8},{10,... | collective-permute-start | bytes 1204232 | tf_op jit(solution)/shard_map/ppermute | solution.py:39
  21.3 2.3 %innerdown32.1.rest_1_ = f32[32,64,128]{2,1,0:T(8,128)S(1)} custom-call(s32[3,32]{1,0:T(4,128)S(1)} %bitcast.9, bf16[32,64,128]{2,1,0:T(8,128)(2,1)S(1)} %copy-done, bf16[32,64,128]{2,1,0:T(8,128)(2,1)S(1)} %copy-done, f32[32,128]{1,0:T(8,128)S(1)} %get-tuple-element.47.g_ref, bf16[12288,128]{1,0:T(8,128)(2,1)S(1)} %get-tuple-element.50.w_ref.rest_0_), custom_call_target="tpu_custom_call" | custom-call | flops 201326592 | bytes 1048576 | tf_op jit(solution)/shard_map/innerdown32/pallas_call | solution.py:601
  23.7 5.8 %down32.1 = (f32[32,64,128]{2,1,0:T(8,128)S(1)}, bf16[8,64,128]{2,1,0:T(8,128)(2,1)S(1)}, f32[8,64,128]{2,1,0:T(8,128)S(1)}, bf16[8,64,128]{2,1,0:T(8,128)(2,1)S(1)}) custom-call(s32[3,32]{1,0:T(4,128)S(1)} %bitcast.10, bf16[32,64,128]{2,1,0:T(8,128)(2,1)S(1)} %copy-done, f32[32,128]{1,0:T(8,128)S(1)} %get-tuple-element.47.g_ref, s32[32,128]{1,0:T(8,128)S(1)} %copy-done.5, ...), custom_call_target="tpu_custom_call" | custom-call | flops 402653184 | bytes 3145728 | tf_op jit(solution)/shard_map/down32/pallas_call | solution.py:413
  29.6 7.2 %collective-permute-start.3 = (bf16[8,64,128]{2,1,0:T(8,128)(2,1)S(1)}, bf16[8,64,128]{2,1,0:T(8,128)(2,1)S(1)}, u32[]{:S(2)}, u32[]{:S(2)}) collective-permute-start(bf16[8,64,128]{2,1,0:T(8,128)(2,1)S(1)} %get-tuple-element.53), channel_id=1, source_target_pairs={{0,255},{1,0},{2,1},{3,2},{4,3},{5,4},{6,5},{7,6},{8,7},{9,8},{10,... | collective-permute-start | bytes 393224 | tf_op jit(solution)/shard_map/ppermute | solution.py:39
  36.8 2.6 %collective-permute-done.2.lo_ref = bf16[8,64,128]{2,1,0:T(8,128)(2,1)S(1)} collective-permute-done((bf16[8,64,128]{2,1,0:T(8,128)(2,1)S(1)}, bf16[8,64,128]{2,1,0:T(8,128)(2,1)S(1)}, u32[]{:S(2)}, u32[]{:S(2)}) %collective-permute-start.2) | collective-permute-done | bytes 131104 | tf_op jit(solution)/shard_map/ppermute | solution.py:39
  39.6 7.2 %collective-permute-start.5 = (bf16[4,64,128]{2,1,0:T(8,128)(2,1)S(1)}, bf16[4,64,128]{2,1,0:T(8,128)(2,1)S(1)}, u32[]{:S(2)}, u32[]{:S(2)}) collective-permute-start(bf16[4,64,128]{2,1,0:T(8,128)(2,1)S(1)} %get-tuple-element.57), channel_id=1, source_target_pairs={{0,255},{1,0},{2,1},{3,2},{4,3},{5,4},{6,5},{7,6},{8,7},{9,8},{10,... | collective-permute-start | bytes 196616 | tf_op jit(solution)/shard_map/ppermute | solution.py:39
  47.0 8.1 %collective-permute-start.13 = (bf16[816,128]{1,0:T(8,128)(2,1)S(1)}, bf16[816,128]{1,0:T(8,128)(2,1)S(1)}, u32[]{:S(2)}, u32[]{:S(2)}) collective-permute-start(bf16[816,128]{1,0:T(8,128)(2,1)S(1)} %get-tuple-element.72), channel_id=1, source_target_pairs={{0,254},{1,255},{2,0},{3,1},{4,2},{5,3},{6,4},{7,5},{8,6},{9,7},{1... | collective-permute-start | bytes 626696 | tf_op jit(solution)/shard_map/ppermute | solution.py:39
  57.9 7.2 %collective-permute-start.9 = (bf16[6,64,128]{2,1,0:T(8,128)(2,1)S(1)}, bf16[6,64,128]{2,1,0:T(8,128)(2,1)S(1)}, u32[]{:S(2)}, u32[]{:S(2)}) collective-permute-start(bf16[6,64,128]{2,1,0:T(8,128)(2,1)S(1)} %get-tuple-element.64.p_ref), channel_id=1, source_target_pairs={{0,255},{1,0},{2,1},{3,2},{4,3},{5,4},{6,5},{7,6},{8,7},{9,8},{10,... | collective-permute-start | bytes 294920 | tf_op jit(solution)/shard_map/ppermute | solution.py:39
  65.0 2.4 %collective-permute-done.8.lo_ref = bf16[6,64,128]{2,1,0:T(8,128)(2,1)S(1)} collective-permute-done((bf16[6,64,128]{2,1,0:T(8,128)(2,1)S(1)}, bf16[6,64,128]{2,1,0:T(8,128)(2,1)S(1)}, u32[]{:S(2)}, u32[]{:S(2)}) %collective-permute-start.8) | collective-permute-done | bytes 98336 | tf_op jit(solution)/shard_map/ppermute | solution.py:39
  67.6 9.0 %collective-permute-start.11 = (bf16[6,64,128]{2,1,0:T(8,128)(2,1)S(1)}, bf16[6,64,128]{2,1,0:T(8,128)(2,1)S(1)}, u32[]{:S(2)}, u32[]{:S(2)}) collective-permute-start(bf16[6,64,128]{2,1,0:T(8,128)(2,1)S(1)} %get-tuple-element.68), channel_id=1, source_target_pairs={{0,253},{1,254},{2,255},{3,0},{4,1},{5,2},{6,3},{7,4},{8,5},{9,6},... | collective-permute-start | bytes 294920 | tf_op jit(solution)/shard_map/ppermute | solution.py:39
  76.6 2.3 %collective-permute-done.10.dlo_ref = bf16[6,64,128]{2,1,0:T(8,128)(2,1)S(1)} collective-permute-done((bf16[6,64,128]{2,1,0:T(8,128)(2,1)S(1)}, bf16[6,64,128]{2,1,0:T(8,128)(2,1)S(1)}, u32[]{:S(2)}, u32[]{:S(2)}) %collective-permute-start.10) | collective-permute-done | bytes 98336 | tf_op jit(solution)/shard_map/ppermute | solution.py:39
  80.7 17.4 %all_to_all.5.got_ref = bf16[32,64,128]{2,1,0:T(8,128)(2,1)S(1)} all-to-all(bf16[32,64,128]{2,1,0:T(8,128)(2,1)S(1)} %get-tuple-element.73), channel_id=1, replica_groups=mesh['row'=8,'col'=32] {'col'}, dimensions={0} | all-to-all | bytes 1048576 | tf_op jit(solution)/shard_map/all_to_all | solution.py:867
  98.6 2.8 %collective-permute-start.14 = (bf16[3,64,128]{2,1,0:T(8,128)(2,1)S(1)}, bf16[3,64,128]{2,1,0:T(8,128)(2,1)S(1)}, u32[]{:S(2)}, u32[]{:S(2)}) collective-permute-start(bf16[3,64,128]{2,1,0:T(8,128)(2,1)S(1)} %get-tuple-element.76), channel_id=1, source_target_pairs={{0,1},{1,2},{2,3},{3,4},{4,5},{5,6},{6,7},{7,8},{8,9},{9,10},{10,1... | collective-permute-start | bytes 147464 | tf_op jit(solution)/shard_map/ppermute | solution.py:39
  101.4 4.9 %collective-permute-start.15 = (bf16[3,64,128]{2,1,0:T(8,128)(2,1)S(1)}, bf16[3,64,128]{2,1,0:T(8,128)(2,1)S(1)}, u32[]{:S(2)}, u32[]{:S(2)}) collective-permute-start(bf16[3,64,128]{2,1,0:T(8,128)(2,1)S(1)} %get-tuple-element.75.own_ref), channel_id=1, source_target_pairs={{0,255},{1,0},{2,1},{3,2},{4,3},{5,4},{6,5},{7,6},{8,7},{9,8},{10,... | collective-permute-start | bytes 147464 | tf_op jit(solution)/shard_map/ppermute | solution.py:39
  108.2 9.0 %collective-permute-start.17 = (bf16[3,64,128]{2,1,0:T(8,128)(2,1)S(1)}, bf16[3,64,128]{2,1,0:T(8,128)(2,1)S(1)}, u32[]{:S(2)}, u32[]{:S(2)}) collective-permute-start(bf16[3,64,128]{2,1,0:T(8,128)(2,1)S(1)} %get-tuple-element.78), channel_id=1, source_target_pairs={{0,253},{1,254},{2,255},{3,0},{4,1},{5,2},{6,3},{7,4},{8,5},{9,6},... | collective-permute-start | bytes 147464 | tf_op jit(solution)/shard_map/ppermute | solution.py:39
  117.2 2.4 %collective-permute-done.16.ulo_ref = bf16[3,64,128]{2,1,0:T(8,128)(2,1)S(1)} collective-permute-done((bf16[3,64,128]{2,1,0:T(8,128)(2,1)S(1)}, bf16[3,64,128]{2,1,0:T(8,128)(2,1)S(1)}, u32[]{:S(2)}, u32[]{:S(2)}) %collective-permute-start.16) | collective-permute-done | bytes 49184 | tf_op jit(solution)/shard_map/ppermute | solution.py:39
  121.1 7.2 %collective-permute-start.19 = (bf16[4,64,128]{2,1,0:T(8,128)(2,1)S(1)}, bf16[4,64,128]{2,1,0:T(8,128)(2,1)S(1)}, u32[]{:S(2)}, u32[]{:S(2)}) collective-permute-start(bf16[4,64,128]{2,1,0:T(8,128)(2,1)S(1)} %get-tuple-element.82), channel_id=1, source_target_pairs={{0,255},{1,0},{2,1},{3,2},{4,3},{5,4},{6,5},{7,6},{8,7},{9,8},{10,... | collective-permute-start | bytes 196616 | tf_op jit(solution)/shard_map/ppermute | solution.py:39
  132.3 7.4 %collective-permute-start.21 = (bf16[8,64,128]{2,1,0:T(8,128)(2,1)S(1)}, bf16[8,64,128]{2,1,0:T(8,128)(2,1)S(1)}, u32[]{:S(2)}, u32[]{:S(2)}) collective-permute-start(bf16[8,64,128]{2,1,0:T(8,128)(2,1)S(1)} %get-tuple-element.84.mid_ref), channel_id=1, source_target_pairs={{0,255},{1,0},{2,1},{3,2},{4,3},{5,4},{6,5},{7,6},{8,7},{9,8},{10,... | collective-permute-start | bytes 393224 | tf_op jit(solution)/shard_map/ppermute | solution.py:39
  139.7 2.6 %collective-permute-done.20.lo_ref = bf16[8,64,128]{2,1,0:T(8,128)(2,1)S(1)} collective-permute-done((bf16[8,64,128]{2,1,0:T(8,128)(2,1)S(1)}, bf16[8,64,128]{2,1,0:T(8,128)(2,1)S(1)}, u32[]{:S(2)}, u32[]{:S(2)}) %collective-permute-start.20) | collective-permute-done | bytes 131104 | tf_op jit(solution)/shard_map/ppermute | solution.py:39
  142.8 3.2 %prolong32.1 = (f32[32,64,128]{2,1,0:T(8,128)S(1)}, bf16[4,64,128]{2,1,0:T(8,128)(2,1)S(1)}, bf16[4,64,128]{2,1,0:T(8,128)(2,1)S(1)}) custom-call(s32[32,128]{1,0:T(8,128)S(1)} %copy-done.5, s32[32,128]{1,0:T(8,128)S(1)} %copy-done.6, bf16[8,64,128]{2,1,0:T(8,128)(2,1)S(1)} %collective-permute-done.20.lo_ref, ...), custom_call_target="tpu_custom_call" | custom-call | flops 1610612736 | bytes 2097152 | tf_op jit(solution)/shard_map/prolong32/pallas_call | solution.py:479
  146.1 7.4 %collective-permute-start.23 = (bf16[4,64,128]{2,1,0:T(8,128)(2,1)S(1)}, bf16[4,64,128]{2,1,0:T(8,128)(2,1)S(1)}, u32[]{:S(2)}, u32[]{:S(2)}) collective-permute-start(bf16[4,64,128]{2,1,0:T(8,128)(2,1)S(1)} %get-tuple-element.88), channel_id=1, source_target_pairs={{0,255},{1,0},{2,1},{3,2},{4,3},{5,4},{6,5},{7,6},{8,7},{9,8},{10,... | collective-permute-start | bytes 196616 | tf_op jit(solution)/shard_map/ppermute | solution.py:39
  155.8 4.1 %up32.1 = f32[32,64,128]{2,1,0:T(8,128)} custom-call(s32[3,32]{1,0:T(4,128)S(1)} %bitcast.12, f32[32,64,128]{2,1,0:T(8,128)S(1)} %get-tuple-element.86.x_ref, bf16[4,64,128]{2,1,0:T(8,128)(2,1)S(1)} %collective-permute-done.22.xlo_ref, bf16[4,64,128]{2,1,0:T(8,128)(2,1)S(1)} %collective-permute-done.23.xhi_ref, bf16[32,64,128]{2,1,0:T(8,128)(2,1)S(1)} %copy-done, ...), custom_call_target="tpu_custom_call" | custom-call | flops 402653184 | bytes 3145728 | tf_op jit(solution)/shard_map/up32/pallas_call | solution.py:559
  (73 shorter events, 17.8 us)
Async XLA Ops:
  1.5 22.2 %collective-permute-start = (bf16[1040,128]{1,0:T(8,128)(2,1)S(1)}, bf16[1040,128]{1,0:T(8,128)(2,1)S(1)}, u32[]{:S(2)}, u32[]{:S(2)}) collective-permute-start(bf16[1040,128]{1,0:T(8,128)(2,1)S(1)} %get-tuple-element.48), channel_id=1, source_target_pairs={{0,1},{1,2},{2,3},{3,4},{4,5},{5,6},{6,7},{7,8},{8,9},{9,10},{10,1... | collective-permute-start | bytes 798728 | tf_op jit(solution)/shard_map/ppermute | solution.py:39
  1.8 21.9 %collective-permute-start.1 = (bf16[1040,128]{1,0:T(8,128)(2,1)S(1)}, bf16[1040,128]{1,0:T(8,128)(2,1)S(1)}, u32[]{:S(2)}, u32[]{:S(2)}) collective-permute-start(bf16[1040,128]{1,0:T(8,128)(2,1)S(1)} %get-tuple-element.49), channel_id=1, source_target_pairs={{0,255},{1,0},{2,1},{3,2},{4,3},{5,4},{6,5},{7,6},{8,7},{9,8},{10,... | collective-permute-start | bytes 798728 | tf_op jit(solution)/shard_map/ppermute | solution.py:39
  14.1 32.8 %collective-permute-start.6 = (bf16[1568,128]{1,0:T(8,128)(2,1)S(1)}, bf16[1568,128]{1,0:T(8,128)(2,1)S(1)}, u32[]{:S(2)}, u32[]{:S(2)}) collective-permute-start(bf16[1568,128]{1,0:T(8,128)(2,1)S(1)} %get-tuple-element.58), channel_id=1, source_target_pairs={{0,1},{1,2},{2,3},{3,4},{4,5},{5,6},{6,7},{7,8},{8,9},{9,10},{10,1... | collective-permute-start | bytes 1204232 | tf_op jit(solution)/shard_map/ppermute | solution.py:39
  14.1 32.7 %collective-permute-start.7 = (bf16[1568,128]{1,0:T(8,128)(2,1)S(1)}, bf16[1568,128]{1,0:T(8,128)(2,1)S(1)}, u32[]{:S(2)}, u32[]{:S(2)}) collective-permute-start(bf16[1568,128]{1,0:T(8,128)(2,1)S(1)} %get-tuple-element.59), channel_id=1, source_target_pairs={{0,255},{1,0},{2,1},{3,2},{4,3},{5,4},{6,5},{7,6},{8,7},{9,8},{10,... | collective-permute-start | bytes 1204232 | tf_op jit(solution)/shard_map/ppermute | solution.py:39
  29.5 9.9 %collective-permute-start.2 = (bf16[8,64,128]{2,1,0:T(8,128)(2,1)S(1)}, bf16[8,64,128]{2,1,0:T(8,128)(2,1)S(1)}, u32[]{:S(2)}, u32[]{:S(2)}) collective-permute-start(bf16[8,64,128]{2,1,0:T(8,128)(2,1)S(1)} %get-tuple-element.52), channel_id=1, source_target_pairs={{0,1},{1,2},{2,3},{3,4},{4,5},{5,6},{6,7},{7,8},{8,9},{9,10},{10,1... | collective-permute-start | bytes 393224 | tf_op jit(solution)/shard_map/ppermute | solution.py:39
  29.6 9.8 %collective-permute-start.3 = (bf16[8,64,128]{2,1,0:T(8,128)(2,1)S(1)}, bf16[8,64,128]{2,1,0:T(8,128)(2,1)S(1)}, u32[]{:S(2)}, u32[]{:S(2)}) collective-permute-start(bf16[8,64,128]{2,1,0:T(8,128)(2,1)S(1)} %get-tuple-element.53), channel_id=1, source_target_pairs={{0,255},{1,0},{2,1},{3,2},{4,3},{5,4},{6,5},{7,6},{8,7},{9,8},{10,... | collective-permute-start | bytes 393224 | tf_op jit(solution)/shard_map/ppermute | solution.py:39
  39.5 16.4 %collective-permute-start.4 = (bf16[4,64,128]{2,1,0:T(8,128)(2,1)S(1)}, bf16[4,64,128]{2,1,0:T(8,128)(2,1)S(1)}, u32[]{:S(2)}, u32[]{:S(2)}) collective-permute-start(bf16[4,64,128]{2,1,0:T(8,128)(2,1)S(1)} %get-tuple-element.56), channel_id=1, source_target_pairs={{0,1},{1,2},{2,3},{3,4},{4,5},{5,6},{6,7},{7,8},{8,9},{9,10},{10,1... | collective-permute-start | bytes 196616 | tf_op jit(solution)/shard_map/ppermute | solution.py:39
  39.6 16.3 %collective-permute-start.5 = (bf16[4,64,128]{2,1,0:T(8,128)(2,1)S(1)}, bf16[4,64,128]{2,1,0:T(8,128)(2,1)S(1)}, u32[]{:S(2)}, u32[]{:S(2)}) collective-permute-start(bf16[4,64,128]{2,1,0:T(8,128)(2,1)S(1)} %get-tuple-element.57), channel_id=1, source_target_pairs={{0,255},{1,0},{2,1},{3,2},{4,3},{5,4},{6,5},{7,6},{8,7},{9,8},{10,... | collective-permute-start | bytes 196616 | tf_op jit(solution)/shard_map/ppermute | solution.py:39
  46.9 29.6 %collective-permute-start.12 = (bf16[816,128]{1,0:T(8,128)(2,1)S(1)}, bf16[816,128]{1,0:T(8,128)(2,1)S(1)}, u32[]{:S(2)}, u32[]{:S(2)}) collective-permute-start(bf16[816,128]{1,0:T(8,128)(2,1)S(1)} %get-tuple-element.71), channel_id=1, source_target_pairs={{0,2},{1,3},{2,4},{3,5},{4,6},{5,7},{6,8},{7,9},{8,10},{9,11},{10,... | collective-permute-start | bytes 626696 | tf_op jit(solution)/shard_map/ppermute | solution.py:39
  47.0 29.6 %collective-permute-start.13 = (bf16[816,128]{1,0:T(8,128)(2,1)S(1)}, bf16[816,128]{1,0:T(8,128)(2,1)S(1)}, u32[]{:S(2)}, u32[]{:S(2)}) collective-permute-start(bf16[816,128]{1,0:T(8,128)(2,1)S(1)} %get-tuple-element.72), channel_id=1, source_target_pairs={{0,254},{1,255},{2,0},{3,1},{4,2},{5,3},{6,4},{7,5},{8,6},{9,7},{1... | collective-permute-start | bytes 626696 | tf_op jit(solution)/shard_map/ppermute | solution.py:39
  57.8 9.7 %collective-permute-start.8 = (bf16[6,64,128]{2,1,0:T(8,128)(2,1)S(1)}, bf16[6,64,128]{2,1,0:T(8,128)(2,1)S(1)}, u32[]{:S(2)}, u32[]{:S(2)}) collective-permute-start(bf16[6,64,128]{2,1,0:T(8,128)(2,1)S(1)} %get-tuple-element.65), channel_id=1, source_target_pairs={{0,1},{1,2},{2,3},{3,4},{4,5},{5,6},{6,7},{7,8},{8,9},{9,10},{10,1... | collective-permute-start | bytes 294920 | tf_op jit(solution)/shard_map/ppermute | solution.py:39
  57.9 9.6 %collective-permute-start.9 = (bf16[6,64,128]{2,1,0:T(8,128)(2,1)S(1)}, bf16[6,64,128]{2,1,0:T(8,128)(2,1)S(1)}, u32[]{:S(2)}, u32[]{:S(2)}) collective-permute-start(bf16[6,64,128]{2,1,0:T(8,128)(2,1)S(1)} %get-tuple-element.64.p_ref), channel_id=1, source_target_pairs={{0,255},{1,0},{2,1},{3,2},{4,3},{5,4},{6,5},{7,6},{8,7},{9,8},{10,... | collective-permute-start | bytes 294920 | tf_op jit(solution)/shard_map/ppermute | solution.py:39
  67.5 11.4 %collective-permute-start.10 = (bf16[6,64,128]{2,1,0:T(8,128)(2,1)S(1)}, bf16[6,64,128]{2,1,0:T(8,128)(2,1)S(1)}, u32[]{:S(2)}, u32[]{:S(2)}) collective-permute-start(bf16[6,64,128]{2,1,0:T(8,128)(2,1)S(1)} %get-tuple-element.67), channel_id=1, source_target_pairs={{0,3},{1,4},{2,5},{3,6},{4,7},{5,8},{6,9},{7,10},{8,11},{9,12},{10... | collective-permute-start | bytes 294920 | tf_op jit(solution)/shard_map/ppermute | solution.py:39
  67.6 12.2 %collective-permute-start.11 = (bf16[6,64,128]{2,1,0:T(8,128)(2,1)S(1)}, bf16[6,64,128]{2,1,0:T(8,128)(2,1)S(1)}, u32[]{:S(2)}, u32[]{:S(2)}) collective-permute-start(bf16[6,64,128]{2,1,0:T(8,128)(2,1)S(1)} %get-tuple-element.68), channel_id=1, source_target_pairs={{0,253},{1,254},{2,255},{3,0},{4,1},{5,2},{6,3},{7,4},{8,5},{9,6},... | collective-permute-start | bytes 294920 | tf_op jit(solution)/shard_map/ppermute | solution.py:39
  98.6 9.4 %collective-permute-start.14 = (bf16[3,64,128]{2,1,0:T(8,128)(2,1)S(1)}, bf16[3,64,128]{2,1,0:T(8,128)(2,1)S(1)}, u32[]{:S(2)}, u32[]{:S(2)}) collective-permute-start(bf16[3,64,128]{2,1,0:T(8,128)(2,1)S(1)} %get-tuple-element.76), channel_id=1, source_target_pairs={{0,1},{1,2},{2,3},{3,4},{4,5},{5,6},{6,7},{7,8},{8,9},{9,10},{10,1... | collective-permute-start | bytes 147464 | tf_op jit(solution)/shard_map/ppermute | solution.py:39
  101.4 6.7 %collective-permute-start.15 = (bf16[3,64,128]{2,1,0:T(8,128)(2,1)S(1)}, bf16[3,64,128]{2,1,0:T(8,128)(2,1)S(1)}, u32[]{:S(2)}, u32[]{:S(2)}) collective-permute-start(bf16[3,64,128]{2,1,0:T(8,128)(2,1)S(1)} %get-tuple-element.75.own_ref), channel_id=1, source_target_pairs={{0,255},{1,0},{2,1},{3,2},{4,3},{5,4},{6,5},{7,6},{8,7},{9,8},{10,... | collective-permute-start | bytes 147464 | tf_op jit(solution)/shard_map/ppermute | solution.py:39
  108.1 11.5 %collective-permute-start.16 = (bf16[3,64,128]{2,1,0:T(8,128)(2,1)S(1)}, bf16[3,64,128]{2,1,0:T(8,128)(2,1)S(1)}, u32[]{:S(2)}, u32[]{:S(2)}) collective-permute-start(bf16[3,64,128]{2,1,0:T(8,128)(2,1)S(1)} %get-tuple-element.77), channel_id=1, source_target_pairs={{0,3},{1,4},{2,5},{3,6},{4,7},{5,8},{6,9},{7,10},{8,11},{9,12},{10... | collective-permute-start | bytes 147464 | tf_op jit(solution)/shard_map/ppermute | solution.py:39
  108.2 11.4 %collective-permute-start.17 = (bf16[3,64,128]{2,1,0:T(8,128)(2,1)S(1)}, bf16[3,64,128]{2,1,0:T(8,128)(2,1)S(1)}, u32[]{:S(2)}, u32[]{:S(2)}) collective-permute-start(bf16[3,64,128]{2,1,0:T(8,128)(2,1)S(1)} %get-tuple-element.78), channel_id=1, source_target_pairs={{0,253},{1,254},{2,255},{3,0},{4,1},{5,2},{6,3},{7,4},{8,5},{9,6},... | collective-permute-start | bytes 147464 | tf_op jit(solution)/shard_map/ppermute | solution.py:39
  121.0 9.3 %collective-permute-start.18 = (bf16[4,64,128]{2,1,0:T(8,128)(2,1)S(1)}, bf16[4,64,128]{2,1,0:T(8,128)(2,1)S(1)}, u32[]{:S(2)}, u32[]{:S(2)}) collective-permute-start(bf16[4,64,128]{2,1,0:T(8,128)(2,1)S(1)} %get-tuple-element.81), channel_id=1, source_target_pairs={{0,1},{1,2},{2,3},{3,4},{4,5},{5,6},{6,7},{7,8},{8,9},{9,10},{10,1... | collective-permute-start | bytes 196616 | tf_op jit(solution)/shard_map/ppermute | solution.py:39
  121.1 9.6 %collective-permute-start.19 = (bf16[4,64,128]{2,1,0:T(8,128)(2,1)S(1)}, bf16[4,64,128]{2,1,0:T(8,128)(2,1)S(1)}, u32[]{:S(2)}, u32[]{:S(2)}) collective-permute-start(bf16[4,64,128]{2,1,0:T(8,128)(2,1)S(1)} %get-tuple-element.82), channel_id=1, source_target_pairs={{0,255},{1,0},{2,1},{3,2},{4,3},{5,4},{6,5},{7,6},{8,7},{9,8},{10,... | collective-permute-start | bytes 196616 | tf_op jit(solution)/shard_map/ppermute | solution.py:39
  132.2 10.1 %collective-permute-start.20 = (bf16[8,64,128]{2,1,0:T(8,128)(2,1)S(1)}, bf16[8,64,128]{2,1,0:T(8,128)(2,1)S(1)}, u32[]{:S(2)}, u32[]{:S(2)}) collective-permute-start(bf16[8,64,128]{2,1,0:T(8,128)(2,1)S(1)} %get-tuple-element.83), channel_id=1, source_target_pairs={{0,1},{1,2},{2,3},{3,4},{4,5},{5,6},{6,7},{7,8},{8,9},{9,10},{10,1... | collective-permute-start | bytes 393224 | tf_op jit(solution)/shard_map/ppermute | solution.py:39
  132.3 10.5 %collective-permute-start.21 = (bf16[8,64,128]{2,1,0:T(8,128)(2,1)S(1)}, bf16[8,64,128]{2,1,0:T(8,128)(2,1)S(1)}, u32[]{:S(2)}, u32[]{:S(2)}) collective-permute-start(bf16[8,64,128]{2,1,0:T(8,128)(2,1)S(1)} %get-tuple-element.84.mid_ref), channel_id=1, source_target_pairs={{0,255},{1,0},{2,1},{3,2},{4,3},{5,4},{6,5},{7,6},{8,7},{9,8},{10,... | collective-permute-start | bytes 393224 | tf_op jit(solution)/shard_map/ppermute | solution.py:39
  146.0 9.8 %collective-permute-start.22 = (bf16[4,64,128]{2,1,0:T(8,128)(2,1)S(1)}, bf16[4,64,128]{2,1,0:T(8,128)(2,1)S(1)}, u32[]{:S(2)}, u32[]{:S(2)}) collective-permute-start(bf16[4,64,128]{2,1,0:T(8,128)(2,1)S(1)} %get-tuple-element.87), channel_id=1, source_target_pairs={{0,1},{1,2},{2,3},{3,4},{4,5},{5,6},{6,7},{7,8},{8,9},{9,10},{10,1... | collective-permute-start | bytes 196616 | tf_op jit(solution)/shard_map/ppermute | solution.py:39
  146.1 9.7 %collective-permute-start.23 = (bf16[4,64,128]{2,1,0:T(8,128)(2,1)S(1)}, bf16[4,64,128]{2,1,0:T(8,128)(2,1)S(1)}, u32[]{:S(2)}, u32[]{:S(2)}) collective-permute-start(bf16[4,64,128]{2,1,0:T(8,128)(2,1)S(1)} %get-tuple-element.88), channel_id=1, source_target_pairs={{0,255},{1,0},{2,1},{3,2},{4,3},{5,4},{6,5},{7,6},{8,7},{9,8},{10,... | collective-permute-start | bytes 196616 | tf_op jit(solution)/shard_map/ppermute | solution.py:39
  (14 other events, 238.6 us)
